TPU v7x, 32 devices: a whole 2x2x4 slice. The times are simulated.
32 devices in a mesh: grp: 2 (over y), pool: 8 (over z, core), tp: 2 (over x).
Axes of the slice: x: 2, y: 2, z: 4, core: 2. Of those that a mesh axis runs over, the one named last changes fastest.
Arguments:
- home_query: bfloat16 [64, 8192], P(('grp', 'pool'), 'tp'), parts along dimension 0, may hold values from -12 to 12
- home_key: bfloat16 [64, 1024], P(('grp', 'pool'), 'tp'), parts along dimension 0, may hold values from -5 to 5
- home_value: bfloat16 [64, 1024], P(('grp', 'pool'), 'tp'), parts along dimension 0, may hold values from -5 to 5
- cache_keys: bfloat16 [8192, 1024], P(('grp', 'pool'), 'tp'), parts along dimension 0, may hold values from -12 to 12
- cache_values: bfloat16 [8192, 1024], P(('grp', 'pool'), 'tp'), parts along dimension 0, may hold values from -5 to 5
- cache_start: int32 [64], P('grp'), parts along dimension 0, may hold values from 0 to 4088, as said below
- cache_len: int32 [64], P('grp'), parts along dimension 0, may hold values from 8 to 64, as said below
- prompt_query: bfloat16 [7168, 8192], P(('grp', 'pool'), 'tp'), parts along dimension 0, may hold values from -12 to 12
- prompt_key: bfloat16 [7168, 1024], P(('grp', 'pool'), 'tp'), parts along dimension 0, may hold values from -12 to 12
- prompt_value: bfloat16 [7168, 1024], P(('grp', 'pool'), 'tp'), parts along dimension 0, may hold values from -5 to 5
- doc_ids: int32 [16, 448], P(('grp', 'pool')), parts along dimension 0, may hold values from 0 to 3, never falling along the last dimension, each value on 1 to 224 neighbouring positions
- out_weight: bfloat16 [8192, 8192], P('tp', 'pool'), may hold values from -0.0625 to 0.0625
Outputs:
- prompt_out: bfloat16 [7168, 8192], P(('grp', 'pool'), 'tp'), parts along dimension 0
- decode_out: bfloat16 [64, 8192], P(('grp', 'tp'), 'pool'), parts along dimension 0
There are 2 independent parts, one for each index of `grp`. A program takes and returns all parts, laid end to end along the dimension named above; an argument that names none is the same for every part. Nothing has to cross between parts.
Inputs may be any that keep to these rules, and one draw needn't show every extreme that they name: Each request's cache occupies cache_len rows from cache_start on, inside the 512 rows of one pool index and apart from every other request's rows; a pool index holds the caches of at most 8 requests, and some pool index of exactly 8. `cache_len`: some request has exactly 64 rows.
All inputs are finite; a program needn't handle non-finite values.
Results may differ from a plain program's by a relative error of at most 0.008.
Values may be sent and summed in bfloat16 or wider, within the bound.
No kernel may reach another device: no remote copies, remote signals or barrier semaphores. Data moves between devices by JAX's collectives and lax.ppermute only.
A program may use at most 128 MiB of HBM per device.

v0:
```python
import functools

import jax
import jax.numpy as jnp
from jax import lax
from jax.experimental import pallas as pl
from jax.experimental.pallas import tpu as pltpu
from jax.sharding import PartitionSpec as P


HEAD_DIM = 128
LOG2E = 1.4426950408889634
ROW_BLOCK = 32
VMEM = pl.BlockSpec(memory_space=pltpu.VMEM)
SMEM = pl.BlockSpec(memory_space=pltpu.SMEM)
HBM = pl.BlockSpec(memory_space=pltpu.HBM)


def prompt_kernel(extra, first, count, group, window, doc_ref, q_hbm, k_hbm, v_hbm, *rest):
    (o_hbm, token_ref, q_ref, k_ref, v_ref, o_ref, bias_ref, s_ref, p_ref) = rest[extra:-3]
    q_sem, kv_sem, o_sem = rest[-3:]
    rows = q_hbm.shape[0]
    width = group * HEAD_DIM
    block = ROW_BLOCK
    blocks = rows // block
    total = count * blocks
    half = blocks // 2
    stacked = group * block
    scale = HEAD_DIM ** (-0.5) * LOG2E

    def fetch_q(i):
        return pltpu.make_async_copy(
            q_hbm.at[:, pl.ds((first + i) * width, width)], q_ref.at[i], q_sem.at[i]
        )

    def fetch_kv(i):
        lanes = pl.ds((first + i) * HEAD_DIM, HEAD_DIM)
        return (
            pltpu.make_async_copy(k_hbm.at[:, lanes], k_ref.at[i], kv_sem.at[2 * i]),
            pltpu.make_async_copy(v_hbm.at[:, lanes], v_ref.at[i], kv_sem.at[2 * i + 1]),
        )

    def flush(i, part):
        lo, hi = ((0, half), (half, blocks))[part]
        span = pl.ds(lo * block, (hi - lo) * block)
        return pltpu.make_async_copy(
            o_ref.at[i, span],
            o_hbm.at[span, pl.ds((first + i) * width, width)],
            o_sem.at[2 * i + part],
        )

    for i in range(count):
        for copy in fetch_kv(i):
            copy.start()
        fetch_q(i).start()
    token_ref[...] = jnp.zeros_like(token_ref)
    for b in range(blocks):
        start = max(0, (b + 1) * block - window)
        key_doc = jnp.broadcast_to(
            doc_ref[:, start : start + window].astype(jnp.float32), (block, window)
        )
        row = lax.broadcasted_iota(jnp.int32, (block, window), 0) + b * block
        col = lax.broadcasted_iota(jnp.int32, (block, window), 1) + start
        row_doc = jnp.sum(jnp.where(row == col, key_doc, 0.0), axis=1, keepdims=True)
        allowed = (col <= row) & (key_doc == row_doc)
        bias_ref[b] = jnp.where(allowed, 0.0, -jnp.inf)

    def place_of(t):
        head, b = divmod(t, blocks)
        start = max(0, (b + 1) * block - window)
        span = min(window, -(-(b + 1) * block // HEAD_DIM) * HEAD_DIM)
        return head, b, slice(b * block, (b + 1) * block), start, span

    def score(t):
        head, _, at, start, span = place_of(t)
        query = jnp.concatenate(
            [q_ref[head, at, h * HEAD_DIM : (h + 1) * HEAD_DIM] for h in range(group)], axis=0
        )
        s_ref[t % 2, :, :span] = lax.dot_general(
            query,
            k_ref[head, start : start + span, :],
            (((1,), (1,)), ((), ())),
            preferred_element_type=jnp.float32,
        )

    def weigh(t):
        _, b, _, _, span = place_of(t)
        scores = s_ref[t % 2, :, :span].reshape(group, block, span) * scale
        scores = scores + bias_ref[b, :, :span][None]
        highest = jnp.max(scores, axis=-1, keepdims=True)
        weights = jnp.exp2(scores - highest).astype(jnp.bfloat16).reshape(stacked, span)
        for c in range(span // HEAD_DIM):
            p_ref[t % 2, c] = weights[:, c * HEAD_DIM : (c + 1) * HEAD_DIM]

    def combine(t):
        head, _, at, start, span = place_of(t)
        values = v_ref[head, start : start + span, :]
        values = jnp.concatenate([values, jnp.ones_like(values)], axis=1)
        weights = jnp.concatenate([p_ref[t % 2, c] for c in range(span // HEAD_DIM)], axis=1)
        both = jnp.dot(weights, values, preferred_element_type=jnp.float32)
        result = (both[:, :HEAD_DIM] / both[:, HEAD_DIM:]).astype(jnp.bfloat16)
        for h in range(group):
            o_ref[head, at, h * HEAD_DIM : (h + 1) * HEAD_DIM] = result[
                h * block : (h + 1) * block
            ]

    for t in range(total + 2):
        if t < total and t % blocks == 0:
            for copy in fetch_kv(t // blocks):
                copy.wait()
            fetch_q(t // blocks).wait()
        if t >= 2:
            combine(t - 2)
        if t < total:
            score(t)
        if 1 <= t <= total:
            weigh(t - 1)
        if t >= 2:
            head, b = divmod(t - 2, blocks)
            if b + 1 == half:
                flush(head, 0).start()
            if b + 1 == blocks:
                flush(head, 1).start()
    for i in range(count):
        flush(i, 0).wait()
        flush(i, 1).wait()


def prompt_part(query, key, value, doc_ids, group, first, count, into, after):
    rows = query.shape[0]
    width = group * HEAD_DIM
    window = min(rows, rows // 2 + ROW_BLOCK)
    extra = [x for x in (into, after) if x is not None]
    flops = 4 * count * group * rows * window * HEAD_DIM
    stacked = group * ROW_BLOCK
    return pl.pallas_call(
        functools.partial(prompt_kernel, len(extra), first, count, group, window),
        in_specs=[VMEM, HBM, HBM, HBM]
        + ([] if into is None else [HBM])
        + ([] if after is None else [VMEM]),
        out_specs=[HBM, VMEM],
        out_shape=[
            jax.ShapeDtypeStruct(query.shape, jnp.bfloat16),
            jax.ShapeDtypeStruct((8, HEAD_DIM), jnp.float32),
        ],
        scratch_shapes=[
            pltpu.VMEM((count, rows, width), jnp.bfloat16),
            pltpu.VMEM((count, rows, HEAD_DIM), jnp.bfloat16),
            pltpu.VMEM((count, rows, HEAD_DIM), jnp.bfloat16),
            pltpu.VMEM((count, rows, width), jnp.bfloat16),
            pltpu.VMEM((rows // ROW_BLOCK, ROW_BLOCK, window), jnp.float32),
            pltpu.VMEM((2, stacked, window), jnp.float32),
            pltpu.VMEM((2, window // HEAD_DIM, stacked, HEAD_DIM), jnp.bfloat16),
            pltpu.SemaphoreType.DMA((count,)),
            pltpu.SemaphoreType.DMA((2 * count,)),
            pltpu.SemaphoreType.DMA((2 * count,)),
        ],
        input_output_aliases={} if into is None else {4: 0},
        cost_estimate=pl.CostEstimate(
            flops=flops, bytes_accessed=4 * rows * width * count, transcendentals=0
        ),
        compiler_params=pltpu.CompilerParams(vmem_limit_bytes=24 << 20),
    )(
        doc_ids,
        *(pltpu.with_memory_space_constraint(x, pltpu.HBM) for x in (query, key, value)),
        *extra,
    )


def xor_plan(n):
    return n & (n - 1) == 0 and 2 <= n <= 8


def spread(x, n):
    if not xor_plan(n):
        return [lax.all_gather(x, "pool", axis=0, tiled=True)]
    pieces = {0: x}
    for d in range(n - 2, 0, -2):
        pieces[d] = lax.ppermute(x, "pool", [(i, i ^ d) for i in range(n)])
    for d in range(0, n, 2):
        pieces[d + 1] = lax.ppermute(
            pieces[d], "pool", [(i, i ^ 1) for i in range(n)]
        )
    return [pieces[d] for d in range(n)]


def place(index, me, n):
    return index ^ me if xor_plan(n) else index


def pack_kernel(q_ref, k_ref, v_ref, o_ref):
    dq, dk = q_ref.shape[1], k_ref.shape[1]
    o_ref[:, :dq] = q_ref[...]
    o_ref[:, dq : dq + dk] = k_ref[...]
    o_ref[:, dq + dk :] = v_ref[...]


def pack(q, k, v):
    shape = (q.shape[0], q.shape[1] + k.shape[1] + v.shape[1])
    return pl.pallas_call(
        pack_kernel,
        in_specs=[VMEM] * 3,
        out_specs=VMEM,
        out_shape=jax.ShapeDtypeStruct(shape, q.dtype),
        name="pack",
    )(q, k, v)


def decode_kernel(n, count, home_rows, slots, kv_local, group, *refs):
    start_ref, len_ref = refs[:2]
    pieces = refs[2 : 2 + count]
    k_ref, v_ref, _, o_ref, all_ref, req_ref = refs[2 + count :]
    me = lax.axis_index("pool")
    cap = k_ref.shape[0]
    requests = start_ref.shape[0]
    q_width = kv_local * group * HEAD_DIM
    kv_width = kv_local * HEAD_DIM

    def find(r, rank):
        mine = start_ref[r] // cap == me

        @pl.when(mine)
        def _():
            req_ref[jnp.minimum(rank, slots - 1)] = r

        return rank + jnp.where(mine, 1, 0)

    used = lax.fori_loop(0, requests, find, 0, unroll=True)
    per = all_ref.shape[0] // count
    for i, piece in enumerate(pieces):
        all_ref[i * per : (i + 1) * per, :] = piece[...].astype(jnp.float32)
    total = all_ref.shape[0]
    slot_of = lax.broadcasted_iota(jnp.int32, (slots, 1), 0)
    row_of = jnp.full((slots, 1), -1, jnp.int32)
    first = jnp.zeros((slots, 1), jnp.int32)
    length = jnp.zeros((slots, 1), jnp.int32)
    for m in range(slots):
        have = m < used
        r = jnp.where(have, req_ref[m], 0)
        row = place(r // home_rows, me, n) * home_rows + r % home_rows
        here = slot_of == m
        row_of = jnp.where(here, jnp.where(have, row, -1), row_of)
        first = jnp.where(here, start_ref[r] - me * cap, first)
        length = jnp.where(here, jnp.where(have, len_ref[r], 0), length)
    select = (
        lax.broadcasted_iota(jnp.int32, (slots, total), 1) == row_of
    ).astype(jnp.bfloat16)
    slot_all = jnp.dot(
        select, all_ref[...].astype(jnp.bfloat16), preferred_element_type=jnp.float32
    )
    col = lax.broadcasted_iota(jnp.int32, (slots, cap), 1)
    inside = (col >= first) & (col < first + length)
    bias = jnp.where(inside, 0.0, -jnp.inf)
    scale = HEAD_DIM ** (-0.5) * LOG2E
    for g in range(kv_local):
        base = g * group * HEAD_DIM
        q32 = jnp.concatenate(
            [
                slot_all[:, base + h * HEAD_DIM : base + (h + 1) * HEAD_DIM]
                for h in range(group)
            ],
            axis=0,
        )
        lanes = slice(g * HEAD_DIM, (g + 1) * HEAD_DIM)
        new_key = slot_all[:, q_width + g * HEAD_DIM : q_width + (g + 1) * HEAD_DIM]
        new_value = slot_all[
            :, q_width + kv_width + g * HEAD_DIM : q_width + kv_width + (g + 1) * HEAD_DIM
        ]
        scores = lax.dot_general(
            q32.astype(jnp.bfloat16),
            k_ref[:, lanes],
            (((1,), (1,)), ((), ())),
            preferred_element_type=jnp.float32,
        )
        scores = scores.reshape(group, slots, cap) * scale + bias[None]
        own = (
            jnp.sum(q32.reshape(group, slots, HEAD_DIM) * new_key[None], axis=-1, keepdims=True)
            * scale
        )
        highest = jnp.maximum(jnp.max(scores, axis=-1, keepdims=True), own)
        weights = jnp.exp2(scores - highest)
        own_weight = jnp.exp2(own - highest)
        inverse = 1.0 / (jnp.sum(weights, axis=-1, keepdims=True) + own_weight)
        probs = (weights * inverse).astype(jnp.bfloat16)
        own_prob = (own_weight * inverse).astype(jnp.bfloat16).astype(jnp.float32)
        result = jnp.dot(
            probs.reshape(group * slots, cap),
            v_ref[:, lanes],
            preferred_element_type=jnp.float32,
        ).reshape(group, slots, HEAD_DIM)
        result = result + own_prob * new_value[None]
        for h in range(group):
            o_ref[:, base + h * HEAD_DIM : base + (h + 1) * HEAD_DIM] = result[h].astype(
                jnp.bfloat16
            )


def decode(pieces, cache_keys, cache_values, start, length, n, home_rows, group, after):
    kv_local = cache_keys.shape[1] // HEAD_DIM
    slots = 2 * home_rows
    total = sum(p.shape[0] for p in pieces)
    width = pieces[0].shape[1]
    q_width = kv_local * group * HEAD_DIM
    return pl.pallas_call(
        functools.partial(
            decode_kernel, n, len(pieces), home_rows, slots, kv_local, group
        ),
        in_specs=[SMEM, SMEM] + [VMEM] * len(pieces) + [VMEM, VMEM, VMEM],
        out_specs=VMEM,
        out_shape=jax.ShapeDtypeStruct((slots, q_width), jnp.bfloat16),
        scratch_shapes=[
            pltpu.VMEM((total, width), jnp.float32),
            pltpu.SMEM((slots,), jnp.int32),
        ],
        cost_estimate=pl.CostEstimate(
            flops=10**9, bytes_accessed=2 * cache_keys.size * 2, transcendentals=0
        ),
        compiler_params=pltpu.CompilerParams(vmem_limit_bytes=24 << 20),
        name="decode",
    )(start, length, *pieces, cache_keys, cache_values, after)


def project_kernel(n, count, cap, slots, tp, *refs):
    start_ref = refs[0]
    pieces = refs[1 : 1 + count]
    w_ref, _, *outs = refs[1 + count :]
    outs, (y_ref, seen_ref) = outs[:-2], outs[-2:]
    me = lax.axis_index("pool")
    requests = start_ref.shape[0]
    rows = jnp.concatenate([p[...].astype(jnp.float32) for p in pieces], axis=0)
    y_ref[...] = jnp.dot(
        rows.astype(jnp.bfloat16), w_ref[...], preferred_element_type=jnp.float32
    )
    for owner in range(n):
        seen_ref[owner] = 0

    def source(r):
        owner = start_ref[r] // cap
        rank = seen_ref[owner]
        seen_ref[owner] = rank + 1
        return place(owner, me, n) * slots + rank

    if tp != 2:
        for r in range(requests):
            outs[0][r : r + 1, :] = y_ref[pl.ds(source(r), 1), :]
        return
    keep_ref, send_ref = outs
    half = requests // 2
    mine = lax.axis_index("tp")

    for r in range(requests):
        row = y_ref[pl.ds(source(r), 1), :]
        target = r % half
        is_keep = (r // half) == mine

        @pl.when(is_keep)
        def _():
            keep_ref[target : target + 1, :] = row

        @pl.when(jnp.logical_not(is_keep))
        def _():
            send_ref[target : target + 1, :] = row


def project(pieces, weight, start, n, cap, slots, tp, after):
    requests = start.shape[0]
    total = sum(p.shape[0] for p in pieces)
    cols = weight.shape[1]
    if tp == 2:
        out_shape = [jax.ShapeDtypeStruct((requests // 2, cols), jnp.float32)] * 2
    else:
        out_shape = [jax.ShapeDtypeStruct((requests, cols), jnp.float32)]
    return pl.pallas_call(
        functools.partial(project_kernel, n, len(pieces), cap, slots, tp),
        in_specs=[SMEM] + [VMEM] * len(pieces) + [VMEM, VMEM],
        out_specs=[VMEM] * len(out_shape),
        out_shape=out_shape,
        scratch_shapes=[
            pltpu.VMEM((total, cols), jnp.float32),
            pltpu.SMEM((n,), jnp.int32),
        ],
        cost_estimate=pl.CostEstimate(
            flops=10**9, bytes_accessed=2 * weight.size, transcendentals=0
        ),
        compiler_params=pltpu.CompilerParams(vmem_limit_bytes=40 << 20),
        name="project",
    )(start, *pieces, weight, after)


def local(
    n,
    tp,
    home_query,
    home_key,
    home_value,
    cache_keys,
    cache_values,
    cache_start,
    cache_len,
    prompt_query,
    prompt_key,
    prompt_value,
    doc_ids,
    out_weight,
):
    home_rows = home_query.shape[0]
    kv_local = home_key.shape[1] // HEAD_DIM
    group = home_query.shape[1] // HEAD_DIM // kv_local
    cap = cache_keys.shape[0]
    slots = 2 * home_rows
    early = kv_local // 2

    def part(first, count, into, after):
        return prompt_part(
            prompt_query,
            prompt_key,
            prompt_value,
            doc_ids,
            group,
            first,
            count,
            into,
            after,
        )

    homes = spread(pack(home_query, home_key, home_value), n)
    prompt_out, token = part(0, early, None, None)
    slot_out = decode(
        homes, cache_keys, cache_values, cache_start, cache_len, n, home_rows, group, token
    )
    pooled = spread(slot_out, n)
    prompt_out, token = part(early, kv_local - early, prompt_out, slot_out)
    partial = project(pooled, out_weight, cache_start, n, cap, slots, tp, token)
    if tp == 2:
        keep, send = partial
        other = lax.ppermute(send.astype(jnp.bfloat16), "tp", [(0, 1), (1, 0)])
        decode_out = (keep + other.astype(jnp.float32)).astype(jnp.bfloat16)
    else:
        decode_out = lax.psum_scatter(
            partial[0], "tp", scatter_dimension=0, tiled=True
        ).astype(jnp.bfloat16)
    return (prompt_out, decode_out)


def layer(n, tp, *args):
    return local(n, tp, *args)


def solution(mesh):
    step = jax.shard_map(
        functools.partial(layer, mesh.shape["pool"], mesh.shape["tp"]),
        mesh=mesh,
        in_specs=(
            P(("grp", "pool"), "tp"),
            P(("grp", "pool"), "tp"),
            P(("grp", "pool"), "tp"),
            P(("grp", "pool"), "tp"),
            P(("grp", "pool"), "tp"),
            P("grp"),
            P("grp"),
            P(("grp", "pool"), "tp"),
            P(("grp", "pool"), "tp"),
            P(("grp", "pool"), "tp"),
            P(("grp", "pool"), None),
            P("tp", "pool"),
        ),
        out_specs=(P(("grp", "pool"), "tp"), P(("grp", "tp"), "pool")),
        check_vma=False,
    )
    n = mesh.shape["pool"]
    return step if xor_plan(n) else step
```

profile of v0, /device:TPU:0, one launch (start us, length us, event | category | flops | bytes accessed | tf_op | source)
XLA Modules:
  0.0 45.7 jit_solution(15368092158427080599)
XLA Ops:
  0.6 0.0 copy-start.3
  0.6 0.0 copy-start.6
  0.7 0.0 copy-start.2
  0.7 1.4 %pack.1.refs_2_ = bf16[4,5120]{1,0:T(4,128)(2,1)} custom-call(bf16[4,4096]{1,0:T(4,128)(2,1)} %q_ref.1, bf16[4,512]{1,0:T(4,128)(2,1)} %k_ref.1, bf16[4,512]{1,0:T(4,128)(2,1)} %v_ref.1), custom_call_target="tpu_custom_call" | custom-call | tf_op jit(solution)/shard_map/pack/pallas_call | solution.py:200
  2.1 5.1 %collective-permute-start.5 = (bf16[4,5120]{1,0:T(4,128)(2,1)}, bf16[4,5120]{1,0:T(4,128)(2,1)S(1)}, u32[]{:S(2)}, u32[]{:S(2)}) collective-permute-start(bf16[4,5120]{1,0:T(4,128)(2,1)} %pack.1.refs_2_), channel_id=1, source_target_pairs={{0,12},{2,14},{4,8},{6,10},{8,4},{10,6},{12,0},{14,2},{1,13},{3,15... | collective-permute-start | bytes 122888 | tf_op jit(solution)/shard_map/ppermute | solution.py:179
  7.1 0.0 collective-permute-start.3
  7.2 0.6 %collective-permute-start.1 = (bf16[4,5120]{1,0:T(4,128)(2,1)}, bf16[4,5120]{1,0:T(4,128)(2,1)S(1)}, u32[]{:S(2)}, u32[]{:S(2)}) collective-permute-start(bf16[4,5120]{1,0:T(4,128)(2,1)} %pack.1.refs_2_), channel_id=1, source_target_pairs={{0,4},{2,6},{4,0},{6,2},{8,12},{10,14},{12,8},{14,10},{1,5},{3,7},... | collective-permute-start | bytes 122888 | tf_op jit(solution)/shard_map/ppermute | solution.py:179
  7.7 0.0 collective-permute-start
  7.7 1.7 %collective-permute-done.5.refs_8_ = bf16[4,5120]{1,0:T(4,128)(2,1)S(1)} collective-permute-done((bf16[4,5120]{1,0:T(4,128)(2,1)}, bf16[4,5120]{1,0:T(4,128)(2,1)S(1)}, u32[]{:S(2)}, u32[]{:S(2)}) %collective-permute-start.5) | collective-permute-done | bytes 40992 | tf_op jit(solution)/shard_map/ppermute | solution.py:179
  9.4 0.0 collective-permute-start.6
  9.4 2.8 %collective-permute-done.3.refs_6_ = bf16[4,5120]{1,0:T(4,128)(2,1)S(1)} collective-permute-done((bf16[4,5120]{1,0:T(4,128)(2,1)}, bf16[4,5120]{1,0:T(4,128)(2,1)S(1)}, u32[]{:S(2)}, u32[]{:S(2)}) %collective-permute-start.3) | collective-permute-done | bytes 40992 | tf_op jit(solution)/shard_map/ppermute | solution.py:179
  12.3 0.0 collective-permute-start.4
  12.3 0.0 collective-permute-done.1.refs_4_
  12.3 0.5 %collective-permute-start.2 = (bf16[4,5120]{1,0:T(4,128)(2,1)S(1)}, bf16[4,5120]{1,0:T(4,128)(2,1)S(1)}, u32[]{:S(2)}, u32[]{:S(2)}) collective-permute-start(bf16[4,5120]{1,0:T(4,128)(2,1)S(1)} %collective-permute-done.1.refs_4_), channel_id=1, source_target_pairs={{0,2},{2,0},{4,6},{6,4},{8,10},{10,8},{12,14},{14,12},{1,3},{3,1},... | collective-permute-start | bytes 122888 | tf_op jit(solution)/shard_map/ppermute | solution.py:181
  12.8 0.7 %copy-done.1 = s32[1,448]{1,0:T(1,128)S(1)} copy-done((s32[1,448]{1,0:T(1,128)S(1)}, s32[1,448]{1,0:T(1,128)}, u32[]{:S(2)}) %copy-start.1) | copy-done | bytes 1816
  13.5 5.6 %shard_map.131 = (bf16[448,4096]{1,0:T(8,128)(2,1)}, f32[8,128]{1,0:T(8,128)S(1)}) custom-call(s32[1,448]{1,0:T(1,128)S(1)} %copy-done.1, bf16[448,4096]{1,0:T(8,128)(2,1)} %q_hbm.3, bf16[448,512]{1,0:T(8,128)(2,1)} %k_hbm.3, bf16[448,512]{1,0:T(8,128)(2,1)} %v_hbm.3), custom_call_target="tpu_custom_call" | custom-call | flops 939524096 | bytes 3670016 | tf_op jit(solution)/shard_map/pallas_call | solution.py:136
  19.1 0.0 collective-permute-done.refs_3_
  19.1 0.0 collective-permute-done.6.refs_9_
  19.1 0.0 collective-permute-done.4.refs_7_
  19.1 0.0 collective-permute-done.2.refs_5_
  19.1 0.0 copy-done.3
  19.1 0.0 copy-done.6
  19.1 0.0 copy-done
  19.1 0.0 copy-start.4
  19.1 1.0 %copy-done.4 = bf16[512,512]{1,0:T(8,128)(2,1)S(1)} copy-done((bf16[512,512]{1,0:T(8,128)(2,1)S(1)}, bf16[512,512]{1,0:T(8,128)(2,1)}, u32[]{:S(2)}) %copy-start.4) | copy-done | bytes 524312
  20.2 1.0 %copy-done.5 = bf16[512,512]{1,0:T(8,128)(2,1)S(1)} copy-done((bf16[512,512]{1,0:T(8,128)(2,1)S(1)}, bf16[512,512]{1,0:T(8,128)(2,1)}, u32[]{:S(2)}) %copy-start.5) | copy-done | bytes 524312
  21.2 2.4 %decode.1.rest_1_.refs_1_ = bf16[8,4096]{1,0:T(8,128)(2,1)S(1)} custom-call(s32[32]{0:T(128)S(1)} %copy-done.3, s32[32]{0:T(128)S(1)} %copy-done.6, bf16[4,5120]{1,0:T(4,128)(2,1)S(1)} %copy-done, bf16[4,5120]{1,0:T(4,128)(2,1)S(1)} %collective-permute-done.refs_3_, bf16[4,5120]{1,0:T(4,128)(2,1)S(1)} %collective-permute-done.1.refs_4_, ...), custom_call_target="tpu_custom_call" | custom-call | flops 1000000000 | bytes 1048576 | tf_op jit(solution)/shard_map/decode/pallas_call | solution.py:304
  23.6 1.2 %collective-permute-start.12 = (bf16[8,4096]{1,0:T(8,128)(2,1)S(1)}, bf16[8,4096]{1,0:T(8,128)(2,1)S(1)}, u32[]{:S(2)}, u32[]{:S(2)}) collective-permute-start(bf16[8,4096]{1,0:T(8,128)(2,1)S(1)} %decode.1.rest_1_.refs_1_), channel_id=1, source_target_pairs={{0,12},{2,14},{4,8},{6,10},{8,4},{10,6},{12,0},{14,2},{1,13},{3,15... | collective-permute-start | bytes 196616 | tf_op jit(solution)/shard_map/ppermute | solution.py:179
  24.9 0.4 collective-permute-start.10
  25.3 2.8 %collective-permute-start.8 = (bf16[8,4096]{1,0:T(8,128)(2,1)S(1)}, bf16[8,4096]{1,0:T(8,128)(2,1)S(1)}, u32[]{:S(2)}, u32[]{:S(2)}) collective-permute-start(bf16[8,4096]{1,0:T(8,128)(2,1)S(1)} %decode.1.rest_1_.refs_1_), channel_id=1, source_target_pairs={{0,4},{2,6},{4,0},{6,2},{8,12},{10,14},{12,8},{14,10},{1,5},{3,7},... | collective-permute-start | bytes 196616 | tf_op jit(solution)/shard_map/ppermute | solution.py:179
  28.1 0.0 collective-permute-start.7
  28.1 2.4 %collective-permute-done.12.refs_7_ = bf16[8,4096]{1,0:T(8,128)(2,1)S(1)} collective-permute-done((bf16[8,4096]{1,0:T(8,128)(2,1)S(1)}, bf16[8,4096]{1,0:T(8,128)(2,1)S(1)}, u32[]{:S(2)}, u32[]{:S(2)}) %collective-permute-start.12) | collective-permute-done | bytes 65568 | tf_op jit(solution)/shard_map/ppermute | solution.py:179
  30.5 0.0 collective-permute-start.13
  30.5 1.8 %collective-permute-done.10.refs_5_ = bf16[8,4096]{1,0:T(8,128)(2,1)S(1)} collective-permute-done((bf16[8,4096]{1,0:T(8,128)(2,1)S(1)}, bf16[8,4096]{1,0:T(8,128)(2,1)S(1)}, u32[]{:S(2)}, u32[]{:S(2)}) %collective-permute-start.10) | collective-permute-done | bytes 65568 | tf_op jit(solution)/shard_map/ppermute | solution.py:179
  32.3 0.0 collective-permute-start.11
  32.3 0.0 collective-permute-done.8.refs_3_
  32.3 0.5 %collective-permute-start.9 = (bf16[8,4096]{1,0:T(8,128)(2,1)S(1)}, bf16[8,4096]{1,0:T(8,128)(2,1)S(1)}, u32[]{:S(2)}, u32[]{:S(2)}) collective-permute-start(bf16[8,4096]{1,0:T(8,128)(2,1)S(1)} %collective-permute-done.8.refs_3_), channel_id=1, source_target_pairs={{0,2},{2,0},{4,6},{6,4},{8,10},{10,8},{12,14},{14,12},{1,3},{3,1},... | collective-permute-start | bytes 196616 | tf_op jit(solution)/shard_map/ppermute | solution.py:181
  32.8 0.0 copy-done.2
  32.8 5.5 %shard_map.132 = (bf16[448,4096]{1,0:T(8,128)(2,1)}, f32[8,128]{1,0:T(8,128)S(1)}) custom-call(s32[1,448]{1,0:T(1,128)S(1)} %copy-done.2, bf16[448,4096]{1,0:T(8,128)(2,1)} %q_hbm.3, bf16[448,512]{1,0:T(8,128)(2,1)} %k_hbm.3, bf16[448,512]{1,0:T(8,128)(2,1)} %v_hbm.3, bf16[448,4096]{1,0:T(8,128)(2,1)} %get-tuple-element.8.rest_0_, ...), custom_call_target="tpu_custom_call", output_to_operand_aliasing={{0}: (4, {})} | custom-call | flops 939524096 | bytes 3670016 | tf_op jit(solution)/shard_map/pallas_call | solution.py:136
  38.3 0.0 collective-permute-done.7.refs_2_
  38.3 0.0 collective-permute-done.13.refs_8_
  38.3 0.0 collective-permute-done.11.refs_6_
  38.3 0.0 collective-permute-done.9.refs_4_
  38.4 0.0 slice-done
  38.4 2.7 %project.1 = (f32[16,1024]{1,0:T(8,128)S(1)}, f32[16,1024]{1,0:T(8,128)S(1)}) custom-call(s32[32]{0:T(128)S(1)} %copy-done.3, bf16[8,4096]{1,0:T(8,128)(2,1)S(1)} %decode.1.rest_1_.refs_1_, bf16[8,4096]{1,0:T(8,128)(2,1)S(1)} %collective-permute-done.7.refs_2_, bf16[8,4096]{1,0:T(8,128)(2,1)S(1)} %collective-permute-done.8.refs_3_, ...), custom_call_target="tpu_custom_call" | custom-call | flops 1000000000 | bytes 8388608 | tf_op jit(solution)/shard_map/project/pallas_call | solution.py:373
  41.1 1.6 %collective-permute-start.14 = (bf16[16,1024]{1,0:T(8,128)(2,1)S(1)}, bf16[16,1024]{1,0:T(8,128)(2,1)S(1)}, u32[]{:S(2)}, u32[]{:S(2)}) collective-permute-start(bf16[16,1024]{1,0:T(8,128)(2,1)S(1)} %convert_element_type.9), channel_id=1, source_target_pairs={{0,1},{1,0},{2,3},{3,2},{4,5},{5,4},{6,7},{7,6},{8,9},{9,8},{10,11... | collective-permute-start | bytes 98312 | tf_op jit(solution)/shard_map/ppermute | solution.py:436
  42.7 2.4 %collective-permute-done.14 = bf16[16,1024]{1,0:T(8,128)(2,1)S(1)} collective-permute-done((bf16[16,1024]{1,0:T(8,128)(2,1)S(1)}, bf16[16,1024]{1,0:T(8,128)(2,1)S(1)}, u32[]{:S(2)}, u32[]{:S(2)}) %collective-permute-start.14) | collective-permute-done | bytes 32800 | tf_op jit(solution)/shard_map/ppermute | solution.py:436
  45.1 0.6 %add_convert_fusion = bf16[16,1024]{1,0:T(8,128)(2,1)} fusion(f32[16,1024]{1,0:T(8,128)S(1)} %get-tuple-element.12, bf16[16,1024]{1,0:T(8,128)(2,1)S(1)} %collective-permute-done.14), kind=kLoop, calls=%fused_computation | loop fusion | flops 49152 | bytes 131072 | tf_op jit(solution)/shard_map/convert_element_type | solution.py:437
  (8 shorter events, 0.0 us)
Async XLA Ops:
  0.6 18.5 %copy-start.3 = (s32[32]{0:T(128)S(1)}, s32[32]{0:T(128)}, u32[]{:S(2)}) copy-start(s32[32]{0:T(128)} %refs_0_.3) | copy-start | bytes 388
  0.6 18.5 %copy-start.6 = (s32[32]{0:T(128)S(1)}, s32[32]{0:T(128)}, u32[]{:S(2)}) copy-start(s32[32]{0:T(128)} %refs_1_.1) | copy-start | bytes 388
  0.7 32.2 %copy-start.2 = (s32[1,448]{1,0:T(1,128)S(1)}, s32[1,448]{1,0:T(1,128)}, u32[]{:S(2)}) copy-start(s32[1,448]{1,0:T(1,128)} %doc_ref.3) | copy-start | bytes 5380
  2.1 17.1 %copy-start = (bf16[4,5120]{1,0:T(4,128)(2,1)S(1)}, bf16[4,5120]{1,0:T(4,128)(2,1)}, u32[]{:S(2)}) copy-start(bf16[4,5120]{1,0:T(4,128)(2,1)} %pack.1.refs_2_) | copy-start | bytes 122884
  2.1 7.3 %collective-permute-start.5 = (bf16[4,5120]{1,0:T(4,128)(2,1)}, bf16[4,5120]{1,0:T(4,128)(2,1)S(1)}, u32[]{:S(2)}, u32[]{:S(2)}) collective-permute-start(bf16[4,5120]{1,0:T(4,128)(2,1)} %pack.1.refs_2_), channel_id=1, source_target_pairs={{0,12},{2,14},{4,8},{6,10},{8,4},{10,6},{12,0},{14,2},{1,13},{3,15... | collective-permute-start | bytes 122888 | tf_op jit(solution)/shard_map/ppermute | solution.py:179
  7.1 5.1 %collective-permute-start.3 = (bf16[4,5120]{1,0:T(4,128)(2,1)}, bf16[4,5120]{1,0:T(4,128)(2,1)S(1)}, u32[]{:S(2)}, u32[]{:S(2)}) collective-permute-start(bf16[4,5120]{1,0:T(4,128)(2,1)} %pack.1.refs_2_), channel_id=1, source_target_pairs={{0,8},{2,10},{4,12},{6,14},{8,0},{10,2},{12,4},{14,6},{1,9},{3,11}... | collective-permute-start | bytes 122888 | tf_op jit(solution)/shard_map/ppermute | solution.py:179
  7.2 5.1 %collective-permute-start.1 = (bf16[4,5120]{1,0:T(4,128)(2,1)}, bf16[4,5120]{1,0:T(4,128)(2,1)S(1)}, u32[]{:S(2)}, u32[]{:S(2)}) collective-permute-start(bf16[4,5120]{1,0:T(4,128)(2,1)} %pack.1.refs_2_), channel_id=1, source_target_pairs={{0,4},{2,6},{4,0},{6,2},{8,12},{10,14},{12,8},{14,10},{1,5},{3,7},... | collective-permute-start | bytes 122888 | tf_op jit(solution)/shard_map/ppermute | solution.py:179
  7.7 11.3 %collective-permute-start = (bf16[4,5120]{1,0:T(4,128)(2,1)}, bf16[4,5120]{1,0:T(4,128)(2,1)S(1)}, u32[]{:S(2)}, u32[]{:S(2)}) collective-permute-start(bf16[4,5120]{1,0:T(4,128)(2,1)} %pack.1.refs_2_), channel_id=1, source_target_pairs={{0,2},{2,0},{4,6},{6,4},{8,10},{10,8},{12,14},{14,12},{1,3},{3,1},... | collective-permute-start | bytes 122888 | tf_op jit(solution)/shard_map/ppermute | solution.py:181
  9.4 9.7 %collective-permute-start.6 = (bf16[4,5120]{1,0:T(4,128)(2,1)S(1)}, bf16[4,5120]{1,0:T(4,128)(2,1)S(1)}, u32[]{:S(2)}, u32[]{:S(2)}) collective-permute-start(bf16[4,5120]{1,0:T(4,128)(2,1)S(1)} %collective-permute-done.5.refs_8_), channel_id=1, source_target_pairs={{0,2},{2,0},{4,6},{6,4},{8,10},{10,8},{12,14},{14,12},{1,3},{3,1},... | collective-permute-start | bytes 122888 | tf_op jit(solution)/shard_map/ppermute | solution.py:181
  12.3 6.8 %collective-permute-start.4 = (bf16[4,5120]{1,0:T(4,128)(2,1)S(1)}, bf16[4,5120]{1,0:T(4,128)(2,1)S(1)}, u32[]{:S(2)}, u32[]{:S(2)}) collective-permute-start(bf16[4,5120]{1,0:T(4,128)(2,1)S(1)} %collective-permute-done.3.refs_6_), channel_id=1, source_target_pairs={{0,2},{2,0},{4,6},{6,4},{8,10},{10,8},{12,14},{14,12},{1,3},{3,1},... | collective-permute-start | bytes 122888 | tf_op jit(solution)/shard_map/ppermute | solution.py:181
  12.3 6.8 %collective-permute-start.2 = (bf16[4,5120]{1,0:T(4,128)(2,1)S(1)}, bf16[4,5120]{1,0:T(4,128)(2,1)S(1)}, u32[]{:S(2)}, u32[]{:S(2)}) collective-permute-start(bf16[4,5120]{1,0:T(4,128)(2,1)S(1)} %collective-permute-done.1.refs_4_), channel_id=1, source_target_pairs={{0,2},{2,0},{4,6},{6,4},{8,10},{10,8},{12,14},{14,12},{1,3},{3,1},... | collective-permute-start | bytes 122888 | tf_op jit(solution)/shard_map/ppermute | solution.py:181
  12.8 0.7 %copy-start.1 = (s32[1,448]{1,0:T(1,128)S(1)}, s32[1,448]{1,0:T(1,128)}, u32[]{:S(2)}) copy-start(s32[1,448]{1,0:T(1,128)} %doc_ref.3) | copy-start | bytes 5380
  13.5 24.9 %slice-start = ((s8[8388608]{0:T(1024)(128)(4,1)}), s8[4194304]{0:T(1024)(128)(4,1)S(1)}, s32[]{:S(2)}) async-start(s8[8388608]{0:T(1024)(128)(4,1)} %bitcast), calls=%async_computation | async-start | bytes 8388608
  19.1 1.0 %copy-start.4 = (bf16[512,512]{1,0:T(8,128)(2,1)S(1)}, bf16[512,512]{1,0:T(8,128)(2,1)}, u32[]{:S(2)}) copy-start(bf16[512,512]{1,0:T(8,128)(2,1)} %refs_10_.1) | copy-start | bytes 1572868
  20.2 1.0 %copy-start.5 = (bf16[512,512]{1,0:T(8,128)(2,1)S(1)}, bf16[512,512]{1,0:T(8,128)(2,1)}, u32[]{:S(2)}) copy-start(bf16[512,512]{1,0:T(8,128)(2,1)} %refs_11_.1) | copy-start | bytes 1572868
  23.6 6.8 %collective-permute-start.12 = (bf16[8,4096]{1,0:T(8,128)(2,1)S(1)}, bf16[8,4096]{1,0:T(8,128)(2,1)S(1)}, u32[]{:S(2)}, u32[]{:S(2)}) collective-permute-start(bf16[8,4096]{1,0:T(8,128)(2,1)S(1)} %decode.1.rest_1_.refs_1_), channel_id=1, source_target_pairs={{0,12},{2,14},{4,8},{6,10},{8,4},{10,6},{12,0},{14,2},{1,13},{3,15... | collective-permute-start | bytes 196616 | tf_op jit(solution)/shard_map/ppermute | solution.py:179
  24.9 7.4 %collective-permute-start.10 = (bf16[8,4096]{1,0:T(8,128)(2,1)S(1)}, bf16[8,4096]{1,0:T(8,128)(2,1)S(1)}, u32[]{:S(2)}, u32[]{:S(2)}) collective-permute-start(bf16[8,4096]{1,0:T(8,128)(2,1)S(1)} %decode.1.rest_1_.refs_1_), channel_id=1, source_target_pairs={{0,8},{2,10},{4,12},{6,14},{8,0},{10,2},{12,4},{14,6},{1,9},{3,11}... | collective-permute-start | bytes 196616 | tf_op jit(solution)/shard_map/ppermute | solution.py:179
  25.3 7.0 %collective-permute-start.8 = (bf16[8,4096]{1,0:T(8,128)(2,1)S(1)}, bf16[8,4096]{1,0:T(8,128)(2,1)S(1)}, u32[]{:S(2)}, u32[]{:S(2)}) collective-permute-start(bf16[8,4096]{1,0:T(8,128)(2,1)S(1)} %decode.1.rest_1_.refs_1_), channel_id=1, source_target_pairs={{0,4},{2,6},{4,0},{6,2},{8,12},{10,14},{12,8},{14,10},{1,5},{3,7},... | collective-permute-start | bytes 196616 | tf_op jit(solution)/shard_map/ppermute | solution.py:179
  28.1 10.2 %collective-permute-start.7 = (bf16[8,4096]{1,0:T(8,128)(2,1)S(1)}, bf16[8,4096]{1,0:T(8,128)(2,1)S(1)}, u32[]{:S(2)}, u32[]{:S(2)}) collective-permute-start(bf16[8,4096]{1,0:T(8,128)(2,1)S(1)} %decode.1.rest_1_.refs_1_), channel_id=1, source_target_pairs={{0,2},{2,0},{4,6},{6,4},{8,10},{10,8},{12,14},{14,12},{1,3},{3,1},... | collective-permute-start | bytes 196616 | tf_op jit(solution)/shard_map/ppermute | solution.py:181
  30.5 7.9 %collective-permute-start.13 = (bf16[8,4096]{1,0:T(8,128)(2,1)S(1)}, bf16[8,4096]{1,0:T(8,128)(2,1)S(1)}, u32[]{:S(2)}, u32[]{:S(2)}) collective-permute-start(bf16[8,4096]{1,0:T(8,128)(2,1)S(1)} %collective-permute-done.12.refs_7_), channel_id=1, source_target_pairs={{0,2},{2,0},{4,6},{6,4},{8,10},{10,8},{12,14},{14,12},{1,3},{3,1},... | collective-permute-start | bytes 196616 | tf_op jit(solution)/shard_map/ppermute | solution.py:181
  32.3 6.0 %collective-permute-start.11 = (bf16[8,4096]{1,0:T(8,128)(2,1)S(1)}, bf16[8,4096]{1,0:T(8,128)(2,1)S(1)}, u32[]{:S(2)}, u32[]{:S(2)}) collective-permute-start(bf16[8,4096]{1,0:T(8,128)(2,1)S(1)} %collective-permute-done.10.refs_5_), channel_id=1, source_target_pairs={{0,2},{2,0},{4,6},{6,4},{8,10},{10,8},{12,14},{14,12},{1,3},{3,1},... | collective-permute-start | bytes 196616 | tf_op jit(solution)/shard_map/ppermute | solution.py:181
  32.3 6.0 %collective-permute-start.9 = (bf16[8,4096]{1,0:T(8,128)(2,1)S(1)}, bf16[8,4096]{1,0:T(8,128)(2,1)S(1)}, u32[]{:S(2)}, u32[]{:S(2)}) collective-permute-start(bf16[8,4096]{1,0:T(8,128)(2,1)S(1)} %collective-permute-done.8.refs_3_), channel_id=1, source_target_pairs={{0,2},{2,0},{4,6},{6,4},{8,10},{10,8},{12,14},{14,12},{1,3},{3,1},... | collective-permute-start | bytes 196616 | tf_op jit(solution)/shard_map/ppermute | solution.py:181
  32.8 5.5 %slice-start.1 = ((s8[8388608]{0:T(1024)(128)(4,1)}), s8[4194304]{0:T(1024)(128)(4,1)S(1)}, s32[]{:S(2)}) async-start(s8[8388608]{0:T(1024)(128)(4,1)} %bitcast), calls=%async_computation.1 | async-start | bytes 8388608
  41.1 4.0 %collective-permute-start.14 = (bf16[16,1024]{1,0:T(8,128)(2,1)S(1)}, bf16[16,1024]{1,0:T(8,128)(2,1)S(1)}, u32[]{:S(2)}, u32[]{:S(2)}) collective-permute-start(bf16[16,1024]{1,0:T(8,128)(2,1)S(1)} %convert_element_type.9), channel_id=1, source_target_pairs={{0,1},{1,0},{2,3},{3,2},{4,5},{5,4},{6,7},{7,6},{8,9},{9,8},{10,11... | collective-permute-start | bytes 98312 | tf_op jit(solution)/shard_map/ppermute | solution.py:436
where the time goes:
time: 46.1 us; the launch traced here: 45.7 us
  Pallas kernels  17.6 us (38%)
  starting transfers between devices  12.7 us (28%)
  waiting for transfers between devices  11.2 us (24%)
  local copies, waits for them, and re-layouts  2.78 us (6%)
  between operations  0.83 us (2%)
  other arithmetic  0.63 us (1%)
    pallas_call x2, Pallas kernels, prompt_part(): pl.pallas_call(functools.partial(prompt_kernel, len(extra), first, count,...  11.1 us
    ppermute x6, starting transfers between devices, spread(): pieces[d] = lax.ppermute(x, 'pool', [(i, i ^ d) for i in range(n)])  10.1 us
    ppermute x6, waiting for transfers between devices, spread(): pieces[d] = lax.ppermute(x, 'pool', [(i, i ^ d) for i in range(n)])  8.75 us
    unnamed x18, local copies, waits for them, and re-layouts  2.78 us
    pallas_call x1, Pallas kernels, project(): pl.pallas_call(functools.partial(project_kernel, n, len(pieces), cap, slo...  2.74 us
    ppermute x1, waiting for transfers between devices, local(): other = lax.ppermute(send.astype(jnp.bfloat16), 'tp', [(0, 1), (1, 0)])  2.43 us
    pallas_call x1, Pallas kernels, decode(): pl.pallas_call(functools.partial(decode_kernel, n, len(pieces), home_rows...  2.41 us
    ppermute x1, starting transfers between devices, local(): other = lax.ppermute(send.astype(jnp.bfloat16), 'tp', [(0, 1), (1, 0)])  1.55 us
  transfers between devices with their start and end apart: 15, of which 5 were waited for; matrix products, arithmetic and copies ran while one was open for 0% of the time, Pallas kernels for 24%

commit v1 on v0

v1 whole, which is shorter than its diff:
```python
import functools

import jax
import jax.numpy as jnp
from jax import lax
from jax.experimental import pallas as pl
from jax.experimental.pallas import tpu as pltpu
from jax.sharding import PartitionSpec as P


HEAD_DIM = 128
LOG2E = 1.4426950408889634
ROW_BLOCK = 32
VMEM = pl.BlockSpec(memory_space=pltpu.VMEM)
HBM = pl.BlockSpec(memory_space=pltpu.HBM)


def attend(items, group, window, ready, q_ref, k_ref, v_ref, bias_ref, s_ref, p_ref,
           o_ref, finished):
    block = ROW_BLOCK
    stacked = group * block
    scale = HEAD_DIM ** (-0.5) * LOG2E

    def place_of(t):
        head, b = items[t]
        start = max(0, (b + 1) * block - window)
        span = min(window, -(-(b + 1) * block // HEAD_DIM) * HEAD_DIM)
        return head, b, slice(b * block, (b + 1) * block), start, span

    def score(t):
        head, _, at, start, span = place_of(t)
        query = jnp.concatenate(
            [q_ref[head, at, h * HEAD_DIM : (h + 1) * HEAD_DIM] for h in range(group)], axis=0
        )
        s_ref[t % 2, :, :span] = lax.dot_general(
            query,
            k_ref[head, start : start + span, :],
            (((1,), (1,)), ((), ())),
            preferred_element_type=jnp.float32,
        )

    def weigh(t):
        _, b, _, _, span = place_of(t)
        scores = s_ref[t % 2, :, :span].reshape(group, block, span) * scale
        scores = scores + bias_ref[b, :, :span][None]
        highest = jnp.max(scores, axis=-1, keepdims=True)
        weights = jnp.exp2(scores - highest).astype(jnp.bfloat16).reshape(stacked, span)
        for c in range(span // HEAD_DIM):
            p_ref[t % 2, c] = weights[:, c * HEAD_DIM : (c + 1) * HEAD_DIM]

    def combine(t):
        head, _, at, start, span = place_of(t)
        values = v_ref[head, start : start + span, :]
        values = jnp.concatenate([values, jnp.ones_like(values)], axis=1)
        weights = jnp.concatenate([p_ref[t % 2, c] for c in range(span // HEAD_DIM)], axis=1)
        both = jnp.dot(weights, values, preferred_element_type=jnp.float32)
        result = (both[:, :HEAD_DIM] / both[:, HEAD_DIM:]).astype(jnp.bfloat16)
        for h in range(group):
            o_ref[head, at, h * HEAD_DIM : (h + 1) * HEAD_DIM] = result[
                h * block : (h + 1) * block
            ]

    total = len(items)
    for t in range(total + 2):
        if t < total:
            ready(*items[t])
        if t >= 2:
            combine(t - 2)
        if t < total:
            score(t)
        if 1 <= t <= total:
            weigh(t - 1)
        if t >= 2:
            finished(*items[t - 2])


def early_kernel(n, tp, early, group, window, home_rows, slots, *refs):
    (doc_hbm, q_hbm, k_hbm, v_hbm, start_hbm, len_hbm, ck_hbm, cv_hbm) = refs[:8]
    (o_ref, q2_ref, k2_ref, v2_ref, bias_ref, ck_ref, cv_ref, pick_ref, seg_ref, gather_ref) = (
        refs[8:18]
    )
    (doc_ref, q_ref, k_ref, v_ref, s_ref, p_ref, pick32, gather32) = refs[18:26]
    (start_ref, len_ref, seen_ref, source_ref, slot_ref, sems) = refs[26:]
    rows = q_hbm.shape[0]
    width = group * HEAD_DIM
    kv_local = k_hbm.shape[1] // HEAD_DIM
    block = ROW_BLOCK
    blocks = rows // block
    cap = ck_hbm.shape[0]
    requests = start_hbm.shape[0]
    half = (blocks + 1) // 2 * block

    copies = {}

    def begin(name, src, dst):
        copy = pltpu.make_async_copy(src, dst, sems.at[len(copies)])
        copies[name] = copy
        copy.start()

    begin("doc", doc_hbm, doc_ref)
    begin("start", start_hbm, start_ref)
    begin("len", len_hbm, len_ref)
    for i in range(early):
        lanes = slice(i * HEAD_DIM, (i + 1) * HEAD_DIM)
        cols = slice(i * width, (i + 1) * width)
        begin(("k", i), k_hbm.at[:, lanes], k_ref.at[i])
        begin(("q", i, 0), q_hbm.at[:half, cols], q_ref.at[i, :half])
        begin(("v", i), v_hbm.at[:, lanes], v_ref.at[i])
        begin(("q", i, 1), q_hbm.at[half:, cols], q_ref.at[i, half:])
    begin("ck", ck_hbm, ck_ref)
    begin("cv", cv_hbm, cv_ref)
    late = []
    for i in range(early, kv_local):
        lanes = slice(i * HEAD_DIM, (i + 1) * HEAD_DIM)
        begin(("k2", i), k_hbm.at[:, lanes], k2_ref.at[i - early])
        begin(("v2", i), v_hbm.at[:, lanes], v2_ref.at[i - early])
        begin(("q2", i), q_hbm.at[:, i * width : (i + 1) * width], q2_ref.at[i - early])
        late += [("k2", i), ("v2", i), ("q2", i)]

    copies["start"].wait()
    copies["len"].wait()
    me = lax.axis_index("pool")
    for owner in range(n):
        seen_ref[owner] = 0
    for m in range(slots):
        slot_ref[m] = -1

    def locate(r, carry):
        owner = start_ref[r] // cap
        rank = seen_ref[owner]
        seen_ref[owner] = rank + 1
        source_ref[r] = place(owner, me, n) * slots + rank

        @pl.when(owner == me)
        def _():
            slot_ref[jnp.minimum(rank, slots - 1)] = r

        return carry

    lax.fori_loop(0, requests, locate, 0)
    homes = lax.broadcasted_iota(jnp.int32, (1, pick32.shape[1]), 1)
    pooled = lax.broadcasted_iota(jnp.int32, (1, gather32.shape[1]), 1)
    cells = lax.broadcasted_iota(jnp.int32, (1, cap), 1)
    for m in range(slots):
        r = slot_ref[m]
        used = r >= 0
        r = jnp.maximum(r, 0)
        row = place(r // home_rows, me, n) * home_rows + r % home_rows
        row = jnp.where(used, row, -1)
        first = start_ref[r] - me * cap
        last = first + jnp.where(used, len_ref[r], 0)
        pick32[m : m + 1, :] = jnp.where(homes == row, 1.0, 0.0)
        seg_ref[m : m + 1, :] = jnp.where((cells >= first) & (cells < last), 0.0, -jnp.inf)
    pick_ref[...] = pick32[...].astype(jnp.bfloat16)
    if tp == 2:
        turn = (1 - lax.axis_index("tp")) * (requests // 2)
    else:
        turn = 0

    def gather(i, carry):
        r = i + turn
        r = jnp.where(r >= requests, r - requests, r)
        gather32[pl.ds(i, 1), :] = jnp.where(pooled == source_ref[r], 1.0, 0.0)
        return carry

    lax.fori_loop(0, requests, gather, 0)
    gather_ref[...] = gather32[...].astype(jnp.bfloat16)

    copies["doc"].wait()
    for b in range(blocks):
        start = max(0, (b + 1) * block - window)
        key_doc = jnp.broadcast_to(
            doc_ref[:, start : start + window].astype(jnp.float32), (block, window)
        )
        row = lax.broadcasted_iota(jnp.int32, (block, window), 0) + b * block
        col = lax.broadcasted_iota(jnp.int32, (block, window), 1) + start
        row_doc = jnp.sum(jnp.where(row == col, key_doc, 0.0), axis=1, keepdims=True)
        allowed = (col <= row) & (key_doc == row_doc)
        bias_ref[b] = jnp.where(allowed, 0.0, -jnp.inf)

    def ready(head, b):
        if b == 0:
            copies["k", head].wait()
            copies["q", head, 0].wait()
            copies["v", head].wait()
        if b == half // block:
            copies["q", head, 1].wait()

    items = [(head, b) for head in range(early) for b in range(blocks)]
    attend(items, group, window, ready, q_ref, k_ref, v_ref, bias_ref, s_ref, p_ref,
           o_ref, lambda head, b: None)
    for name in ["ck", "cv"] + late:
        copies[name].wait()


def late_kernel(early, group, window, *refs):
    (o1_ref, q_ref, k_ref, v_ref, bias_ref, _, out_hbm) = refs[:7]
    (o_ref, s_ref, p_ref, sems) = refs[7:]
    late, rows, width = q_ref.shape
    blocks = rows // ROW_BLOCK
    cut = blocks // 2
    copies = []

    def store(src, dst):
        copy = pltpu.make_async_copy(src, dst, sems.at[len(copies)])
        copies.append(copy)
        copy.start()

    for i in range(early):
        store(o1_ref.at[i], out_hbm.at[:, i * width : (i + 1) * width])

    def finished(head, b):
        if b + 1 in (cut, blocks):
            span = slice(0, cut * ROW_BLOCK) if b + 1 == cut else slice(cut * ROW_BLOCK, rows)
            cols = slice((early + head) * width, (early + head + 1) * width)
            store(o_ref.at[head, span], out_hbm.at[span, cols])

    items = [(head, b) for head in range(late) for b in range(blocks)]
    attend(items, group, window, lambda head, b: None, q_ref, k_ref, v_ref, bias_ref,
           s_ref, p_ref, o_ref, finished)
    for copy in copies:
        copy.wait()


def pipeline_scratch(group, window):
    stacked = group * ROW_BLOCK
    return [
        pltpu.VMEM((2, stacked, window), jnp.float32),
        pltpu.VMEM((2, window // HEAD_DIM, stacked, HEAD_DIM), jnp.bfloat16),
    ]


def cost(group, rows, window, heads):
    return pl.CostEstimate(
        flops=4 * heads * group * rows * window * HEAD_DIM,
        bytes_accessed=4 * rows * group * HEAD_DIM * heads,
        transcendentals=0,
    )


def early_part(n, tp, early, group, window, home_rows, doc_ids, query, key, value, start, length,
               cache_keys, cache_values):
    rows, width = query.shape[0], group * HEAD_DIM
    kv_local = key.shape[1] // HEAD_DIM
    late = kv_local - early
    blocks = rows // ROW_BLOCK
    slots = 2 * home_rows
    requests = start.shape[0]
    bf16, f32 = jnp.bfloat16, jnp.float32
    out_shape = [
        jax.ShapeDtypeStruct((early, rows, width), bf16),
        jax.ShapeDtypeStruct((late, rows, width), bf16),
        jax.ShapeDtypeStruct((late, rows, HEAD_DIM), bf16),
        jax.ShapeDtypeStruct((late, rows, HEAD_DIM), bf16),
        jax.ShapeDtypeStruct((blocks, ROW_BLOCK, window), f32),
        jax.ShapeDtypeStruct(cache_keys.shape, bf16),
        jax.ShapeDtypeStruct(cache_values.shape, bf16),
        jax.ShapeDtypeStruct((slots, n * home_rows), bf16),
        jax.ShapeDtypeStruct((slots, cache_keys.shape[0]), f32),
        jax.ShapeDtypeStruct((requests, n * slots), bf16),
    ]
    operands = (doc_ids, query, key, value, start, length, cache_keys, cache_values)
    return pl.pallas_call(
        functools.partial(early_kernel, n, tp, early, group, window, home_rows, slots),
        in_specs=[HBM] * len(operands),
        out_specs=[VMEM] * len(out_shape),
        out_shape=out_shape,
        scratch_shapes=[
            pltpu.VMEM(doc_ids.shape, jnp.int32),
            pltpu.VMEM((early, rows, width), bf16),
            pltpu.VMEM((early, rows, HEAD_DIM), bf16),
            pltpu.VMEM((early, rows, HEAD_DIM), bf16),
            *pipeline_scratch(group, window),
            pltpu.VMEM((slots, n * home_rows), f32),
            pltpu.VMEM((requests, n * slots), f32),
            pltpu.SMEM((requests,), jnp.int32),
            pltpu.SMEM((requests,), jnp.int32),
            pltpu.SMEM((n,), jnp.int32),
            pltpu.SMEM((requests,), jnp.int32),
            pltpu.SMEM((slots,), jnp.int32),
            pltpu.SemaphoreType.DMA((5 + 4 * early + 3 * late,)),
        ],
        cost_estimate=cost(group, rows, window, early),
        compiler_params=pltpu.CompilerParams(vmem_limit_bytes=24 << 20),
        name="early",
    )(*(pltpu.with_memory_space_constraint(x, pltpu.HBM) for x in operands))


def late_part(early, group, window, shape, first, q, k, v, bias, after):
    late, rows, width = q.shape
    return pl.pallas_call(
        functools.partial(late_kernel, early, group, window),
        in_specs=[VMEM] * 6,
        out_specs=HBM,
        out_shape=jax.ShapeDtypeStruct(shape, jnp.bfloat16),
        scratch_shapes=[
            pltpu.VMEM((late, rows, width), jnp.bfloat16),
            *pipeline_scratch(group, window),
            pltpu.SemaphoreType.DMA((early + 2 * late,)),
        ],
        cost_estimate=cost(group, rows, window, late),
        compiler_params=pltpu.CompilerParams(vmem_limit_bytes=24 << 20),
        name="late",
    )(first, q, k, v, bias, after)


def xor_plan(n):
    return n & (n - 1) == 0 and 2 <= n <= 8


def spread(x, n):
    if not xor_plan(n):
        return [lax.all_gather(x, "pool", axis=0, tiled=True)]
    pieces = {0: x}
    for d in range(n - 2, 0, -2):
        pieces[d] = lax.ppermute(x, "pool", [(i, i ^ d) for i in range(n)])
    for d in range(0, n, 2):
        pieces[d + 1] = lax.ppermute(
            pieces[d], "pool", [(i, i ^ 1) for i in range(n)]
        )
    return [pieces[d] for d in range(n)]


def place(index, me, n):
    return index ^ me if xor_plan(n) else index


def pack_kernel(q_ref, k_ref, v_ref, o_ref):
    dq, dk = q_ref.shape[1], k_ref.shape[1]
    o_ref[:, :dq] = q_ref[...]
    o_ref[:, dq : dq + dk] = k_ref[...]
    o_ref[:, dq + dk :] = v_ref[...]


def pack(q, k, v):
    shape = (q.shape[0], q.shape[1] + k.shape[1] + v.shape[1])
    return pl.pallas_call(
        pack_kernel,
        in_specs=[VMEM] * 3,
        out_specs=VMEM,
        out_shape=pltpu.VMEM(shape, q.dtype),
        name="pack",
    )(q, k, v)


def decode_kernel(kv_local, group, count, *refs):
    pieces = refs[:count]
    pick_ref, seg_ref, k_ref, v_ref, o_ref, all_ref = refs[count:]
    slots, cap = seg_ref.shape
    q_width = kv_local * group * HEAD_DIM
    kv_width = kv_local * HEAD_DIM
    per = all_ref.shape[0] // count
    for i, piece in enumerate(pieces):
        all_ref[i * per : (i + 1) * per, :] = piece[...].astype(jnp.float32)
    bias = seg_ref[...]
    scale = HEAD_DIM ** (-0.5) * LOG2E

    def slot_rows(first, width):
        return jnp.dot(
            pick_ref[...],
            all_ref[:, first : first + width].astype(jnp.bfloat16),
            preferred_element_type=jnp.float32,
        )

    for g in range(kv_local):
        base = g * group * HEAD_DIM
        slot_q = slot_rows(base, group * HEAD_DIM)
        new_key = slot_rows(q_width + g * HEAD_DIM, HEAD_DIM)
        new_value = slot_rows(q_width + kv_width + g * HEAD_DIM, HEAD_DIM)
        q32 = jnp.concatenate(
            [slot_q[:, h * HEAD_DIM : (h + 1) * HEAD_DIM] for h in range(group)], axis=0
        )
        lanes = slice(g * HEAD_DIM, (g + 1) * HEAD_DIM)
        scores = lax.dot_general(
            q32.astype(jnp.bfloat16),
            k_ref[:, lanes],
            (((1,), (1,)), ((), ())),
            preferred_element_type=jnp.float32,
        )
        scores = scores.reshape(group, slots, cap) * scale + bias[None]
        own = (
            jnp.sum(q32.reshape(group, slots, HEAD_DIM) * new_key[None], axis=-1, keepdims=True)
            * scale
        )
        highest = jnp.maximum(jnp.max(scores, axis=-1, keepdims=True), own)
        weights = jnp.exp2(scores - highest)
        own_weight = jnp.exp2(own - highest)
        inverse = 1.0 / (jnp.sum(weights, axis=-1, keepdims=True) + own_weight)
        probs = (weights * inverse).astype(jnp.bfloat16)
        own_prob = (own_weight * inverse).astype(jnp.bfloat16).astype(jnp.float32)
        result = jnp.dot(
            probs.reshape(group * slots, cap),
            v_ref[:, lanes],
            preferred_element_type=jnp.float32,
        ).reshape(group, slots, HEAD_DIM)
        result = result + own_prob * new_value[None]
        for h in range(group):
            o_ref[:, base + h * HEAD_DIM : base + (h + 1) * HEAD_DIM] = result[h].astype(
                jnp.bfloat16
            )


def decode(pieces, pick, seg, cache_keys, cache_values, group):
    kv_local = cache_keys.shape[1] // HEAD_DIM
    total = sum(p.shape[0] for p in pieces)
    width = pieces[0].shape[1]
    operands = (*pieces, pick, seg, cache_keys, cache_values)
    return pl.pallas_call(
        functools.partial(decode_kernel, kv_local, group, len(pieces)),
        in_specs=[VMEM] * len(operands),
        out_specs=VMEM,
        out_shape=jax.ShapeDtypeStruct(
            (pick.shape[0], kv_local * group * HEAD_DIM), jnp.bfloat16
        ),
        scratch_shapes=[pltpu.VMEM((total, width), jnp.float32)],
        cost_estimate=pl.CostEstimate(
            flops=10**9, bytes_accessed=4 * cache_keys.size, transcendentals=0
        ),
        compiler_params=pltpu.CompilerParams(vmem_limit_bytes=24 << 20),
        name="decode",
    )(*operands)


def project_kernel(count, tp, *refs):
    pieces = refs[:count]
    gather_ref, w_ref, _, *outs = refs[count:]
    step = min(512, w_ref.shape[0])
    total = None
    for first in range(0, w_ref.shape[0], step):
        cols = slice(first, first + step)
        if count == 1:
            rows = pieces[0][:, cols]
        else:
            rows = jnp.concatenate([p[:, cols] for p in pieces], axis=0)
        rows = jnp.dot(gather_ref[...], rows, preferred_element_type=jnp.float32)
        part = jnp.dot(
            rows.astype(jnp.bfloat16), w_ref[cols, :], preferred_element_type=jnp.float32
        )
        total = part if total is None else total + part
    if tp == 2:
        half = total.shape[0] // 2
        outs[0][...] = total[:half].astype(outs[0].dtype)
        outs[1][...] = total[half:]
    else:
        outs[0][...] = total


def project(pieces, gather, weight, tp, after):
    requests, cols = gather.shape[0], weight.shape[1]
    if tp == 2:
        out_shape = [
            jax.ShapeDtypeStruct((requests // 2, cols), jnp.bfloat16),
            jax.ShapeDtypeStruct((requests // 2, cols), jnp.float32),
        ]
    else:
        out_shape = [jax.ShapeDtypeStruct((requests, cols), jnp.float32)]
    return pl.pallas_call(
        functools.partial(project_kernel, len(pieces), tp),
        in_specs=[VMEM] * (len(pieces) + 2) + [HBM],
        out_specs=[VMEM] * len(out_shape),
        out_shape=out_shape,
        cost_estimate=pl.CostEstimate(
            flops=10**9, bytes_accessed=2 * weight.size, transcendentals=0
        ),
        compiler_params=pltpu.CompilerParams(vmem_limit_bytes=40 << 20),
        name="project",
    )(*pieces, gather, weight, after)


def local(
    n,
    tp,
    home_query,
    home_key,
    home_value,
    cache_keys,
    cache_values,
    cache_start,
    cache_len,
    prompt_query,
    prompt_key,
    prompt_value,
    doc_ids,
    out_weight,
):
    home_rows = home_query.shape[0]
    rows = prompt_query.shape[0]
    kv_local = home_key.shape[1] // HEAD_DIM
    group = home_query.shape[1] // HEAD_DIM // kv_local
    window = min(rows, rows // 2 + ROW_BLOCK)
    early = kv_local // 2

    homes = spread(pack(home_query, home_key, home_value), n)
    first, q2, k2, v2, bias, ck, cv, pick, seg, gather = early_part(
        n, tp, early, group, window, home_rows, doc_ids, prompt_query, prompt_key,
        prompt_value, cache_start, cache_len, cache_keys, cache_values,
    )
    slot_out = decode(homes, pick, seg, ck, cv, group)
    pooled = spread(slot_out, n)
    prompt_out = late_part(
        early, group, window, prompt_query.shape, first, q2, k2, v2, bias, slot_out
    )
    partial = project(pooled, gather, out_weight, tp, prompt_out)
    if tp == 2:
        send, keep = partial
        other = lax.ppermute(send, "tp", [(0, 1), (1, 0)])
        decode_out = (keep + other.astype(jnp.float32)).astype(jnp.bfloat16)
    else:
        decode_out = lax.psum_scatter(
            partial[0], "tp", scatter_dimension=0, tiled=True
        ).astype(jnp.bfloat16)
    return (prompt_out, decode_out)


def layer(n, tp, *args):
    return local(n, tp, *args)


def solution(mesh):
    step = jax.shard_map(
        functools.partial(layer, mesh.shape["pool"], mesh.shape["tp"]),
        mesh=mesh,
        in_specs=(
            P(("grp", "pool"), "tp"),
            P(("grp", "pool"), "tp"),
            P(("grp", "pool"), "tp"),
            P(("grp", "pool"), "tp"),
            P(("grp", "pool"), "tp"),
            P("grp"),
            P("grp"),
            P(("grp", "pool"), "tp"),
            P(("grp", "pool"), "tp"),
            P(("grp", "pool"), "tp"),
            P(("grp", "pool"), None),
            P("tp", "pool"),
        ),
        out_specs=(P(("grp", "pool"), "tp"), P(("grp", "tp"), "pool")),
        check_vma=False,
    )
    n = mesh.shape["pool"]
    return step if xor_plan(n) else step
```

time: 46.1 us -> 41.7 us (0.905)
  Pallas kernels: 17.6 us -> 14.4 us
  local copies, waits for them, and re-layouts: 2.78 us -> 2.05 us
    pallas_call x4, Pallas kernels: 16.2 us -> 13.6 us  [the longest x1 6.06 us: early_part(): pl.pallas_call(functools.partial(early_kernel, n, tp, early, group, windo...]
    unnamed x18 -> x6, local copies, waits for them, and re-layouts: 2.78 us -> 2.05 us
    pallas_call x1, Pallas kernels: 1.4 us -> 0.78 us  [pack(): pl.pallas_call(pack_kernel, in_specs=[VMEM] * 3, out_specs=VMEM, out_shap...]
  transfers between devices with their start and end apart: 15 -> 15, of which waited for: 5 -> 5; matrix products, arithmetic and copies ran while one was open for 0% -> 0% of each run, Pallas kernels for 24% -> 23%
where the time goes in v1:
time: 41.7 us; the launch traced here: 41.5 us
  Pallas kernels  14.4 us (35%)
  starting transfers between devices  12.6 us (30%)
  waiting for transfers between devices  11 us (26%)
  local copies, waits for them, and re-layouts  2.05 us (5%)
  between operations  0.76 us (2%)
  other arithmetic  0.62 us (1%)
    ppermute x6, starting transfers between devices, spread(): pieces[d] = lax.ppermute(x, 'pool', [(i, i ^ d) for i in range(n)])  10.1 us
    ppermute x6, waiting for transfers between devices, spread(): pieces[d] = lax.ppermute(x, 'pool', [(i, i ^ d) for i in range(n)])  8.56 us
    pallas_call x1, Pallas kernels, early_part(): pl.pallas_call(functools.partial(early_kernel, n, tp, early, group, windo...  6.06 us
    pallas_call x1, Pallas kernels, late_part(): pl.pallas_call(functools.partial(late_kernel, early, group, window), in_s...  3.52 us
    ppermute x1, waiting for transfers between devices, local(): other = lax.ppermute(send, 'tp', [(0, 1), (1, 0)])  2.43 us
    pallas_call x1, Pallas kernels, project(): pl.pallas_call(functools.partial(project_kernel, len(pieces), tp), in_spe...  2.13 us
    unnamed x6, local copies, waits for them, and re-layouts  2.05 us
    pallas_call x1, Pallas kernels, decode(): pl.pallas_call(functools.partial(decode_kernel, kv_local, group, len(piec...  1.9 us
  transfers between devices with their start and end apart: 15, of which 5 were waited for; matrix products, arithmetic and copies ran while one was open for 0% of the time, Pallas kernels for 23%

profile of v1, /device:TPU:0, one launch (start us, length us, event | category | flops | bytes accessed | tf_op | source)
XLA Modules:
  0.0 41.5 jit_solution(15850591117087921512)
XLA Ops:
  0.6 0.8 %pack.1.refs_0_ = bf16[4,5120]{1,0:T(4,128)(2,1)S(1)} custom-call(bf16[4,4096]{1,0:T(4,128)(2,1)} %q_ref.1, bf16[4,512]{1,0:T(4,128)(2,1)} %k_ref.1, bf16[4,512]{1,0:T(4,128)(2,1)} %v_ref.1), custom_call_target="tpu_custom_call" | custom-call | tf_op jit(solution)/shard_map/pack/pallas_call | solution.py:337
  1.4 5.1 %collective-permute-start.5 = (bf16[4,5120]{1,0:T(4,128)(2,1)S(1)}, bf16[4,5120]{1,0:T(4,128)(2,1)S(1)}, u32[]{:S(2)}, u32[]{:S(2)}) collective-permute-start(bf16[4,5120]{1,0:T(4,128)(2,1)S(1)} %pack.1.refs_0_), channel_id=1, source_target_pairs={{0,12},{2,14},{4,8},{6,10},{8,4},{10,6},{12,0},{14,2},{1,13},{3,15... | collective-permute-start | bytes 122888 | tf_op jit(solution)/shard_map/ppermute | solution.py:316
  6.5 0.0 collective-permute-start.3
  6.5 0.6 %collective-permute-start.1 = (bf16[4,5120]{1,0:T(4,128)(2,1)S(1)}, bf16[4,5120]{1,0:T(4,128)(2,1)S(1)}, u32[]{:S(2)}, u32[]{:S(2)}) collective-permute-start(bf16[4,5120]{1,0:T(4,128)(2,1)S(1)} %pack.1.refs_0_), channel_id=1, source_target_pairs={{0,4},{2,6},{4,0},{6,2},{8,12},{10,14},{12,8},{14,10},{1,5},{3,7},... | collective-permute-start | bytes 122888 | tf_op jit(solution)/shard_map/ppermute | solution.py:316
  7.1 0.0 collective-permute-start
  7.1 1.4 %collective-permute-done.5.refs_6_ = bf16[4,5120]{1,0:T(4,128)(2,1)S(1)} collective-permute-done((bf16[4,5120]{1,0:T(4,128)(2,1)S(1)}, bf16[4,5120]{1,0:T(4,128)(2,1)S(1)}, u32[]{:S(2)}, u32[]{:S(2)}) %collective-permute-start.5) | collective-permute-done | bytes 40992 | tf_op jit(solution)/shard_map/ppermute | solution.py:316
  8.5 0.0 collective-permute-start.6
  8.5 2.9 %collective-permute-done.3.refs_4_ = bf16[4,5120]{1,0:T(4,128)(2,1)S(1)} collective-permute-done((bf16[4,5120]{1,0:T(4,128)(2,1)S(1)}, bf16[4,5120]{1,0:T(4,128)(2,1)S(1)}, u32[]{:S(2)}, u32[]{:S(2)}) %collective-permute-start.3) | collective-permute-done | bytes 40992 | tf_op jit(solution)/shard_map/ppermute | solution.py:316
  11.4 0.0 collective-permute-start.4
  11.4 0.0 collective-permute-done.1.refs_2_
  11.4 0.5 %collective-permute-start.2 = (bf16[4,5120]{1,0:T(4,128)(2,1)S(1)}, bf16[4,5120]{1,0:T(4,128)(2,1)S(1)}, u32[]{:S(2)}, u32[]{:S(2)}) collective-permute-start(bf16[4,5120]{1,0:T(4,128)(2,1)S(1)} %collective-permute-done.1.refs_2_), channel_id=1, source_target_pairs={{0,2},{2,0},{4,6},{6,4},{8,10},{10,8},{12,14},{14,12},{1,3},{3,1},... | collective-permute-start | bytes 122888 | tf_op jit(solution)/shard_map/ppermute | solution.py:318
  11.9 0.0 slice-start
  11.9 6.1 %early.1 = (bf16[2,448,1024]{2,1,0:T(8,128)(2,1)S(1)}, bf16[2,448,1024]{2,1,0:T(8,128)(2,1)S(1)}, bf16[2,448,128]{2,1,0:T(8,128)(2,1)S(1)}, bf16[2,448,128]{2,1,...) custom-call(s32[1,448]{1,0:T(1,128)} %refs_0_.1, ...), custom_call_target="tpu_custom_call" | custom-call | flops 939524096 | bytes 3670016 | tf_op jit(solution)/shard_map/early/pallas_call | solution.py:263
  18.0 0.0 collective-permute-done.refs_1_
  18.0 0.0 collective-permute-done.6.refs_7_
  18.0 0.0 collective-permute-done.4.refs_5_
  18.0 0.0 collective-permute-done.2.refs_3_
  18.0 0.0 slice-start.1
  18.0 1.9 %decode.1.refs_5_.refs_0_ = bf16[8,4096]{1,0:T(8,128)(2,1)S(1)} custom-call(bf16[4,5120]{1,0:T(4,128)(2,1)S(1)} %pack.1.refs_0_, bf16[4,5120]{1,0:T(4,128)(2,1)S(1)} %collective-permute-done.refs_1_, bf16[4,5120]{1,0:T(4,128)(2,1)S(1)} %collective-permute-done.1.refs_2_, bf16[4,5120]{1,0:T(4,128)(2,1)S(1)} %collective-permute-done.2.refs_3_, ...), custom_call_target="tpu_custom_call" | custom-call | flops 1000000000 | bytes 1048576 | tf_op jit(solution)/shard_map/decode/pallas_call | solution.py:408
  19.9 1.2 %collective-permute-start.12 = (bf16[8,4096]{1,0:T(8,128)(2,1)S(1)}, bf16[8,4096]{1,0:T(8,128)(2,1)S(1)}, u32[]{:S(2)}, u32[]{:S(2)}) collective-permute-start(bf16[8,4096]{1,0:T(8,128)(2,1)S(1)} %decode.1.refs_5_.refs_0_), channel_id=1, source_target_pairs={{0,12},{2,14},{4,8},{6,10},{8,4},{10,6},{12,0},{14,2},{1,13},{3,15... | collective-permute-start | bytes 196616 | tf_op jit(solution)/shard_map/ppermute | solution.py:316
  21.2 0.4 %collective-permute-start.10 = (bf16[8,4096]{1,0:T(8,128)(2,1)S(1)}, bf16[8,4096]{1,0:T(8,128)(2,1)S(1)}, u32[]{:S(2)}, u32[]{:S(2)}) collective-permute-start(bf16[8,4096]{1,0:T(8,128)(2,1)S(1)} %decode.1.refs_5_.refs_0_), channel_id=1, source_target_pairs={{0,8},{2,10},{4,12},{6,14},{8,0},{10,2},{12,4},{14,6},{1,9},{3,11}... | collective-permute-start | bytes 196616 | tf_op jit(solution)/shard_map/ppermute | solution.py:316
  21.6 2.8 %collective-permute-start.8 = (bf16[8,4096]{1,0:T(8,128)(2,1)S(1)}, bf16[8,4096]{1,0:T(8,128)(2,1)S(1)}, u32[]{:S(2)}, u32[]{:S(2)}) collective-permute-start(bf16[8,4096]{1,0:T(8,128)(2,1)S(1)} %decode.1.refs_5_.refs_0_), channel_id=1, source_target_pairs={{0,4},{2,6},{4,0},{6,2},{8,12},{10,14},{12,8},{14,10},{1,5},{3,7},... | collective-permute-start | bytes 196616 | tf_op jit(solution)/shard_map/ppermute | solution.py:316
  24.4 0.0 collective-permute-start.7
  24.4 2.4 %collective-permute-done.12.refs_6_ = bf16[8,4096]{1,0:T(8,128)(2,1)S(1)} collective-permute-done((bf16[8,4096]{1,0:T(8,128)(2,1)S(1)}, bf16[8,4096]{1,0:T(8,128)(2,1)S(1)}, u32[]{:S(2)}, u32[]{:S(2)}) %collective-permute-start.12) | collective-permute-done | bytes 65568 | tf_op jit(solution)/shard_map/ppermute | solution.py:316
  26.8 0.0 collective-permute-start.13
  26.8 1.9 %collective-permute-done.10.refs_4_ = bf16[8,4096]{1,0:T(8,128)(2,1)S(1)} collective-permute-done((bf16[8,4096]{1,0:T(8,128)(2,1)S(1)}, bf16[8,4096]{1,0:T(8,128)(2,1)S(1)}, u32[]{:S(2)}, u32[]{:S(2)}) %collective-permute-start.10) | collective-permute-done | bytes 65568 | tf_op jit(solution)/shard_map/ppermute | solution.py:316
  28.6 0.0 collective-permute-start.11
  28.6 0.0 collective-permute-done.8.refs_2_
  28.6 0.5 %collective-permute-start.9 = (bf16[8,4096]{1,0:T(8,128)(2,1)S(1)}, bf16[8,4096]{1,0:T(8,128)(2,1)S(1)}, u32[]{:S(2)}, u32[]{:S(2)}) collective-permute-start(bf16[8,4096]{1,0:T(8,128)(2,1)S(1)} %collective-permute-done.8.refs_2_), channel_id=1, source_target_pairs={{0,2},{2,0},{4,6},{6,4},{8,10},{10,8},{12,14},{14,12},{1,3},{3,1},... | collective-permute-start | bytes 196616 | tf_op jit(solution)/shard_map/ppermute | solution.py:318
  29.1 3.5 %late.1.refs_10_ = bf16[448,4096]{1,0:T(8,128)(2,1)} custom-call(bf16[2,448,1024]{2,1,0:T(8,128)(2,1)S(1)} %get-tuple-element.14.refs_0_, bf16[2,448,1024]{2,1,0:T(8,128)(2,1)S(1)} %get-tuple-element.15.refs_1_, bf16[2,448,128]{2,1,0:T(8,128)(2,1)S(1)} %get-tuple-element.16.refs_2_, bf16[2,448,128]{2,1,0:T(8,128)(2,1)S(1)} %get-tuple-element.17.refs_3_, ...), custom_call_target="tpu_custom_call" | custom-call | flops 939524096 | bytes 3670016 | tf_op jit(solution)/shard_map/late/pallas_call | solution.py:291
  32.7 0.0 collective-permute-done.7.refs_1_
  32.7 0.0 collective-permute-done.13.refs_7_
  32.7 0.0 collective-permute-done.11.refs_5_
  32.7 0.0 collective-permute-done.9.refs_3_
  32.7 0.0 slice-done
  32.7 0.0 slice-done.1
  32.7 0.0 copy-start
  32.7 2.0 %copy-done = bf16[448,4096]{1,0:T(8,128)(2,1)S(1)} copy-done((bf16[448,4096]{1,0:T(8,128)(2,1)S(1)}, bf16[448,4096]{1,0:T(8,128)(2,1)}, u32[]{:S(2)}) %copy-start) | copy-done | bytes 3670040
  34.8 2.1 %project.1 = (bf16[16,1024]{1,0:T(8,128)(2,1)S(1)}, f32[16,1024]{1,0:T(8,128)S(1)}) custom-call(bf16[8,4096]{1,0:T(8,128)(2,1)S(1)} %decode.1.refs_5_.refs_0_, bf16[8,4096]{1,0:T(8,128)(2,1)S(1)} %collective-permute-done.7.refs_1_, bf16[8,4096]{1,0:T(8,128)(2,1)S(1)} %collective-permute-done.8.refs_2_, bf16[8,4096]{1,0:T(8,128)(2,1)S(1)} %collective-permute-done.9.refs_3_, ...), custom_call_target="tpu_custom_call" | custom-call | flops 1000000000 | bytes 8388608 | tf_op jit(solution)/shard_map/project/pallas_call | solution.py:457
  36.9 1.5 %collective-permute-start.14 = (bf16[16,1024]{1,0:T(8,128)(2,1)S(1)}, bf16[16,1024]{1,0:T(8,128)(2,1)S(1)}, u32[]{:S(2)}, u32[]{:S(2)}) collective-permute-start(bf16[16,1024]{1,0:T(8,128)(2,1)S(1)} %get-tuple-element.25), channel_id=1, source_target_pairs={{0,1},{1,0},{2,3},{3,2},{4,5},{5,4},{6,7},{7,6},{8,9},{9,8},{10,11... | collective-permute-start | bytes 98312 | tf_op jit(solution)/shard_map/ppermute | solution.py:506
  38.4 2.4 %collective-permute-done.14 = bf16[16,1024]{1,0:T(8,128)(2,1)S(1)} collective-permute-done((bf16[16,1024]{1,0:T(8,128)(2,1)S(1)}, bf16[16,1024]{1,0:T(8,128)(2,1)S(1)}, u32[]{:S(2)}, u32[]{:S(2)}) %collective-permute-start.14) | collective-permute-done | bytes 32800 | tf_op jit(solution)/shard_map/ppermute | solution.py:506
  40.8 0.6 %add_convert_fusion = bf16[16,1024]{1,0:T(8,128)(2,1)} fusion(f32[16,1024]{1,0:T(8,128)S(1)} %get-tuple-element.24, bf16[16,1024]{1,0:T(8,128)(2,1)S(1)} %collective-permute-done.14), kind=kLoop, calls=%fused_computation | loop fusion | flops 49152 | bytes 131072 | tf_op jit(solution)/shard_map/convert_element_type | solution.py:507
  (1 shorter events, 0.0 us)
Async XLA Ops:
  1.4 7.1 %collective-permute-start.5 = (bf16[4,5120]{1,0:T(4,128)(2,1)S(1)}, bf16[4,5120]{1,0:T(4,128)(2,1)S(1)}, u32[]{:S(2)}, u32[]{:S(2)}) collective-permute-start(bf16[4,5120]{1,0:T(4,128)(2,1)S(1)} %pack.1.refs_0_), channel_id=1, source_target_pairs={{0,12},{2,14},{4,8},{6,10},{8,4},{10,6},{12,0},{14,2},{1,13},{3,15... | collective-permute-start | bytes 122888 | tf_op jit(solution)/shard_map/ppermute | solution.py:316
  6.5 4.9 %collective-permute-start.3 = (bf16[4,5120]{1,0:T(4,128)(2,1)S(1)}, bf16[4,5120]{1,0:T(4,128)(2,1)S(1)}, u32[]{:S(2)}, u32[]{:S(2)}) collective-permute-start(bf16[4,5120]{1,0:T(4,128)(2,1)S(1)} %pack.1.refs_0_), channel_id=1, source_target_pairs={{0,8},{2,10},{4,12},{6,14},{8,0},{10,2},{12,4},{14,6},{1,9},{3,11}... | collective-permute-start | bytes 122888 | tf_op jit(solution)/shard_map/ppermute | solution.py:316
  6.5 4.9 %collective-permute-start.1 = (bf16[4,5120]{1,0:T(4,128)(2,1)S(1)}, bf16[4,5120]{1,0:T(4,128)(2,1)S(1)}, u32[]{:S(2)}, u32[]{:S(2)}) collective-permute-start(bf16[4,5120]{1,0:T(4,128)(2,1)S(1)} %pack.1.refs_0_), channel_id=1, source_target_pairs={{0,4},{2,6},{4,0},{6,2},{8,12},{10,14},{12,8},{14,10},{1,5},{3,7},... | collective-permute-start | bytes 122888 | tf_op jit(solution)/shard_map/ppermute | solution.py:316
  7.1 10.9 %collective-permute-start = (bf16[4,5120]{1,0:T(4,128)(2,1)S(1)}, bf16[4,5120]{1,0:T(4,128)(2,1)S(1)}, u32[]{:S(2)}, u32[]{:S(2)}) collective-permute-start(bf16[4,5120]{1,0:T(4,128)(2,1)S(1)} %pack.1.refs_0_), channel_id=1, source_target_pairs={{0,2},{2,0},{4,6},{6,4},{8,10},{10,8},{12,14},{14,12},{1,3},{3,1},... | collective-permute-start | bytes 122888 | tf_op jit(solution)/shard_map/ppermute | solution.py:318
  8.5 9.5 %collective-permute-start.6 = (bf16[4,5120]{1,0:T(4,128)(2,1)S(1)}, bf16[4,5120]{1,0:T(4,128)(2,1)S(1)}, u32[]{:S(2)}, u32[]{:S(2)}) collective-permute-start(bf16[4,5120]{1,0:T(4,128)(2,1)S(1)} %collective-permute-done.5.refs_6_), channel_id=1, source_target_pairs={{0,2},{2,0},{4,6},{6,4},{8,10},{10,8},{12,14},{14,12},{1,3},{3,1},... | collective-permute-start | bytes 122888 | tf_op jit(solution)/shard_map/ppermute | solution.py:318
  11.4 6.6 %collective-permute-start.4 = (bf16[4,5120]{1,0:T(4,128)(2,1)S(1)}, bf16[4,5120]{1,0:T(4,128)(2,1)S(1)}, u32[]{:S(2)}, u32[]{:S(2)}) collective-permute-start(bf16[4,5120]{1,0:T(4,128)(2,1)S(1)} %collective-permute-done.3.refs_4_), channel_id=1, source_target_pairs={{0,2},{2,0},{4,6},{6,4},{8,10},{10,8},{12,14},{14,12},{1,3},{3,1},... | collective-permute-start | bytes 122888 | tf_op jit(solution)/shard_map/ppermute | solution.py:318
  11.4 6.6 %collective-permute-start.2 = (bf16[4,5120]{1,0:T(4,128)(2,1)S(1)}, bf16[4,5120]{1,0:T(4,128)(2,1)S(1)}, u32[]{:S(2)}, u32[]{:S(2)}) collective-permute-start(bf16[4,5120]{1,0:T(4,128)(2,1)S(1)} %collective-permute-done.1.refs_2_), channel_id=1, source_target_pairs={{0,2},{2,0},{4,6},{6,4},{8,10},{10,8},{12,14},{14,12},{1,3},{3,1},... | collective-permute-start | bytes 122888 | tf_op jit(solution)/shard_map/ppermute | solution.py:318
  11.9 20.8 %slice-start = ((s8[8388608]{0:T(1024)(128)(4,1)}), s8[4194304]{0:T(1024)(128)(4,1)S(1)}, s32[]{:S(2)}) async-start(s8[8388608]{0:T(1024)(128)(4,1)} %bitcast), calls=%async_computation | async-start | bytes 8388608
  18.0 14.7 %slice-start.1 = ((s8[8388608]{0:T(1024)(128)(4,1)}), s8[4194304]{0:T(1024)(128)(4,1)S(1)}, s32[]{:S(2)}) async-start(s8[8388608]{0:T(1024)(128)(4,1)} %bitcast), calls=%async_computation.1 | async-start | bytes 8388608
  19.9 6.8 %collective-permute-start.12 = (bf16[8,4096]{1,0:T(8,128)(2,1)S(1)}, bf16[8,4096]{1,0:T(8,128)(2,1)S(1)}, u32[]{:S(2)}, u32[]{:S(2)}) collective-permute-start(bf16[8,4096]{1,0:T(8,128)(2,1)S(1)} %decode.1.refs_5_.refs_0_), channel_id=1, source_target_pairs={{0,12},{2,14},{4,8},{6,10},{8,4},{10,6},{12,0},{14,2},{1,13},{3,15... | collective-permute-start | bytes 196616 | tf_op jit(solution)/shard_map/ppermute | solution.py:316
  21.2 7.5 %collective-permute-start.10 = (bf16[8,4096]{1,0:T(8,128)(2,1)S(1)}, bf16[8,4096]{1,0:T(8,128)(2,1)S(1)}, u32[]{:S(2)}, u32[]{:S(2)}) collective-permute-start(bf16[8,4096]{1,0:T(8,128)(2,1)S(1)} %decode.1.refs_5_.refs_0_), channel_id=1, source_target_pairs={{0,8},{2,10},{4,12},{6,14},{8,0},{10,2},{12,4},{14,6},{1,9},{3,11}... | collective-permute-start | bytes 196616 | tf_op jit(solution)/shard_map/ppermute | solution.py:316
  21.6 7.0 %collective-permute-start.8 = (bf16[8,4096]{1,0:T(8,128)(2,1)S(1)}, bf16[8,4096]{1,0:T(8,128)(2,1)S(1)}, u32[]{:S(2)}, u32[]{:S(2)}) collective-permute-start(bf16[8,4096]{1,0:T(8,128)(2,1)S(1)} %decode.1.refs_5_.refs_0_), channel_id=1, source_target_pairs={{0,4},{2,6},{4,0},{6,2},{8,12},{10,14},{12,8},{14,10},{1,5},{3,7},... | collective-permute-start | bytes 196616 | tf_op jit(solution)/shard_map/ppermute | solution.py:316
  24.4 8.3 %collective-permute-start.7 = (bf16[8,4096]{1,0:T(8,128)(2,1)S(1)}, bf16[8,4096]{1,0:T(8,128)(2,1)S(1)}, u32[]{:S(2)}, u32[]{:S(2)}) collective-permute-start(bf16[8,4096]{1,0:T(8,128)(2,1)S(1)} %decode.1.refs_5_.refs_0_), channel_id=1, source_target_pairs={{0,2},{2,0},{4,6},{6,4},{8,10},{10,8},{12,14},{14,12},{1,3},{3,1},... | collective-permute-start | bytes 196616 | tf_op jit(solution)/shard_map/ppermute | solution.py:318
  26.8 5.9 %collective-permute-start.13 = (bf16[8,4096]{1,0:T(8,128)(2,1)S(1)}, bf16[8,4096]{1,0:T(8,128)(2,1)S(1)}, u32[]{:S(2)}, u32[]{:S(2)}) collective-permute-start(bf16[8,4096]{1,0:T(8,128)(2,1)S(1)} %collective-permute-done.12.refs_6_), channel_id=1, source_target_pairs={{0,2},{2,0},{4,6},{6,4},{8,10},{10,8},{12,14},{14,12},{1,3},{3,1},... | collective-permute-start | bytes 196616 | tf_op jit(solution)/shard_map/ppermute | solution.py:318
  28.6 4.1 %collective-permute-start.11 = (bf16[8,4096]{1,0:T(8,128)(2,1)S(1)}, bf16[8,4096]{1,0:T(8,128)(2,1)S(1)}, u32[]{:S(2)}, u32[]{:S(2)}) collective-permute-start(bf16[8,4096]{1,0:T(8,128)(2,1)S(1)} %collective-permute-done.10.refs_4_), channel_id=1, source_target_pairs={{0,2},{2,0},{4,6},{6,4},{8,10},{10,8},{12,14},{14,12},{1,3},{3,1},... | collective-permute-start | bytes 196616 | tf_op jit(solution)/shard_map/ppermute | solution.py:318
  28.6 4.1 %collective-permute-start.9 = (bf16[8,4096]{1,0:T(8,128)(2,1)S(1)}, bf16[8,4096]{1,0:T(8,128)(2,1)S(1)}, u32[]{:S(2)}, u32[]{:S(2)}) collective-permute-start(bf16[8,4096]{1,0:T(8,128)(2,1)S(1)} %collective-permute-done.8.refs_2_), channel_id=1, source_target_pairs={{0,2},{2,0},{4,6},{6,4},{8,10},{10,8},{12,14},{14,12},{1,3},{3,1},... | collective-permute-start | bytes 196616 | tf_op jit(solution)/shard_map/ppermute | solution.py:318
  32.7 2.0 %copy-start = (bf16[448,4096]{1,0:T(8,128)(2,1)S(1)}, bf16[448,4096]{1,0:T(8,128)(2,1)}, u32[]{:S(2)}) copy-start(bf16[448,4096]{1,0:T(8,128)(2,1)} %late.1.refs_10_) | copy-start | bytes 11010052
  36.9 3.9 %collective-permute-start.14 = (bf16[16,1024]{1,0:T(8,128)(2,1)S(1)}, bf16[16,1024]{1,0:T(8,128)(2,1)S(1)}, u32[]{:S(2)}, u32[]{:S(2)}) collective-permute-start(bf16[16,1024]{1,0:T(8,128)(2,1)S(1)} %get-tuple-element.25), channel_id=1, source_target_pairs={{0,1},{1,0},{2,3},{3,2},{4,5},{5,4},{6,7},{7,6},{8,9},{9,8},{10,11... | collective-permute-start | bytes 98312 | tf_op jit(solution)/shard_map/ppermute | solution.py:506

commit v2 on v1

--- a/solution.py
+++ b/solution.py
@@ -194,8 +194,8 @@
 
 
 def late_kernel(early, group, window, *refs):
-    (o1_ref, q_ref, k_ref, v_ref, bias_ref, _, out_hbm) = refs[:7]
-    (o_ref, s_ref, p_ref, sems) = refs[7:]
+    (o1_ref, q_ref, k_ref, v_ref, bias_ref, out_hbm) = refs[:6]
+    (o_ref, s_ref, p_ref, sems) = refs[6:]
     late, rows, width = q_ref.shape
     blocks = rows // ROW_BLOCK
     cut = blocks // 2
@@ -286,11 +286,11 @@
     )(*(pltpu.with_memory_space_constraint(x, pltpu.HBM) for x in operands))
 
 
-def late_part(early, group, window, shape, first, q, k, v, bias, after):
+def late_part(early, group, window, shape, first, q, k, v, bias):
     late, rows, width = q.shape
     return pl.pallas_call(
         functools.partial(late_kernel, early, group, window),
-        in_specs=[VMEM] * 6,
+        in_specs=[VMEM] * 5,
         out_specs=HBM,
         out_shape=jax.ShapeDtypeStruct(shape, jnp.bfloat16),
         scratch_shapes=[
@@ -301,7 +301,7 @@
         cost_estimate=cost(group, rows, window, late),
         compiler_params=pltpu.CompilerParams(vmem_limit_bytes=24 << 20),
         name="late",
-    )(first, q, k, v, bias, after)
+    )(first, q, k, v, bias)
 
 
 def xor_plan(n):
@@ -423,7 +423,7 @@
 
 def project_kernel(count, tp, *refs):
     pieces = refs[:count]
-    gather_ref, w_ref, _, *outs = refs[count:]
+    gather_ref, w_ref, *outs = refs[count:]
     step = min(512, w_ref.shape[0])
     total = None
     for first in range(0, w_ref.shape[0], step):
@@ -445,7 +445,7 @@
         outs[0][...] = total
 
 
-def project(pieces, gather, weight, tp, after):
+def project(pieces, gather, weight, tp):
     requests, cols = gather.shape[0], weight.shape[1]
     if tp == 2:
         out_shape = [
@@ -456,7 +456,7 @@
         out_shape = [jax.ShapeDtypeStruct((requests, cols), jnp.float32)]
     return pl.pallas_call(
         functools.partial(project_kernel, len(pieces), tp),
-        in_specs=[VMEM] * (len(pieces) + 2) + [HBM],
+        in_specs=[VMEM] * (len(pieces) + 2),
         out_specs=[VMEM] * len(out_shape),
         out_shape=out_shape,
         cost_estimate=pl.CostEstimate(
@@ -464,7 +464,7 @@
         ),
         compiler_params=pltpu.CompilerParams(vmem_limit_bytes=40 << 20),
         name="project",
-    )(*pieces, gather, weight, after)
+    )(*pieces, gather, weight)
 
 
 def local(
@@ -498,9 +498,9 @@
     slot_out = decode(homes, pick, seg, ck, cv, group)
     pooled = spread(slot_out, n)
     prompt_out = late_part(
-        early, group, window, prompt_query.shape, first, q2, k2, v2, bias, slot_out
+        early, group, window, prompt_query.shape, first, q2, k2, v2, bias
     )
-    partial = project(pooled, gather, out_weight, tp, prompt_out)
+    partial = project(pooled, gather, out_weight, tp)
     if tp == 2:
         send, keep = partial
         other = lax.ppermute(send, "tp", [(0, 1), (1, 0)])

time: 41.7 us -> 38.4 us (0.921)
  local copies, waits for them, and re-layouts: 2.05 us -> 0.01 us
  starting transfers between devices: 12.6 us -> 11.8 us
    ppermute x1, waiting for transfers between devices: 2.43 us -> 0.01 us  [local(): other = lax.ppermute(send, 'tp', [(0, 1), (1, 0)])]
    unnamed x6 -> x2, local copies, waits for them, and re-layouts: 2.05 us -> 0.01 us
    ppermute x8, waiting for transfers between devices: 0.02 us -> 1.22 us  [spread(): lax.ppermute(pieces[d], 'pool', [(i, i ^ 1) for i in range(n)])]
    ppermute x6, waiting for transfers between devices: 8.56 us -> 9.48 us  [spread(): pieces[d] = lax.ppermute(x, 'pool', [(i, i ^ d) for i in range(n)])]
    ppermute x6, starting transfers between devices: 10.1 us -> 9.19 us  [spread(): pieces[d] = lax.ppermute(x, 'pool', [(i, i ^ d) for i in range(n)])]
  transfers between devices with their start and end apart: 15 -> 15, of which waited for: 5 -> 7; matrix products, arithmetic and copies ran while one was open for 0% -> 0% of each run, Pallas kernels for 23% -> 25%
where the time goes in v2:
time: 38.4 us; the launch traced here: 38.2 us
  Pallas kernels  14.4 us (38%)
  starting transfers between devices  11.8 us (31%)
  waiting for transfers between devices  10.7 us (28%)
  between operations  0.71 us (2%)
  other arithmetic  0.62 us (2%)
    ppermute x6, waiting for transfers between devices, spread(): pieces[d] = lax.ppermute(x, 'pool', [(i, i ^ d) for i in range(n)])  9.48 us
    ppermute x6, starting transfers between devices, spread(): pieces[d] = lax.ppermute(x, 'pool', [(i, i ^ d) for i in range(n)])  9.19 us
    pallas_call x1, Pallas kernels, early_part(): pl.pallas_call(functools.partial(early_kernel, n, tp, early, group, windo...  6.08 us
    pallas_call x1, Pallas kernels, late_part(): pl.pallas_call(functools.partial(late_kernel, early, group, window), in_s...  3.53 us
    pallas_call x1, Pallas kernels, project(): pl.pallas_call(functools.partial(project_kernel, len(pieces), tp), in_spe...  2.13 us
    pallas_call x1, Pallas kernels, decode(): pl.pallas_call(functools.partial(decode_kernel, kv_local, group, len(piec...  1.9 us
    ppermute x1, starting transfers between devices, local(): other = lax.ppermute(send, 'tp', [(0, 1), (1, 0)])  1.51 us
    ppermute x8, waiting for transfers between devices, spread(): lax.ppermute(pieces[d], 'pool', [(i, i ^ 1) for i in range(n)])  1.22 us
  transfers between devices with their start and end apart: 15, of which 7 were waited for; matrix products, arithmetic and copies ran while one was open for 0% of the time, Pallas kernels for 25%

profile of v2, /device:TPU:0, one launch (start us, length us, event | category | flops | bytes accessed | tf_op | source)
XLA Modules:
  0.0 38.2 jit_solution(5390725334954374484)
XLA Ops:
  0.6 0.8 %pack.1.refs_0_ = bf16[4,5120]{1,0:T(4,128)(2,1)S(1)} custom-call(bf16[4,4096]{1,0:T(4,128)(2,1)} %q_ref.1, bf16[4,512]{1,0:T(4,128)(2,1)} %k_ref.1, bf16[4,512]{1,0:T(4,128)(2,1)} %v_ref.1), custom_call_target="tpu_custom_call" | custom-call | tf_op jit(solution)/shard_map/pack/pallas_call | solution.py:337
  1.4 0.0 copy-start
  1.4 3.1 %collective-permute-start.1 = (bf16[4,5120]{1,0:T(4,128)(2,1)S(1)}, bf16[4,5120]{1,0:T(4,128)(2,1)S(1)}, u32[]{:S(2)}, u32[]{:S(2)}) collective-permute-start(bf16[4,5120]{1,0:T(4,128)(2,1)S(1)} %pack.1.refs_0_), channel_id=1, source_target_pairs={{0,4},{2,6},{4,0},{6,2},{8,12},{10,14},{12,8},{14,10},{1,5},{3,7},... | collective-permute-start | bytes 122888 | tf_op jit(solution)/shard_map/ppermute | solution.py:316
  4.5 2.6 %collective-permute-start.3 = (bf16[4,5120]{1,0:T(4,128)(2,1)S(1)}, bf16[4,5120]{1,0:T(4,128)(2,1)S(1)}, u32[]{:S(2)}, u32[]{:S(2)}) collective-permute-start(bf16[4,5120]{1,0:T(4,128)(2,1)S(1)} %pack.1.refs_0_), channel_id=1, source_target_pairs={{0,8},{2,10},{4,12},{6,14},{8,0},{10,2},{12,4},{14,6},{1,9},{3,11}... | collective-permute-start | bytes 122888 | tf_op jit(solution)/shard_map/ppermute | solution.py:316
  7.1 0.0 collective-permute-start.5
  7.1 0.0 collective-permute-start
  7.1 0.0 collective-permute-done.1.refs_2_
  7.1 0.5 %collective-permute-start.2 = (bf16[4,5120]{1,0:T(4,128)(2,1)S(1)}, bf16[4,5120]{1,0:T(4,128)(2,1)S(1)}, u32[]{:S(2)}, u32[]{:S(2)}) collective-permute-start(bf16[4,5120]{1,0:T(4,128)(2,1)S(1)} %collective-permute-done.1.refs_2_), channel_id=1, source_target_pairs={{0,2},{2,0},{4,6},{6,4},{8,10},{10,8},{12,14},{14,12},{1,3},{3,1},... | collective-permute-start | bytes 122888 | tf_op jit(solution)/shard_map/ppermute | solution.py:318
  7.6 2.6 %collective-permute-done.3.refs_4_ = bf16[4,5120]{1,0:T(4,128)(2,1)S(1)} collective-permute-done((bf16[4,5120]{1,0:T(4,128)(2,1)S(1)}, bf16[4,5120]{1,0:T(4,128)(2,1)S(1)}, u32[]{:S(2)}, u32[]{:S(2)}) %collective-permute-start.3) | collective-permute-done | bytes 40992 | tf_op jit(solution)/shard_map/ppermute | solution.py:316
  10.1 0.0 collective-permute-start.4
  10.1 2.7 %collective-permute-done.5.refs_6_ = bf16[4,5120]{1,0:T(4,128)(2,1)S(1)} collective-permute-done((bf16[4,5120]{1,0:T(4,128)(2,1)S(1)}, bf16[4,5120]{1,0:T(4,128)(2,1)S(1)}, u32[]{:S(2)}, u32[]{:S(2)}) %collective-permute-start.5) | collective-permute-done | bytes 40992 | tf_op jit(solution)/shard_map/ppermute | solution.py:316
  12.9 0.0 collective-permute-start.6
  12.9 6.1 %early.1 = (bf16[2,448,1024]{2,1,0:T(8,128)(2,1)S(1)}, bf16[2,448,1024]{2,1,0:T(8,128)(2,1)S(1)}, bf16[2,448,128]{2,1,0:T(8,128)(2,1)S(1)}, bf16[2,448,128]{2,1,...) custom-call(s32[1,448]{1,0:T(1,128)} %refs_0_.1, ...), custom_call_target="tpu_custom_call" | custom-call | flops 939524096 | bytes 3670016 | tf_op jit(solution)/shard_map/early/pallas_call | solution.py:263
  18.9 0.0 collective-permute-done.refs_1_
  19.0 0.0 collective-permute-done.2.refs_3_
  19.0 0.0 collective-permute-done.4.refs_5_
  19.0 0.0 collective-permute-done.6.refs_7_
  19.0 1.9 %decode.1.refs_0_ = bf16[8,4096]{1,0:T(8,128)(2,1)S(1)} custom-call(bf16[4,5120]{1,0:T(4,128)(2,1)S(1)} %pack.1.refs_0_, bf16[4,5120]{1,0:T(4,128)(2,1)S(1)} %collective-permute-done.refs_1_, bf16[4,5120]{1,0:T(4,128)(2,1)S(1)} %collective-permute-done.1.refs_2_, bf16[4,5120]{1,0:T(4,128)(2,1)S(1)} %collective-permute-done.2.refs_3_, ...), custom_call_target="tpu_custom_call" | custom-call | flops 1000000000 | bytes 1048576 | tf_op jit(solution)/shard_map/decode/pallas_call | solution.py:408
  20.9 0.1 collective-permute-start.10
  21.0 1.4 %collective-permute-start.12 = (bf16[8,4096]{1,0:T(8,128)(2,1)S(1)}, bf16[8,4096]{1,0:T(8,128)(2,1)S(1)}, u32[]{:S(2)}, u32[]{:S(2)}) collective-permute-start(bf16[8,4096]{1,0:T(8,128)(2,1)S(1)} %decode.1.refs_0_), channel_id=1, source_target_pairs={{0,12},{2,14},{4,8},{6,10},{8,4},{10,6},{12,0},{14,2},{1,13},{3,15... | collective-permute-start | bytes 196616 | tf_op jit(solution)/shard_map/ppermute | solution.py:316
  22.4 2.0 %collective-permute-start.8 = (bf16[8,4096]{1,0:T(8,128)(2,1)S(1)}, bf16[8,4096]{1,0:T(8,128)(2,1)S(1)}, u32[]{:S(2)}, u32[]{:S(2)}) collective-permute-start(bf16[8,4096]{1,0:T(8,128)(2,1)S(1)} %decode.1.refs_0_), channel_id=1, source_target_pairs={{0,4},{2,6},{4,0},{6,2},{8,12},{10,14},{12,8},{14,10},{1,5},{3,7},... | collective-permute-start | bytes 196616 | tf_op jit(solution)/shard_map/ppermute | solution.py:316
  24.4 0.0 collective-permute-start.7
  24.5 3.8 %collective-permute-done.10.refs_4_ = bf16[8,4096]{1,0:T(8,128)(2,1)S(1)} collective-permute-done((bf16[8,4096]{1,0:T(8,128)(2,1)S(1)}, bf16[8,4096]{1,0:T(8,128)(2,1)S(1)}, u32[]{:S(2)}, u32[]{:S(2)}) %collective-permute-start.10) | collective-permute-done | bytes 65568 | tf_op jit(solution)/shard_map/ppermute | solution.py:316
  28.2 0.0 collective-permute-start.11
  28.2 0.0 collective-permute-done.12.refs_6_
  28.2 0.5 %collective-permute-start.13 = (bf16[8,4096]{1,0:T(8,128)(2,1)S(1)}, bf16[8,4096]{1,0:T(8,128)(2,1)S(1)}, u32[]{:S(2)}, u32[]{:S(2)}) collective-permute-start(bf16[8,4096]{1,0:T(8,128)(2,1)S(1)} %collective-permute-done.12.refs_6_), channel_id=1, source_target_pairs={{0,2},{2,0},{4,6},{6,4},{8,10},{10,8},{12,14},{14,12},{1,3},{3,1},... | collective-permute-start | bytes 196616 | tf_op jit(solution)/shard_map/ppermute | solution.py:318
  28.7 0.4 %collective-permute-done.8.refs_2_ = bf16[8,4096]{1,0:T(8,128)(2,1)S(1)} collective-permute-done((bf16[8,4096]{1,0:T(8,128)(2,1)S(1)}, bf16[8,4096]{1,0:T(8,128)(2,1)S(1)}, u32[]{:S(2)}, u32[]{:S(2)}) %collective-permute-start.8) | collective-permute-done | bytes 65568 | tf_op jit(solution)/shard_map/ppermute | solution.py:316
  29.2 0.0 collective-permute-start.9
  29.2 0.0 collective-permute-done.7.refs_1_
  29.2 0.3 collective-permute-done.11.refs_5_
  29.5 0.2 collective-permute-done.13.refs_7_
  29.6 0.8 %collective-permute-done.9.refs_3_ = bf16[8,4096]{1,0:T(8,128)(2,1)S(1)} collective-permute-done((bf16[8,4096]{1,0:T(8,128)(2,1)S(1)}, bf16[8,4096]{1,0:T(8,128)(2,1)S(1)}, u32[]{:S(2)}, u32[]{:S(2)}) %collective-permute-start.9) | collective-permute-done | bytes 65568 | tf_op jit(solution)/shard_map/ppermute | solution.py:318
  30.4 0.0 copy-done
  30.4 2.1 %project.1 = (bf16[16,1024]{1,0:T(8,128)(2,1)S(1)}, f32[16,1024]{1,0:T(8,128)S(1)}) custom-call(bf16[8,4096]{1,0:T(8,128)(2,1)S(1)} %decode.1.refs_0_, bf16[8,4096]{1,0:T(8,128)(2,1)S(1)} %collective-permute-done.7.refs_1_, bf16[8,4096]{1,0:T(8,128)(2,1)S(1)} %collective-permute-done.8.refs_2_, bf16[8,4096]{1,0:T(8,128)(2,1)S(1)} %collective-permute-done.9.refs_3_, ...), custom_call_target="tpu_custom_call" | custom-call | flops 1000000000 | bytes 8388608 | tf_op jit(solution)/shard_map/project/pallas_call | solution.py:457
  32.6 1.5 %collective-permute-start.14 = (bf16[16,1024]{1,0:T(8,128)(2,1)S(1)}, bf16[16,1024]{1,0:T(8,128)(2,1)S(1)}, u32[]{:S(2)}, u32[]{:S(2)}) collective-permute-start(bf16[16,1024]{1,0:T(8,128)(2,1)S(1)} %get-tuple-element.25), channel_id=1, source_target_pairs={{0,1},{1,0},{2,3},{3,2},{4,5},{5,4},{6,7},{7,6},{8,9},{9,8},{10,11... | collective-permute-start | bytes 98312 | tf_op jit(solution)/shard_map/ppermute | solution.py:506
  34.1 3.5 %late.1 = bf16[448,4096]{1,0:T(8,128)(2,1)} custom-call(bf16[2,448,1024]{2,1,0:T(8,128)(2,1)S(1)} %get-tuple-element.14.refs_0_, bf16[2,448,1024]{2,1,0:T(8,128)(2,1)S(1)} %get-tuple-element.15.refs_1_, bf16[2,448,128]{2,1,0:T(8,128)(2,1)S(1)} %get-tuple-element.16.refs_2_, bf16[2,448,128]{2,1,0:T(8,128)(2,1)S(1)} %get-tuple-element.17.refs_3_, ...), custom_call_target="tpu_custom_call" | custom-call | flops 939524096 | bytes 3670016 | tf_op jit(solution)/shard_map/late/pallas_call | solution.py:291
  37.6 0.0 collective-permute-done.14
  37.6 0.6 %add_convert_fusion = bf16[16,1024]{1,0:T(8,128)(2,1)} fusion(f32[16,1024]{1,0:T(8,128)S(1)} %get-tuple-element.24, bf16[16,1024]{1,0:T(8,128)(2,1)S(1)} %collective-permute-done.14), kind=kLoop, calls=%fused_computation | loop fusion | flops 49152 | bytes 131072 | tf_op jit(solution)/shard_map/convert_element_type | solution.py:507
Async XLA Ops:
  1.4 29.0 %copy-start = (bf16[4096,1024]{1,0:T(8,128)(2,1)S(1)}, bf16[4096,1024]{1,0:T(8,128)(2,1)}, u32[]{:S(2)}) copy-start(bf16[4096,1024]{1,0:T(8,128)(2,1)} %refs_9_.1) | copy-start | bytes 25165828
  1.4 5.7 %collective-permute-start.1 = (bf16[4,5120]{1,0:T(4,128)(2,1)S(1)}, bf16[4,5120]{1,0:T(4,128)(2,1)S(1)}, u32[]{:S(2)}, u32[]{:S(2)}) collective-permute-start(bf16[4,5120]{1,0:T(4,128)(2,1)S(1)} %pack.1.refs_0_), channel_id=1, source_target_pairs={{0,4},{2,6},{4,0},{6,2},{8,12},{10,14},{12,8},{14,10},{1,5},{3,7},... | collective-permute-start | bytes 122888 | tf_op jit(solution)/shard_map/ppermute | solution.py:316
  4.5 5.7 %collective-permute-start.3 = (bf16[4,5120]{1,0:T(4,128)(2,1)S(1)}, bf16[4,5120]{1,0:T(4,128)(2,1)S(1)}, u32[]{:S(2)}, u32[]{:S(2)}) collective-permute-start(bf16[4,5120]{1,0:T(4,128)(2,1)S(1)} %pack.1.refs_0_), channel_id=1, source_target_pairs={{0,8},{2,10},{4,12},{6,14},{8,0},{10,2},{12,4},{14,6},{1,9},{3,11}... | collective-permute-start | bytes 122888 | tf_op jit(solution)/shard_map/ppermute | solution.py:316
  7.1 5.8 %collective-permute-start.5 = (bf16[4,5120]{1,0:T(4,128)(2,1)S(1)}, bf16[4,5120]{1,0:T(4,128)(2,1)S(1)}, u32[]{:S(2)}, u32[]{:S(2)}) collective-permute-start(bf16[4,5120]{1,0:T(4,128)(2,1)S(1)} %pack.1.refs_0_), channel_id=1, source_target_pairs={{0,12},{2,14},{4,8},{6,10},{8,4},{10,6},{12,0},{14,2},{1,13},{3,15... | collective-permute-start | bytes 122888 | tf_op jit(solution)/shard_map/ppermute | solution.py:316
  7.1 11.9 %collective-permute-start = (bf16[4,5120]{1,0:T(4,128)(2,1)S(1)}, bf16[4,5120]{1,0:T(4,128)(2,1)S(1)}, u32[]{:S(2)}, u32[]{:S(2)}) collective-permute-start(bf16[4,5120]{1,0:T(4,128)(2,1)S(1)} %pack.1.refs_0_), channel_id=1, source_target_pairs={{0,2},{2,0},{4,6},{6,4},{8,10},{10,8},{12,14},{14,12},{1,3},{3,1},... | collective-permute-start | bytes 122888 | tf_op jit(solution)/shard_map/ppermute | solution.py:318
  7.1 11.9 %collective-permute-start.2 = (bf16[4,5120]{1,0:T(4,128)(2,1)S(1)}, bf16[4,5120]{1,0:T(4,128)(2,1)S(1)}, u32[]{:S(2)}, u32[]{:S(2)}) collective-permute-start(bf16[4,5120]{1,0:T(4,128)(2,1)S(1)} %collective-permute-done.1.refs_2_), channel_id=1, source_target_pairs={{0,2},{2,0},{4,6},{6,4},{8,10},{10,8},{12,14},{14,12},{1,3},{3,1},... | collective-permute-start | bytes 122888 | tf_op jit(solution)/shard_map/ppermute | solution.py:318
  10.1 8.8 %collective-permute-start.4 = (bf16[4,5120]{1,0:T(4,128)(2,1)S(1)}, bf16[4,5120]{1,0:T(4,128)(2,1)S(1)}, u32[]{:S(2)}, u32[]{:S(2)}) collective-permute-start(bf16[4,5120]{1,0:T(4,128)(2,1)S(1)} %collective-permute-done.3.refs_4_), channel_id=1, source_target_pairs={{0,2},{2,0},{4,6},{6,4},{8,10},{10,8},{12,14},{14,12},{1,3},{3,1},... | collective-permute-start | bytes 122888 | tf_op jit(solution)/shard_map/ppermute | solution.py:318
  12.9 6.1 %collective-permute-start.6 = (bf16[4,5120]{1,0:T(4,128)(2,1)S(1)}, bf16[4,5120]{1,0:T(4,128)(2,1)S(1)}, u32[]{:S(2)}, u32[]{:S(2)}) collective-permute-start(bf16[4,5120]{1,0:T(4,128)(2,1)S(1)} %collective-permute-done.5.refs_6_), channel_id=1, source_target_pairs={{0,2},{2,0},{4,6},{6,4},{8,10},{10,8},{12,14},{14,12},{1,3},{3,1},... | collective-permute-start | bytes 122888 | tf_op jit(solution)/shard_map/ppermute | solution.py:318
  20.9 7.3 %collective-permute-start.10 = (bf16[8,4096]{1,0:T(8,128)(2,1)S(1)}, bf16[8,4096]{1,0:T(8,128)(2,1)S(1)}, u32[]{:S(2)}, u32[]{:S(2)}) collective-permute-start(bf16[8,4096]{1,0:T(8,128)(2,1)S(1)} %decode.1.refs_0_), channel_id=1, source_target_pairs={{0,8},{2,10},{4,12},{6,14},{8,0},{10,2},{12,4},{14,6},{1,9},{3,11}... | collective-permute-start | bytes 196616 | tf_op jit(solution)/shard_map/ppermute | solution.py:316
  21.0 7.3 %collective-permute-start.12 = (bf16[8,4096]{1,0:T(8,128)(2,1)S(1)}, bf16[8,4096]{1,0:T(8,128)(2,1)S(1)}, u32[]{:S(2)}, u32[]{:S(2)}) collective-permute-start(bf16[8,4096]{1,0:T(8,128)(2,1)S(1)} %decode.1.refs_0_), channel_id=1, source_target_pairs={{0,12},{2,14},{4,8},{6,10},{8,4},{10,6},{12,0},{14,2},{1,13},{3,15... | collective-permute-start | bytes 196616 | tf_op jit(solution)/shard_map/ppermute | solution.py:316
  22.4 6.8 %collective-permute-start.8 = (bf16[8,4096]{1,0:T(8,128)(2,1)S(1)}, bf16[8,4096]{1,0:T(8,128)(2,1)S(1)}, u32[]{:S(2)}, u32[]{:S(2)}) collective-permute-start(bf16[8,4096]{1,0:T(8,128)(2,1)S(1)} %decode.1.refs_0_), channel_id=1, source_target_pairs={{0,4},{2,6},{4,0},{6,2},{8,12},{10,14},{12,8},{14,10},{1,5},{3,7},... | collective-permute-start | bytes 196616 | tf_op jit(solution)/shard_map/ppermute | solution.py:316
  24.4 4.8 %collective-permute-start.7 = (bf16[8,4096]{1,0:T(8,128)(2,1)S(1)}, bf16[8,4096]{1,0:T(8,128)(2,1)S(1)}, u32[]{:S(2)}, u32[]{:S(2)}) collective-permute-start(bf16[8,4096]{1,0:T(8,128)(2,1)S(1)} %decode.1.refs_0_), channel_id=1, source_target_pairs={{0,2},{2,0},{4,6},{6,4},{8,10},{10,8},{12,14},{14,12},{1,3},{3,1},... | collective-permute-start | bytes 196616 | tf_op jit(solution)/shard_map/ppermute | solution.py:318
  28.2 1.3 %collective-permute-start.11 = (bf16[8,4096]{1,0:T(8,128)(2,1)S(1)}, bf16[8,4096]{1,0:T(8,128)(2,1)S(1)}, u32[]{:S(2)}, u32[]{:S(2)}) collective-permute-start(bf16[8,4096]{1,0:T(8,128)(2,1)S(1)} %collective-permute-done.10.refs_4_), channel_id=1, source_target_pairs={{0,2},{2,0},{4,6},{6,4},{8,10},{10,8},{12,14},{14,12},{1,3},{3,1},... | collective-permute-start | bytes 196616 | tf_op jit(solution)/shard_map/ppermute | solution.py:318
  28.2 1.4 %collective-permute-start.13 = (bf16[8,4096]{1,0:T(8,128)(2,1)S(1)}, bf16[8,4096]{1,0:T(8,128)(2,1)S(1)}, u32[]{:S(2)}, u32[]{:S(2)}) collective-permute-start(bf16[8,4096]{1,0:T(8,128)(2,1)S(1)} %collective-permute-done.12.refs_6_), channel_id=1, source_target_pairs={{0,2},{2,0},{4,6},{6,4},{8,10},{10,8},{12,14},{14,12},{1,3},{3,1},... | collective-permute-start | bytes 196616 | tf_op jit(solution)/shard_map/ppermute | solution.py:318
  29.2 1.3 %collective-permute-start.9 = (bf16[8,4096]{1,0:T(8,128)(2,1)S(1)}, bf16[8,4096]{1,0:T(8,128)(2,1)S(1)}, u32[]{:S(2)}, u32[]{:S(2)}) collective-permute-start(bf16[8,4096]{1,0:T(8,128)(2,1)S(1)} %collective-permute-done.8.refs_2_), channel_id=1, source_target_pairs={{0,2},{2,0},{4,6},{6,4},{8,10},{10,8},{12,14},{14,12},{1,3},{3,1},... | collective-permute-start | bytes 196616 | tf_op jit(solution)/shard_map/ppermute | solution.py:318
  32.6 5.1 %collective-permute-start.14 = (bf16[16,1024]{1,0:T(8,128)(2,1)S(1)}, bf16[16,1024]{1,0:T(8,128)(2,1)S(1)}, u32[]{:S(2)}, u32[]{:S(2)}) collective-permute-start(bf16[16,1024]{1,0:T(8,128)(2,1)S(1)} %get-tuple-element.25), channel_id=1, source_target_pairs={{0,1},{1,0},{2,3},{3,2},{4,5},{5,4},{6,7},{7,6},{8,9},{9,8},{10,11... | collective-permute-start | bytes 98312 | tf_op jit(solution)/shard_map/ppermute | solution.py:506

commit v3 on v2

v3 whole, which is shorter than its diff:
```python
import functools

import jax
import jax.numpy as jnp
from jax import lax
from jax.experimental import pallas as pl
from jax.experimental.pallas import tpu as pltpu
from jax.sharding import PartitionSpec as P


HEAD_DIM = 128
LOG2E = 1.4426950408889634
ROW_BLOCK = 32
VMEM = pl.BlockSpec(memory_space=pltpu.VMEM)
HBM = pl.BlockSpec(memory_space=pltpu.HBM)


def attend(items, group, window, q_ref, k_ref, v_ref, bias_ref, s_ref, p_ref, o_ref,
           finished=lambda head, b: None):
    block = ROW_BLOCK
    stacked = group * block
    scale = HEAD_DIM ** (-0.5) * LOG2E

    def place_of(t):
        head, b = items[t]
        start = max(0, (b + 1) * block - window)
        span = min(window, -(-(b + 1) * block // HEAD_DIM) * HEAD_DIM)
        return head, b, slice(b * block, (b + 1) * block), start, span

    def score(t):
        head, _, at, start, span = place_of(t)
        query = jnp.concatenate(
            [q_ref[head, at, h * HEAD_DIM : (h + 1) * HEAD_DIM] for h in range(group)], axis=0
        )
        s_ref[t % 2, :, :span] = lax.dot_general(
            query,
            k_ref[head, start : start + span, :],
            (((1,), (1,)), ((), ())),
            preferred_element_type=jnp.float32,
        )

    def weigh(t):
        _, b, _, _, span = place_of(t)
        scores = s_ref[t % 2, :, :span].reshape(group, block, span) * scale
        scores = scores + bias_ref[b, :, :span][None]
        highest = jnp.max(scores, axis=-1, keepdims=True)
        weights = jnp.exp2(scores - highest).astype(jnp.bfloat16).reshape(stacked, span)
        for c in range(span // HEAD_DIM):
            p_ref[t % 2, c] = weights[:, c * HEAD_DIM : (c + 1) * HEAD_DIM]

    def combine(t):
        head, _, at, start, span = place_of(t)
        values = v_ref[head, start : start + span, :]
        values = jnp.concatenate([values, jnp.ones_like(values)], axis=1)
        weights = jnp.concatenate([p_ref[t % 2, c] for c in range(span // HEAD_DIM)], axis=1)
        both = jnp.dot(weights, values, preferred_element_type=jnp.float32)
        result = (both[:, :HEAD_DIM] / both[:, HEAD_DIM:]).astype(jnp.bfloat16)
        for h in range(group):
            o_ref[head, at, h * HEAD_DIM : (h + 1) * HEAD_DIM] = result[
                h * block : (h + 1) * block
            ]

    total = len(items)
    for t in range(total + 2):
        if t >= 2:
            combine(t - 2)
        if t < total:
            score(t)
        if 1 <= t <= total:
            weigh(t - 1)
        if t >= 2:
            finished(*items[t - 2])


def early_kernel(n, tp, group, window, home_rows, slots, head_items, *refs):
    (doc_hbm, q_hbm, k_hbm, v_hbm, start_hbm, len_hbm, ck_hbm, cv_hbm) = refs[:8]
    (o_ref, q_ref, k_ref, v_ref, bias_ref, ck_ref, cv_ref, pick_ref, seg_ref, gather_ref) = (
        refs[8:18]
    )
    doc_ref, start_ref, len_ref, s_ref, p_ref, sems = refs[18:]
    near, rows, width = q_ref.shape
    block = ROW_BLOCK
    blocks = rows // block
    cap = ck_hbm.shape[0]
    requests = start_hbm.shape[1]
    cut = head_items * block
    copies = {}

    def begin(name, src, dst):
        copy = pltpu.make_async_copy(src, dst, sems.at[len(copies)])
        copies[name] = copy
        copy.start()

    begin("doc", doc_hbm, doc_ref)
    begin("start", start_hbm, start_ref)
    begin("len", len_hbm, len_ref)
    for i in range(near):
        lanes = slice(i * HEAD_DIM, (i + 1) * HEAD_DIM)
        cols = slice(i * width, (i + 1) * width)
        begin(("k", i), k_hbm.at[:, lanes], k_ref.at[i])
        if i == 0:
            begin("q", q_hbm.at[:cut, cols], q_ref.at[i, :cut])
        begin(("v", i), v_hbm.at[:, lanes], v_ref.at[i])
        if i == 0:
            begin("ck", ck_hbm, ck_ref)
            begin("cv", cv_hbm, cv_ref)
            begin(("q", i), q_hbm.at[cut:, cols], q_ref.at[i, cut:])
        else:
            begin(("q", i), q_hbm.at[:, cols], q_ref.at[i])

    def grid(shape):
        return lax.broadcasted_iota(jnp.int32, shape, 0), lax.broadcasted_iota(jnp.int32, shape, 1)

    for name in ("doc", "start", "len"):
        copies[name].wait()
    for b in range(blocks):
        start = max(0, (b + 1) * block - window)
        key_doc = jnp.broadcast_to(
            doc_ref[:, start : start + window].astype(jnp.float32), (block, window)
        )
        row, col = grid((block, window))
        row, col = row + b * block, col + start
        row_doc = jnp.sum(jnp.where(row == col, key_doc, 0.0), axis=1, keepdims=True)
        allowed = (col <= row) & (key_doc == row_doc)
        bias_ref[b] = jnp.where(allowed, 0.0, -jnp.inf)

    me = lax.axis_index("pool")
    first = start_ref[...].astype(jnp.float32)
    owner = jnp.floor((first + 0.5) / cap)
    sub, lane = grid((requests, requests))
    owner_col = jnp.sum(jnp.where(sub == lane, owner, 0.0), axis=1, keepdims=True)
    same = owner_col == owner
    rank_col = jnp.sum(jnp.where(same & (lane < sub), 1.0, 0.0), axis=1, keepdims=True)
    rank = jnp.sum(jnp.where(same & (sub < lane), 1.0, 0.0), axis=0, keepdims=True)
    source = place(owner_col.astype(jnp.int32), me, n) * slots + rank_col.astype(jnp.int32)
    gather = jnp.where(grid((requests, n * slots))[1] == source, 1.0, 0.0)
    if tp == 2:
        half = requests // 2
        turned = jnp.concatenate([gather[half:], gather[:half]], axis=0)
        gather = jnp.where(lax.axis_index("tp") == 0, turned, gather)
    gather_ref[...] = gather.astype(jnp.bfloat16)
    slot = grid((slots, requests))[0].astype(jnp.float32)
    select = jnp.where((owner == me.astype(jnp.float32)) & (rank == slot), 1.0, 0.0)
    home = jnp.floor((lane.astype(jnp.float32) + 0.5) / home_rows).astype(jnp.int32)
    turn = jnp.where(
        place(home, me, n) * home_rows + lane - home * home_rows == sub, 1.0, 0.0
    )
    pick = jnp.dot(
        select.astype(jnp.bfloat16),
        turn.astype(jnp.bfloat16),
        preferred_element_type=jnp.float32,
    )
    pick_ref[...] = pick.astype(jnp.bfloat16)
    low = jnp.sum(select * first, axis=1, keepdims=True) - (me * cap).astype(jnp.float32)
    high = low + jnp.sum(select * len_ref[...].astype(jnp.float32), axis=1, keepdims=True)
    cell = grid((slots, cap))[1].astype(jnp.float32)
    seg_ref[...] = jnp.where((cell >= low) & (cell < high), 0.0, -jnp.inf)

    copies["k", 0].wait()
    copies["q"].wait()
    copies["v", 0].wait()
    items = [(0, b) for b in range(head_items)]
    attend(items, group, window, q_ref, k_ref, v_ref, bias_ref, s_ref, p_ref, o_ref)
    for name, copy in copies.items():
        if name not in ("doc", "start", "len", "q", ("k", 0), ("v", 0)):
            copy.wait()


def late_kernel(group, window, head_items, *refs):
    (q_ref, k_ref, v_ref, bias_ref, _, q_hbm, k_hbm, v_hbm) = refs[:8]
    (o_ref, q2_ref, k2_ref, v2_ref, s_ref, p_ref, sems) = refs[8:]
    near, rows, width = q_ref.shape
    blocks = rows // ROW_BLOCK
    copies = []
    for i in range(q2_ref.shape[0]):
        lanes = slice((near + i) * HEAD_DIM, (near + i + 1) * HEAD_DIM)
        cols = slice((near + i) * width, (near + i + 1) * width)
        for src, dst in (
            (q_hbm.at[:, cols], q2_ref.at[i]),
            (k_hbm.at[:, lanes], k2_ref.at[i]),
            (v_hbm.at[:, lanes], v2_ref.at[i]),
        ):
            copies.append(pltpu.make_async_copy(src, dst, sems.at[len(copies)]))
            copies[-1].start()
    items = [(head, b) for head in range(near) for b in range(blocks)][head_items:]
    attend(items, group, window, q_ref, k_ref, v_ref, bias_ref, s_ref, p_ref, o_ref)
    for copy in copies:
        copy.wait()


def last_kernel(group, window, *refs):
    (done_ref, q_ref, k_ref, v_ref, bias_ref, out_hbm) = refs[:6]
    (o_ref, s_ref, p_ref, sems) = refs[6:]
    near = done_ref.shape[0]
    far, rows, width = q_ref.shape
    blocks = rows // ROW_BLOCK
    cut = blocks // 2
    copies = []

    def store(src, dst):
        copies.append(pltpu.make_async_copy(src, dst, sems.at[len(copies)]))
        copies[-1].start()

    for i in range(near):
        store(done_ref.at[i], out_hbm.at[:, i * width : (i + 1) * width])

    def finished(head, b):
        if b + 1 in (cut, blocks):
            span = slice(0, cut * ROW_BLOCK) if b + 1 == cut else slice(cut * ROW_BLOCK, rows)
            cols = slice((near + head) * width, (near + head + 1) * width)
            store(o_ref.at[head, span], out_hbm.at[span, cols])

    items = [(head, b) for head in range(far) for b in range(blocks)]
    attend(items, group, window, q_ref, k_ref, v_ref, bias_ref, s_ref, p_ref, o_ref,
           finished)
    for copy in copies:
        copy.wait()


def pipeline_scratch(group, window):
    stacked = group * ROW_BLOCK
    return [
        pltpu.VMEM((2, stacked, window), jnp.float32),
        pltpu.VMEM((2, window // HEAD_DIM, stacked, HEAD_DIM), jnp.bfloat16),
    ]


def cost(group, rows, window, heads):
    return pl.CostEstimate(
        flops=4 * heads * group * rows * window * HEAD_DIM,
        bytes_accessed=4 * rows * group * HEAD_DIM * heads,
        transcendentals=0,
    )


def in_hbm(*arrays):
    return tuple(pltpu.with_memory_space_constraint(x, pltpu.HBM) for x in arrays)


def early_part(n, tp, near, group, window, home_rows, head_items, doc_ids, query, key, value,
               start, length, cache_keys, cache_values):
    rows, width = query.shape[0], group * HEAD_DIM
    slots = 2 * home_rows
    requests = start.shape[0]
    bf16, f32 = jnp.bfloat16, jnp.float32
    out_shape = [
        jax.ShapeDtypeStruct((near, rows, width), bf16),
        jax.ShapeDtypeStruct((near, rows, width), bf16),
        jax.ShapeDtypeStruct((near, rows, HEAD_DIM), bf16),
        jax.ShapeDtypeStruct((near, rows, HEAD_DIM), bf16),
        jax.ShapeDtypeStruct((rows // ROW_BLOCK, ROW_BLOCK, window), f32),
        jax.ShapeDtypeStruct(cache_keys.shape, bf16),
        jax.ShapeDtypeStruct(cache_values.shape, bf16),
        jax.ShapeDtypeStruct((slots, n * home_rows), bf16),
        jax.ShapeDtypeStruct((slots, cache_keys.shape[0]), f32),
        jax.ShapeDtypeStruct((requests, n * slots), bf16),
    ]
    operands = (doc_ids, query, key, value, start.reshape(1, -1), length.reshape(1, -1),
                cache_keys, cache_values)
    return pl.pallas_call(
        functools.partial(early_kernel, n, tp, group, window, home_rows, slots, head_items),
        in_specs=[HBM] * len(operands),
        out_specs=[VMEM] * len(out_shape),
        out_shape=out_shape,
        scratch_shapes=[
            pltpu.VMEM(doc_ids.shape, jnp.int32),
            pltpu.VMEM((1, requests), jnp.int32),
            pltpu.VMEM((1, requests), jnp.int32),
            *pipeline_scratch(group, window),
            pltpu.SemaphoreType.DMA((6 + 3 * near,)),
        ],
        cost_estimate=cost(group, rows, window, near),
        compiler_params=pltpu.CompilerParams(vmem_limit_bytes=24 << 20),
        name="early",
    )(*in_hbm(*operands))


def late_part(far, group, window, head_items, done, q, k, v, bias, query, key, value):
    near, rows, width = q.shape
    return pl.pallas_call(
        functools.partial(late_kernel, group, window, head_items),
        in_specs=[VMEM] * 5 + [HBM] * 3,
        out_specs=[VMEM] * 4,
        out_shape=[
            jax.ShapeDtypeStruct(done.shape, done.dtype),
            jax.ShapeDtypeStruct((far, rows, width), jnp.bfloat16),
            jax.ShapeDtypeStruct((far, rows, HEAD_DIM), jnp.bfloat16),
            jax.ShapeDtypeStruct((far, rows, HEAD_DIM), jnp.bfloat16),
        ],
        scratch_shapes=[
            *pipeline_scratch(group, window),
            pltpu.SemaphoreType.DMA((3 * far,)),
        ],
        input_output_aliases={4: 0},
        cost_estimate=cost(group, rows, window, near),
        compiler_params=pltpu.CompilerParams(vmem_limit_bytes=24 << 20),
        name="late",
    )(q, k, v, bias, done, *in_hbm(query, key, value))


def last_part(group, window, shape, done, q, k, v, bias):
    far, rows, width = q.shape
    return pl.pallas_call(
        functools.partial(last_kernel, group, window),
        in_specs=[VMEM] * 5,
        out_specs=HBM,
        out_shape=jax.ShapeDtypeStruct(shape, jnp.bfloat16),
        scratch_shapes=[
            pltpu.VMEM((far, rows, width), jnp.bfloat16),
            *pipeline_scratch(group, window),
            pltpu.SemaphoreType.DMA((done.shape[0] + 2 * far,)),
        ],
        cost_estimate=cost(group, rows, window, far),
        compiler_params=pltpu.CompilerParams(vmem_limit_bytes=24 << 20),
        name="last",
    )(done, q, k, v, bias)


def xor_plan(n):
    return n & (n - 1) == 0 and 2 <= n <= 8


def spread(x, n):
    if not xor_plan(n):
        return [lax.all_gather(x, "pool", axis=0, tiled=True)]
    pieces = {0: x}
    for d in range(n - 2, 0, -2):
        pieces[d] = lax.ppermute(x, "pool", [(i, i ^ d) for i in range(n)])
    for d in range(0, n, 2):
        pieces[d + 1] = lax.ppermute(
            pieces[d], "pool", [(i, i ^ 1) for i in range(n)]
        )
    return [pieces[d] for d in range(n)]


def place(index, me, n):
    return index ^ me if xor_plan(n) else index


def pack_kernel(q_ref, k_ref, v_ref, o_ref):
    dq, dk = q_ref.shape[1], k_ref.shape[1]
    o_ref[:, :dq] = q_ref[...]
    o_ref[:, dq : dq + dk] = k_ref[...]
    o_ref[:, dq + dk :] = v_ref[...]


def pack(q, k, v):
    shape = (q.shape[0], q.shape[1] + k.shape[1] + v.shape[1])
    return pl.pallas_call(
        pack_kernel,
        in_specs=[VMEM] * 3,
        out_specs=VMEM,
        out_shape=pltpu.VMEM(shape, q.dtype),
        name="pack",
    )(q, k, v)


def decode_kernel(kv_local, group, count, *refs):
    pieces = refs[:count]
    pick_ref, seg_ref, k_ref, v_ref, o_ref, all_ref = refs[count:]
    slots, cap = seg_ref.shape
    q_width = kv_local * group * HEAD_DIM
    kv_width = kv_local * HEAD_DIM
    per = all_ref.shape[0] // count
    for i, piece in enumerate(pieces):
        all_ref[i * per : (i + 1) * per, :] = piece[...].astype(jnp.float32)
    bias = seg_ref[...]
    scale = HEAD_DIM ** (-0.5) * LOG2E
    rows = jnp.dot(
        pick_ref[...], all_ref[...].astype(jnp.bfloat16), preferred_element_type=jnp.float32
    )
    heads = range(kv_local)

    def stack(g):
        first = g * group * HEAD_DIM
        return jnp.concatenate(
            [rows[:, first + h * HEAD_DIM : first + (h + 1) * HEAD_DIM] for h in range(group)],
            axis=0,
        )

    def lanes(g, first=0):
        return slice(first + g * HEAD_DIM, first + (g + 1) * HEAD_DIM)

    queries = [stack(g) for g in heads]
    scores = [
        lax.dot_general(
            queries[g].astype(jnp.bfloat16),
            k_ref[:, lanes(g)],
            (((1,), (1,)), ((), ())),
            preferred_element_type=jnp.float32,
        )
        for g in heads
    ]
    weights, own_weights, inverses = [], [], []
    for g in heads:
        new_key = rows[:, lanes(g, q_width)]
        own = jnp.sum(
            queries[g].reshape(group, slots, HEAD_DIM) * new_key[None], axis=-1, keepdims=True
        )
        own = own * scale
        score = scores[g].reshape(group, slots, cap) * scale + bias[None]
        highest = jnp.maximum(jnp.max(score, axis=-1, keepdims=True), own)
        weight = jnp.exp2(score - highest)
        own_weight = jnp.exp2(own - highest)
        inverses.append(1.0 / (jnp.sum(weight, axis=-1, keepdims=True) + own_weight))
        weights.append(weight.astype(jnp.bfloat16).reshape(group * slots, cap))
        own_weights.append(own_weight)
    for g in heads:
        result = jnp.dot(weights[g], v_ref[:, lanes(g)], preferred_element_type=jnp.float32)
        result = result.reshape(group, slots, HEAD_DIM)
        new_value = rows[:, lanes(g, q_width + kv_width)]
        result = (result + own_weights[g] * new_value[None]) * inverses[g]
        for h in range(group):
            o_ref[:, lanes(g * group + h)] = result[h].astype(jnp.bfloat16)


def decode(pieces, pick, seg, cache_keys, cache_values, group):
    kv_local = cache_keys.shape[1] // HEAD_DIM
    total = sum(p.shape[0] for p in pieces)
    width = pieces[0].shape[1]
    operands = (*pieces, pick, seg, cache_keys, cache_values)
    return pl.pallas_call(
        functools.partial(decode_kernel, kv_local, group, len(pieces)),
        in_specs=[VMEM] * len(operands),
        out_specs=VMEM,
        out_shape=jax.ShapeDtypeStruct(
            (pick.shape[0], kv_local * group * HEAD_DIM), jnp.bfloat16
        ),
        scratch_shapes=[pltpu.VMEM((total, width), jnp.float32)],
        cost_estimate=pl.CostEstimate(
            flops=10**9, bytes_accessed=4 * cache_keys.size, transcendentals=0
        ),
        compiler_params=pltpu.CompilerParams(vmem_limit_bytes=24 << 20),
        name="decode",
    )(*operands)


def project_kernel(count, tp, *refs):
    pieces = refs[:count]
    gather_ref, w_ref, *outs = refs[count:]
    step = min(512, w_ref.shape[0])
    total = None
    for first in range(0, w_ref.shape[0], step):
        cols = slice(first, first + step)
        if count == 1:
            rows = pieces[0][:, cols]
        else:
            rows = jnp.concatenate([p[:, cols] for p in pieces], axis=0)
        rows = jnp.dot(gather_ref[...], rows, preferred_element_type=jnp.float32)
        part = jnp.dot(
            rows.astype(jnp.bfloat16), w_ref[cols, :], preferred_element_type=jnp.float32
        )
        total = part if total is None else total + part
    if tp == 2:
        half = total.shape[0] // 2
        outs[0][...] = total[:half].astype(outs[0].dtype)
        outs[1][...] = total[half:]
    else:
        outs[0][...] = total


def project(pieces, gather, weight, tp):
    requests, cols = gather.shape[0], weight.shape[1]
    if tp == 2:
        out_shape = [
            jax.ShapeDtypeStruct((requests // 2, cols), jnp.bfloat16),
            jax.ShapeDtypeStruct((requests // 2, cols), jnp.float32),
        ]
    else:
        out_shape = [jax.ShapeDtypeStruct((requests, cols), jnp.float32)]
    return pl.pallas_call(
        functools.partial(project_kernel, len(pieces), tp),
        in_specs=[VMEM] * (len(pieces) + 2),
        out_specs=[VMEM] * len(out_shape),
        out_shape=out_shape,
        cost_estimate=pl.CostEstimate(
            flops=10**9, bytes_accessed=2 * weight.size, transcendentals=0
        ),
        compiler_params=pltpu.CompilerParams(vmem_limit_bytes=40 << 20),
        name="project",
    )(*pieces, gather, weight)


def local(
    n,
    tp,
    home_query,
    home_key,
    home_value,
    cache_keys,
    cache_values,
    cache_start,
    cache_len,
    prompt_query,
    prompt_key,
    prompt_value,
    doc_ids,
    out_weight,
):
    home_rows = home_query.shape[0]
    rows = prompt_query.shape[0]
    kv_local = home_key.shape[1] // HEAD_DIM
    group = home_query.shape[1] // HEAD_DIM // kv_local
    window = min(rows, rows // 2 + ROW_BLOCK)
    far = max(1, kv_local // 4)
    near = kv_local - far
    head_items = (rows // ROW_BLOCK) * 3 // 7
    prompt = (prompt_query, prompt_key, prompt_value)

    homes = spread(pack(home_query, home_key, home_value), n)
    done, q1, k1, v1, bias, ck, cv, pick, seg, gather = early_part(
        n, tp, near, group, window, home_rows, head_items, doc_ids, *prompt, cache_start,
        cache_len, cache_keys, cache_values,
    )
    slot_out = decode(homes, pick, seg, ck, cv, group)
    pooled = spread(slot_out, n)
    done, q2, k2, v2 = late_part(far, group, window, head_items, done, q1, k1, v1, bias, *prompt)
    partial = project(pooled, gather, out_weight, tp)
    prompt_out = last_part(group, window, prompt_query.shape, done, q2, k2, v2, bias)
    if tp == 2:
        send, keep = partial
        other = lax.ppermute(send, "tp", [(0, 1), (1, 0)])
        decode_out = (keep + other.astype(jnp.float32)).astype(jnp.bfloat16)
    else:
        decode_out = lax.psum_scatter(
            partial[0], "tp", scatter_dimension=0, tiled=True
        ).astype(jnp.bfloat16)
    return (prompt_out, decode_out)


def layer(n, tp, *args):
    return local(n, tp, *args)


def solution(mesh):
    return jax.shard_map(
        functools.partial(layer, mesh.shape["pool"], mesh.shape["tp"]),
        mesh=mesh,
        in_specs=(
            P(("grp", "pool"), "tp"),
            P(("grp", "pool"), "tp"),
            P(("grp", "pool"), "tp"),
            P(("grp", "pool"), "tp"),
            P(("grp", "pool"), "tp"),
            P("grp"),
            P("grp"),
            P(("grp", "pool"), "tp"),
            P(("grp", "pool"), "tp"),
            P(("grp", "pool"), "tp"),
            P(("grp", "pool"), None),
            P("tp", "pool"),
        ),
        out_specs=(P(("grp", "pool"), "tp"), P(("grp", "tp"), "pool")),
        check_vma=False,
    )
```

time: 38.4 us -> 36.2 us (0.943)
  Pallas kernels: 14.4 us -> 13.2 us
  waiting for transfers between devices: 10.7 us -> 9.66 us
    ppermute x8, waiting for transfers between devices: 1.22 us -> 0.02 us  [spread(): lax.ppermute(pieces[d], 'pool', [(i, i ^ 1) for i in range(n)])]
    pallas_call x1, Pallas kernels: 1.9 us -> 0.71 us  [decode(): pl.pallas_call(functools.partial(decode_kernel, kv_local, group, len(piec...]
    pallas_call x2 -> x3, Pallas kernels: 9.62 us -> 9.55 us  [the longest x1 4.63 us: late_part(): pl.pallas_call(functools.partial(late_kernel, group, window, head_items),...]
  transfers between devices with their start and end apart: 15 -> 15, of which waited for: 7 -> 5; matrix products, arithmetic and copies ran while one was open for 0% -> 0% of each run, Pallas kernels for 25% -> 27%
where the time goes in v3:
time: 36.2 us; the launch traced here: 36 us
  Pallas kernels  13.2 us (36%)
  starting transfers between devices  11.8 us (33%)
  waiting for transfers between devices  9.66 us (27%)
  between operations  0.76 us (2%)
  other arithmetic  0.62 us (2%)
    ppermute x6, waiting for transfers between devices, spread(): pieces[d] = lax.ppermute(x, 'pool', [(i, i ^ d) for i in range(n)])  9.49 us
    ppermute x6, starting transfers between devices, spread(): pieces[d] = lax.ppermute(x, 'pool', [(i, i ^ d) for i in range(n)])  9.19 us
    pallas_call x1, Pallas kernels, late_part(): pl.pallas_call(functools.partial(late_kernel, group, window, head_items),...  4.63 us
    pallas_call x1, Pallas kernels, early_part(): pl.pallas_call(functools.partial(early_kernel, n, tp, group, window, home...  2.65 us
    pallas_call x1, Pallas kernels, last_part(): pl.pallas_call(functools.partial(last_kernel, group, window), in_specs=[V...  2.27 us
    pallas_call x1, Pallas kernels, project(): pl.pallas_call(functools.partial(project_kernel, len(pieces), tp), in_spe...  2.13 us
    ppermute x1, starting transfers between devices, local(): other = lax.ppermute(send, 'tp', [(0, 1), (1, 0)])  1.5 us
    ppermute x8, starting transfers between devices, spread(): lax.ppermute(pieces[d], 'pool', [(i, i ^ 1) for i in range(n)])  1.07 us
  transfers between devices with their start and end apart: 15, of which 5 were waited for; matrix products, arithmetic and copies ran while one was open for 0% of the time, Pallas kernels for 27%

profile of v3, /device:TPU:0, one launch (start us, length us, event | category | flops | bytes accessed | tf_op | source)
XLA Modules:
  0.0 36.0 jit_solution(5126854758739286819)
XLA Ops:
  0.6 0.8 %pack.1.refs_0_ = bf16[4,5120]{1,0:T(4,128)(2,1)S(1)} custom-call(bf16[4,4096]{1,0:T(4,128)(2,1)} %q_ref.1, bf16[4,512]{1,0:T(4,128)(2,1)} %k_ref.1, bf16[4,512]{1,0:T(4,128)(2,1)} %v_ref.1), custom_call_target="tpu_custom_call" | custom-call | tf_op jit(solution)/shard_map/pack/pallas_call | solution.py:349
  1.4 3.1 %collective-permute-start.1 = (bf16[4,5120]{1,0:T(4,128)(2,1)S(1)}, bf16[4,5120]{1,0:T(4,128)(2,1)S(1)}, u32[]{:S(2)}, u32[]{:S(2)}) collective-permute-start(bf16[4,5120]{1,0:T(4,128)(2,1)S(1)} %pack.1.refs_0_), channel_id=1, source_target_pairs={{0,4},{2,6},{4,0},{6,2},{8,12},{10,14},{12,8},{14,10},{1,5},{3,7},... | collective-permute-start | bytes 122888 | tf_op jit(solution)/shard_map/ppermute | solution.py:328
  4.5 2.6 %collective-permute-start.3 = (bf16[4,5120]{1,0:T(4,128)(2,1)S(1)}, bf16[4,5120]{1,0:T(4,128)(2,1)S(1)}, u32[]{:S(2)}, u32[]{:S(2)}) collective-permute-start(bf16[4,5120]{1,0:T(4,128)(2,1)S(1)} %pack.1.refs_0_), channel_id=1, source_target_pairs={{0,8},{2,10},{4,12},{6,14},{8,0},{10,2},{12,4},{14,6},{1,9},{3,11}... | collective-permute-start | bytes 122888 | tf_op jit(solution)/shard_map/ppermute | solution.py:328
  7.1 0.0 collective-permute-start.5
  7.1 0.0 collective-permute-start
  7.1 0.0 collective-permute-done.1.refs_2_
  7.1 0.5 %collective-permute-start.2 = (bf16[4,5120]{1,0:T(4,128)(2,1)S(1)}, bf16[4,5120]{1,0:T(4,128)(2,1)S(1)}, u32[]{:S(2)}, u32[]{:S(2)}) collective-permute-start(bf16[4,5120]{1,0:T(4,128)(2,1)S(1)} %collective-permute-done.1.refs_2_), channel_id=1, source_target_pairs={{0,2},{2,0},{4,6},{6,4},{8,10},{10,8},{12,14},{14,12},{1,3},{3,1},... | collective-permute-start | bytes 122888 | tf_op jit(solution)/shard_map/ppermute | solution.py:330
  7.6 2.6 %collective-permute-done.3.refs_4_ = bf16[4,5120]{1,0:T(4,128)(2,1)S(1)} collective-permute-done((bf16[4,5120]{1,0:T(4,128)(2,1)S(1)}, bf16[4,5120]{1,0:T(4,128)(2,1)S(1)}, u32[]{:S(2)}, u32[]{:S(2)}) %collective-permute-start.3) | collective-permute-done | bytes 40992 | tf_op jit(solution)/shard_map/ppermute | solution.py:328
  10.1 0.0 collective-permute-start.4
  10.1 2.7 %collective-permute-done.5.refs_6_ = bf16[4,5120]{1,0:T(4,128)(2,1)S(1)} collective-permute-done((bf16[4,5120]{1,0:T(4,128)(2,1)S(1)}, bf16[4,5120]{1,0:T(4,128)(2,1)S(1)}, u32[]{:S(2)}, u32[]{:S(2)}) %collective-permute-start.5) | collective-permute-done | bytes 40992 | tf_op jit(solution)/shard_map/ppermute | solution.py:328
  12.9 0.0 collective-permute-start.6
  12.9 0.0 slice-start
  12.9 2.7 %early.1 = (bf16[3,448,1024]{2,1,0:T(8,128)(2,1)S(1)}, bf16[3,448,1024]{2,1,0:T(8,128)(2,1)S(1)}, bf16[3,448,128]{2,1,0:T(8,128)(2,1)S(1)}, bf16[3,448,128]{2,1,...) custom-call(s32[1,448]{1,0:T(1,128)} %refs_0_.1, ...), custom_call_target="tpu_custom_call" | custom-call | flops 1409286144 | bytes 5505024 | tf_op jit(solution)/shard_map/early/pallas_call | solution.py:260
  15.5 0.0 collective-permute-done.refs_1_
  15.5 0.0 collective-permute-done.2.refs_3_
  15.5 0.0 collective-permute-done.4.refs_5_
  15.5 0.0 collective-permute-done.6.refs_7_
  15.6 0.7 %decode.1.refs_0_ = bf16[8,4096]{1,0:T(8,128)(2,1)S(1)} custom-call(bf16[4,5120]{1,0:T(4,128)(2,1)S(1)} %pack.1.refs_0_, bf16[4,5120]{1,0:T(4,128)(2,1)S(1)} %collective-permute-done.refs_1_, bf16[4,5120]{1,0:T(4,128)(2,1)S(1)} %collective-permute-done.1.refs_2_, bf16[4,5120]{1,0:T(4,128)(2,1)S(1)} %collective-permute-done.2.refs_3_, ...), custom_call_target="tpu_custom_call" | custom-call | flops 1000000000 | bytes 1048576 | tf_op jit(solution)/shard_map/decode/pallas_call | solution.py:422
  16.3 0.1 collective-permute-start.10
  16.3 1.4 %collective-permute-start.12 = (bf16[8,4096]{1,0:T(8,128)(2,1)S(1)}, bf16[8,4096]{1,0:T(8,128)(2,1)S(1)}, u32[]{:S(2)}, u32[]{:S(2)}) collective-permute-start(bf16[8,4096]{1,0:T(8,128)(2,1)S(1)} %decode.1.refs_0_), channel_id=1, source_target_pairs={{0,12},{2,14},{4,8},{6,10},{8,4},{10,6},{12,0},{14,2},{1,13},{3,15... | collective-permute-start | bytes 196616 | tf_op jit(solution)/shard_map/ppermute | solution.py:328
  17.8 2.0 %collective-permute-start.8 = (bf16[8,4096]{1,0:T(8,128)(2,1)S(1)}, bf16[8,4096]{1,0:T(8,128)(2,1)S(1)}, u32[]{:S(2)}, u32[]{:S(2)}) collective-permute-start(bf16[8,4096]{1,0:T(8,128)(2,1)S(1)} %decode.1.refs_0_), channel_id=1, source_target_pairs={{0,4},{2,6},{4,0},{6,2},{8,12},{10,14},{12,8},{14,10},{1,5},{3,7},... | collective-permute-start | bytes 196616 | tf_op jit(solution)/shard_map/ppermute | solution.py:328
  19.8 0.0 collective-permute-start.7
  19.8 3.8 %collective-permute-done.10.refs_4_ = bf16[8,4096]{1,0:T(8,128)(2,1)S(1)} collective-permute-done((bf16[8,4096]{1,0:T(8,128)(2,1)S(1)}, bf16[8,4096]{1,0:T(8,128)(2,1)S(1)}, u32[]{:S(2)}, u32[]{:S(2)}) %collective-permute-start.10) | collective-permute-done | bytes 65568 | tf_op jit(solution)/shard_map/ppermute | solution.py:328
  23.6 0.0 collective-permute-start.11
  23.6 0.0 collective-permute-done.12.refs_6_
  23.6 0.5 %collective-permute-start.13 = (bf16[8,4096]{1,0:T(8,128)(2,1)S(1)}, bf16[8,4096]{1,0:T(8,128)(2,1)S(1)}, u32[]{:S(2)}, u32[]{:S(2)}) collective-permute-start(bf16[8,4096]{1,0:T(8,128)(2,1)S(1)} %collective-permute-done.12.refs_6_), channel_id=1, source_target_pairs={{0,2},{2,0},{4,6},{6,4},{8,10},{10,8},{12,14},{14,12},{1,3},{3,1},... | collective-permute-start | bytes 196616 | tf_op jit(solution)/shard_map/ppermute | solution.py:330
  24.1 0.4 %collective-permute-done.8.refs_2_ = bf16[8,4096]{1,0:T(8,128)(2,1)S(1)} collective-permute-done((bf16[8,4096]{1,0:T(8,128)(2,1)S(1)}, bf16[8,4096]{1,0:T(8,128)(2,1)S(1)}, u32[]{:S(2)}, u32[]{:S(2)}) %collective-permute-start.8) | collective-permute-done | bytes 65568 | tf_op jit(solution)/shard_map/ppermute | solution.py:328
  24.5 0.0 collective-permute-start.9
  24.6 0.0 slice-start.1
  24.6 4.6 %late.1 = (bf16[3,448,1024]{2,1,0:T(8,128)(2,1)S(1)}, bf16[1,448,1024]{2,1,0:T(8,128)(2,1)S(1)}, bf16[1,448,128]{2,1,0:T(8,128)(2,1)S(1)}, bf16[1,448,128]{2,1,0:T(8,128)(2,1)S(1)}) custom-call(bf16[3,448,1024]{2,1,0:T(8,128)(2,1)S(1)} %get-tuple-element.18.refs_0_, ...), custom_call_target="tpu_custom_call", output_to_operand_aliasing={{0}: (4, {})} | custom-call | flops 1409286144 | bytes 5505024 | tf_op jit(solution)/shard_map/late/pallas_call | solution.py:280
  29.2 0.0 collective-permute-done.7.refs_1_
  29.2 0.0 collective-permute-done.11.refs_5_
  29.3 0.0 collective-permute-done.13.refs_7_
  29.3 0.0 collective-permute-done.9.refs_3_
  29.3 0.0 slice-done
  29.3 0.0 slice-done.1
  29.3 2.1 %project.1 = (bf16[16,1024]{1,0:T(8,128)(2,1)S(1)}, f32[16,1024]{1,0:T(8,128)S(1)}) custom-call(bf16[8,4096]{1,0:T(8,128)(2,1)S(1)} %decode.1.refs_0_, bf16[8,4096]{1,0:T(8,128)(2,1)S(1)} %collective-permute-done.7.refs_1_, bf16[8,4096]{1,0:T(8,128)(2,1)S(1)} %collective-permute-done.8.refs_2_, bf16[8,4096]{1,0:T(8,128)(2,1)S(1)} %collective-permute-done.9.refs_3_, ...), custom_call_target="tpu_custom_call" | custom-call | flops 1000000000 | bytes 8388608 | tf_op jit(solution)/shard_map/project/pallas_call | solution.py:471
  31.4 1.5 %collective-permute-start.14 = (bf16[16,1024]{1,0:T(8,128)(2,1)S(1)}, bf16[16,1024]{1,0:T(8,128)(2,1)S(1)}, u32[]{:S(2)}, u32[]{:S(2)}) collective-permute-start(bf16[16,1024]{1,0:T(8,128)(2,1)S(1)} %get-tuple-element.33), channel_id=1, source_target_pairs={{0,1},{1,0},{2,3},{3,2},{4,5},{5,4},{6,7},{7,6},{8,9},{9,8},{10,11... | collective-permute-start | bytes 98312 | tf_op jit(solution)/shard_map/ppermute | solution.py:522
  32.9 2.3 %last.1 = bf16[448,4096]{1,0:T(8,128)(2,1)} custom-call(bf16[3,448,1024]{2,1,0:T(8,128)(2,1)S(1)} %get-tuple-element.23.refs_0_, bf16[1,448,1024]{2,1,0:T(8,128)(2,1)S(1)} %get-tuple-element.24.refs_1_, bf16[1,448,128]{2,1,0:T(8,128)(2,1)S(1)} %get-tuple-element.25.refs_2_, bf16[1,448,128]{2,1,0:T(8,128)(2,1)S(1)} %get-tuple-element.26.refs_3_, ...), custom_call_target="tpu_custom_call" | custom-call | flops 469762048 | bytes 1835008 | tf_op jit(solution)/shard_map/last/pallas_call | solution.py:303
  35.2 0.2 collective-permute-done.14
  35.4 0.6 %add_convert_fusion = bf16[16,1024]{1,0:T(8,128)(2,1)} fusion(f32[16,1024]{1,0:T(8,128)S(1)} %get-tuple-element.32, bf16[16,1024]{1,0:T(8,128)(2,1)S(1)} %collective-permute-done.14), kind=kLoop, calls=%fused_computation | loop fusion | flops 49152 | bytes 131072 | tf_op jit(solution)/shard_map/convert_element_type | solution.py:523
  (1 shorter events, 0.0 us)
Async XLA Ops:
  1.4 5.7 %collective-permute-start.1 = (bf16[4,5120]{1,0:T(4,128)(2,1)S(1)}, bf16[4,5120]{1,0:T(4,128)(2,1)S(1)}, u32[]{:S(2)}, u32[]{:S(2)}) collective-permute-start(bf16[4,5120]{1,0:T(4,128)(2,1)S(1)} %pack.1.refs_0_), channel_id=1, source_target_pairs={{0,4},{2,6},{4,0},{6,2},{8,12},{10,14},{12,8},{14,10},{1,5},{3,7},... | collective-permute-start | bytes 122888 | tf_op jit(solution)/shard_map/ppermute | solution.py:328
  4.5 5.7 %collective-permute-start.3 = (bf16[4,5120]{1,0:T(4,128)(2,1)S(1)}, bf16[4,5120]{1,0:T(4,128)(2,1)S(1)}, u32[]{:S(2)}, u32[]{:S(2)}) collective-permute-start(bf16[4,5120]{1,0:T(4,128)(2,1)S(1)} %pack.1.refs_0_), channel_id=1, source_target_pairs={{0,8},{2,10},{4,12},{6,14},{8,0},{10,2},{12,4},{14,6},{1,9},{3,11}... | collective-permute-start | bytes 122888 | tf_op jit(solution)/shard_map/ppermute | solution.py:328
  7.1 5.8 %collective-permute-start.5 = (bf16[4,5120]{1,0:T(4,128)(2,1)S(1)}, bf16[4,5120]{1,0:T(4,128)(2,1)S(1)}, u32[]{:S(2)}, u32[]{:S(2)}) collective-permute-start(bf16[4,5120]{1,0:T(4,128)(2,1)S(1)} %pack.1.refs_0_), channel_id=1, source_target_pairs={{0,12},{2,14},{4,8},{6,10},{8,4},{10,6},{12,0},{14,2},{1,13},{3,15... | collective-permute-start | bytes 122888 | tf_op jit(solution)/shard_map/ppermute | solution.py:328
  7.1 8.5 %collective-permute-start = (bf16[4,5120]{1,0:T(4,128)(2,1)S(1)}, bf16[4,5120]{1,0:T(4,128)(2,1)S(1)}, u32[]{:S(2)}, u32[]{:S(2)}) collective-permute-start(bf16[4,5120]{1,0:T(4,128)(2,1)S(1)} %pack.1.refs_0_), channel_id=1, source_target_pairs={{0,2},{2,0},{4,6},{6,4},{8,10},{10,8},{12,14},{14,12},{1,3},{3,1},... | collective-permute-start | bytes 122888 | tf_op jit(solution)/shard_map/ppermute | solution.py:330
  7.1 8.5 %collective-permute-start.2 = (bf16[4,5120]{1,0:T(4,128)(2,1)S(1)}, bf16[4,5120]{1,0:T(4,128)(2,1)S(1)}, u32[]{:S(2)}, u32[]{:S(2)}) collective-permute-start(bf16[4,5120]{1,0:T(4,128)(2,1)S(1)} %collective-permute-done.1.refs_2_), channel_id=1, source_target_pairs={{0,2},{2,0},{4,6},{6,4},{8,10},{10,8},{12,14},{14,12},{1,3},{3,1},... | collective-permute-start | bytes 122888 | tf_op jit(solution)/shard_map/ppermute | solution.py:330
  10.1 5.4 %collective-permute-start.4 = (bf16[4,5120]{1,0:T(4,128)(2,1)S(1)}, bf16[4,5120]{1,0:T(4,128)(2,1)S(1)}, u32[]{:S(2)}, u32[]{:S(2)}) collective-permute-start(bf16[4,5120]{1,0:T(4,128)(2,1)S(1)} %collective-permute-done.3.refs_4_), channel_id=1, source_target_pairs={{0,2},{2,0},{4,6},{6,4},{8,10},{10,8},{12,14},{14,12},{1,3},{3,1},... | collective-permute-start | bytes 122888 | tf_op jit(solution)/shard_map/ppermute | solution.py:330
  12.9 2.7 %collective-permute-start.6 = (bf16[4,5120]{1,0:T(4,128)(2,1)S(1)}, bf16[4,5120]{1,0:T(4,128)(2,1)S(1)}, u32[]{:S(2)}, u32[]{:S(2)}) collective-permute-start(bf16[4,5120]{1,0:T(4,128)(2,1)S(1)} %collective-permute-done.5.refs_6_), channel_id=1, source_target_pairs={{0,2},{2,0},{4,6},{6,4},{8,10},{10,8},{12,14},{14,12},{1,3},{3,1},... | collective-permute-start | bytes 122888 | tf_op jit(solution)/shard_map/ppermute | solution.py:330
  12.9 16.4 %slice-start = ((s8[8388608]{0:T(1024)(128)(4,1)}), s8[4194304]{0:T(1024)(128)(4,1)S(1)}, s32[]{:S(2)}) async-start(s8[8388608]{0:T(1024)(128)(4,1)} %bitcast.2), calls=%async_computation | async-start | bytes 8388608
  16.3 7.3 %collective-permute-start.10 = (bf16[8,4096]{1,0:T(8,128)(2,1)S(1)}, bf16[8,4096]{1,0:T(8,128)(2,1)S(1)}, u32[]{:S(2)}, u32[]{:S(2)}) collective-permute-start(bf16[8,4096]{1,0:T(8,128)(2,1)S(1)} %decode.1.refs_0_), channel_id=1, source_target_pairs={{0,8},{2,10},{4,12},{6,14},{8,0},{10,2},{12,4},{14,6},{1,9},{3,11}... | collective-permute-start | bytes 196616 | tf_op jit(solution)/shard_map/ppermute | solution.py:328
  16.3 7.3 %collective-permute-start.12 = (bf16[8,4096]{1,0:T(8,128)(2,1)S(1)}, bf16[8,4096]{1,0:T(8,128)(2,1)S(1)}, u32[]{:S(2)}, u32[]{:S(2)}) collective-permute-start(bf16[8,4096]{1,0:T(8,128)(2,1)S(1)} %decode.1.refs_0_), channel_id=1, source_target_pairs={{0,12},{2,14},{4,8},{6,10},{8,4},{10,6},{12,0},{14,2},{1,13},{3,15... | collective-permute-start | bytes 196616 | tf_op jit(solution)/shard_map/ppermute | solution.py:328
  17.8 6.8 %collective-permute-start.8 = (bf16[8,4096]{1,0:T(8,128)(2,1)S(1)}, bf16[8,4096]{1,0:T(8,128)(2,1)S(1)}, u32[]{:S(2)}, u32[]{:S(2)}) collective-permute-start(bf16[8,4096]{1,0:T(8,128)(2,1)S(1)} %decode.1.refs_0_), channel_id=1, source_target_pairs={{0,4},{2,6},{4,0},{6,2},{8,12},{10,14},{12,8},{14,10},{1,5},{3,7},... | collective-permute-start | bytes 196616 | tf_op jit(solution)/shard_map/ppermute | solution.py:328
  19.8 9.4 %collective-permute-start.7 = (bf16[8,4096]{1,0:T(8,128)(2,1)S(1)}, bf16[8,4096]{1,0:T(8,128)(2,1)S(1)}, u32[]{:S(2)}, u32[]{:S(2)}) collective-permute-start(bf16[8,4096]{1,0:T(8,128)(2,1)S(1)} %decode.1.refs_0_), channel_id=1, source_target_pairs={{0,2},{2,0},{4,6},{6,4},{8,10},{10,8},{12,14},{14,12},{1,3},{3,1},... | collective-permute-start | bytes 196616 | tf_op jit(solution)/shard_map/ppermute | solution.py:330
  23.6 5.6 %collective-permute-start.11 = (bf16[8,4096]{1,0:T(8,128)(2,1)S(1)}, bf16[8,4096]{1,0:T(8,128)(2,1)S(1)}, u32[]{:S(2)}, u32[]{:S(2)}) collective-permute-start(bf16[8,4096]{1,0:T(8,128)(2,1)S(1)} %collective-permute-done.10.refs_4_), channel_id=1, source_target_pairs={{0,2},{2,0},{4,6},{6,4},{8,10},{10,8},{12,14},{14,12},{1,3},{3,1},... | collective-permute-start | bytes 196616 | tf_op jit(solution)/shard_map/ppermute | solution.py:330
  23.6 5.6 %collective-permute-start.13 = (bf16[8,4096]{1,0:T(8,128)(2,1)S(1)}, bf16[8,4096]{1,0:T(8,128)(2,1)S(1)}, u32[]{:S(2)}, u32[]{:S(2)}) collective-permute-start(bf16[8,4096]{1,0:T(8,128)(2,1)S(1)} %collective-permute-done.12.refs_6_), channel_id=1, source_target_pairs={{0,2},{2,0},{4,6},{6,4},{8,10},{10,8},{12,14},{14,12},{1,3},{3,1},... | collective-permute-start | bytes 196616 | tf_op jit(solution)/shard_map/ppermute | solution.py:330
  24.5 4.7 %collective-permute-start.9 = (bf16[8,4096]{1,0:T(8,128)(2,1)S(1)}, bf16[8,4096]{1,0:T(8,128)(2,1)S(1)}, u32[]{:S(2)}, u32[]{:S(2)}) collective-permute-start(bf16[8,4096]{1,0:T(8,128)(2,1)S(1)} %collective-permute-done.8.refs_2_), channel_id=1, source_target_pairs={{0,2},{2,0},{4,6},{6,4},{8,10},{10,8},{12,14},{14,12},{1,3},{3,1},... | collective-permute-start | bytes 196616 | tf_op jit(solution)/shard_map/ppermute | solution.py:330
  24.6 4.7 %slice-start.1 = ((s8[8388608]{0:T(1024)(128)(4,1)}), s8[4194304]{0:T(1024)(128)(4,1)S(1)}, s32[]{:S(2)}) async-start(s8[8388608]{0:T(1024)(128)(4,1)} %bitcast.2), calls=%async_computation.1 | async-start | bytes 8388608
  31.4 3.9 %collective-permute-start.14 = (bf16[16,1024]{1,0:T(8,128)(2,1)S(1)}, bf16[16,1024]{1,0:T(8,128)(2,1)S(1)}, u32[]{:S(2)}, u32[]{:S(2)}) collective-permute-start(bf16[16,1024]{1,0:T(8,128)(2,1)S(1)} %get-tuple-element.33), channel_id=1, source_target_pairs={{0,1},{1,0},{2,3},{3,2},{4,5},{5,4},{6,7},{7,6},{8,9},{9,8},{10,11... | collective-permute-start | bytes 98312 | tf_op jit(solution)/shard_map/ppermute | solution.py:522

commit v4 on v3

--- a/solution.py
+++ b/solution.py
@@ -320,11 +320,18 @@
     return n & (n - 1) == 0 and 2 <= n <= 8
 
 
-def spread(x, n):
+def far_order(n, name):
+    order = list(range(n - 2, 0, -2))
+    if name == "pooled" and len(order) == 3:
+        order = [order[1], order[0], order[2]]
+    return order
+
+
+def spread(x, n, name):
     if not xor_plan(n):
         return [lax.all_gather(x, "pool", axis=0, tiled=True)]
     pieces = {0: x}
-    for d in range(n - 2, 0, -2):
+    for d in far_order(n, name):
         pieces[d] = lax.ppermute(x, "pool", [(i, i ^ d) for i in range(n)])
     for d in range(0, n, 2):
         pieces[d + 1] = lax.ppermute(
@@ -391,7 +398,7 @@
         )
         for g in heads
     ]
-    weights, own_weights, inverses = [], [], []
+    weights, own_weights = [], []
     for g in heads:
         new_key = rows[:, lanes(g, q_width)]
         own = jnp.sum(
@@ -402,14 +409,14 @@
         highest = jnp.maximum(jnp.max(score, axis=-1, keepdims=True), own)
         weight = jnp.exp2(score - highest)
         own_weight = jnp.exp2(own - highest)
-        inverses.append(1.0 / (jnp.sum(weight, axis=-1, keepdims=True) + own_weight))
-        weights.append(weight.astype(jnp.bfloat16).reshape(group * slots, cap))
-        own_weights.append(own_weight)
+        inverse = 1.0 / (jnp.sum(weight, axis=-1, keepdims=True) + own_weight)
+        weights.append((weight * inverse).astype(jnp.bfloat16).reshape(group * slots, cap))
+        own_weights.append((own_weight * inverse).astype(jnp.bfloat16).astype(jnp.float32))
     for g in heads:
         result = jnp.dot(weights[g], v_ref[:, lanes(g)], preferred_element_type=jnp.float32)
         result = result.reshape(group, slots, HEAD_DIM)
         new_value = rows[:, lanes(g, q_width + kv_width)]
-        result = (result + own_weights[g] * new_value[None]) * inverses[g]
+        result = result + own_weights[g] * new_value[None]
         for h in range(group):
             o_ref[:, lanes(g * group + h)] = result[h].astype(jnp.bfloat16)
 
@@ -507,13 +514,13 @@
     head_items = (rows // ROW_BLOCK) * 3 // 7
     prompt = (prompt_query, prompt_key, prompt_value)
 
-    homes = spread(pack(home_query, home_key, home_value), n)
+    homes = spread(pack(home_query, home_key, home_value), n, "home")
     done, q1, k1, v1, bias, ck, cv, pick, seg, gather = early_part(
         n, tp, near, group, window, home_rows, head_items, doc_ids, *prompt, cache_start,
         cache_len, cache_keys, cache_values,
     )
     slot_out = decode(homes, pick, seg, ck, cv, group)
-    pooled = spread(slot_out, n)
+    pooled = spread(slot_out, n, "pooled")
     done, q2, k2, v2 = late_part(far, group, window, head_items, done, q1, k1, v1, bias, *prompt)
     partial = project(pooled, gather, out_weight, tp)
     prompt_out = last_part(group, window, prompt_query.shape, done, q2, k2, v2, bias)

time: 36.2 us -> 36.3 us (level)
  transfers between devices with their start and end apart: 15 -> 15, of which waited for: 5 -> 5; matrix products, arithmetic and copies ran while one was open for 0% -> 0% of each run, Pallas kernels for 27% -> 26%
where the time goes in v4:
time: 36.3 us; the launch traced here: 36.1 us
  Pallas kernels  13.3 us (37%)
  starting transfers between devices  11.8 us (33%)
  waiting for transfers between devices  9.67 us (27%)
  between operations  0.76 us (2%)
  other arithmetic  0.62 us (2%)
    ppermute x6, waiting for transfers between devices, spread(): pieces[d] = lax.ppermute(x, 'pool', [(i, i ^ d) for i in range(n)])  9.49 us
    ppermute x6, starting transfers between devices, spread(): pieces[d] = lax.ppermute(x, 'pool', [(i, i ^ d) for i in range(n)])  9.19 us
    pallas_call x1, Pallas kernels, late_part(): pl.pallas_call(functools.partial(late_kernel, group, window, head_items),...  4.63 us
    pallas_call x1, Pallas kernels, early_part(): pl.pallas_call(functools.partial(early_kernel, n, tp, group, window, home...  2.65 us
    pallas_call x1, Pallas kernels, last_part(): pl.pallas_call(functools.partial(last_kernel, group, window), in_specs=[V...  2.27 us
    pallas_call x1, Pallas kernels, project(): pl.pallas_call(functools.partial(project_kernel, len(pieces), tp), in_spe...  2.13 us
    ppermute x1, starting transfers between devices, local(): other = lax.ppermute(send, 'tp', [(0, 1), (1, 0)])  1.5 us
    ppermute x8, starting transfers between devices, spread(): lax.ppermute(pieces[d], 'pool', [(i, i ^ 1) for i in range(n)])  1.07 us
  transfers between devices with their start and end apart: 15, of which 5 were waited for; matrix products, arithmetic and copies ran while one was open for 0% of the time, Pallas kernels for 26%

profile of v4, /device:TPU:0, one launch (start us, length us, event | category | flops | bytes accessed | tf_op | source)
XLA Modules:
  0.0 36.1 jit_solution(12671292820395145293)
XLA Ops:
  0.6 0.8 %pack.1.refs_0_ = bf16[4,5120]{1,0:T(4,128)(2,1)S(1)} custom-call(bf16[4,4096]{1,0:T(4,128)(2,1)} %q_ref.1, bf16[4,512]{1,0:T(4,128)(2,1)} %k_ref.1, bf16[4,512]{1,0:T(4,128)(2,1)} %v_ref.1), custom_call_target="tpu_custom_call" | custom-call | tf_op jit(solution)/shard_map/pack/pallas_call | solution.py:356
  1.4 3.1 %collective-permute-start.1 = (bf16[4,5120]{1,0:T(4,128)(2,1)S(1)}, bf16[4,5120]{1,0:T(4,128)(2,1)S(1)}, u32[]{:S(2)}, u32[]{:S(2)}) collective-permute-start(bf16[4,5120]{1,0:T(4,128)(2,1)S(1)} %pack.1.refs_0_), channel_id=1, source_target_pairs={{0,4},{2,6},{4,0},{6,2},{8,12},{10,14},{12,8},{14,10},{1,5},{3,7},... | collective-permute-start | bytes 122888 | tf_op jit(solution)/shard_map/ppermute | solution.py:335
  4.5 2.6 %collective-permute-start.3 = (bf16[4,5120]{1,0:T(4,128)(2,1)S(1)}, bf16[4,5120]{1,0:T(4,128)(2,1)S(1)}, u32[]{:S(2)}, u32[]{:S(2)}) collective-permute-start(bf16[4,5120]{1,0:T(4,128)(2,1)S(1)} %pack.1.refs_0_), channel_id=1, source_target_pairs={{0,8},{2,10},{4,12},{6,14},{8,0},{10,2},{12,4},{14,6},{1,9},{3,11}... | collective-permute-start | bytes 122888 | tf_op jit(solution)/shard_map/ppermute | solution.py:335
  7.1 0.0 collective-permute-start.5
  7.1 0.0 collective-permute-start
  7.1 0.0 collective-permute-done.1.refs_2_
  7.1 0.5 %collective-permute-start.2 = (bf16[4,5120]{1,0:T(4,128)(2,1)S(1)}, bf16[4,5120]{1,0:T(4,128)(2,1)S(1)}, u32[]{:S(2)}, u32[]{:S(2)}) collective-permute-start(bf16[4,5120]{1,0:T(4,128)(2,1)S(1)} %collective-permute-done.1.refs_2_), channel_id=1, source_target_pairs={{0,2},{2,0},{4,6},{6,4},{8,10},{10,8},{12,14},{14,12},{1,3},{3,1},... | collective-permute-start | bytes 122888 | tf_op jit(solution)/shard_map/ppermute | solution.py:337
  7.6 2.6 %collective-permute-done.3.refs_4_ = bf16[4,5120]{1,0:T(4,128)(2,1)S(1)} collective-permute-done((bf16[4,5120]{1,0:T(4,128)(2,1)S(1)}, bf16[4,5120]{1,0:T(4,128)(2,1)S(1)}, u32[]{:S(2)}, u32[]{:S(2)}) %collective-permute-start.3) | collective-permute-done | bytes 40992 | tf_op jit(solution)/shard_map/ppermute | solution.py:335
  10.1 0.0 collective-permute-start.4
  10.1 2.7 %collective-permute-done.5.refs_6_ = bf16[4,5120]{1,0:T(4,128)(2,1)S(1)} collective-permute-done((bf16[4,5120]{1,0:T(4,128)(2,1)S(1)}, bf16[4,5120]{1,0:T(4,128)(2,1)S(1)}, u32[]{:S(2)}, u32[]{:S(2)}) %collective-permute-start.5) | collective-permute-done | bytes 40992 | tf_op jit(solution)/shard_map/ppermute | solution.py:335
  12.9 0.0 collective-permute-start.6
  12.9 0.0 slice-start
  12.9 2.7 %early.1 = (bf16[3,448,1024]{2,1,0:T(8,128)(2,1)S(1)}, bf16[3,448,1024]{2,1,0:T(8,128)(2,1)S(1)}, bf16[3,448,128]{2,1,0:T(8,128)(2,1)S(1)}, bf16[3,448,128]{2,1,...) custom-call(s32[1,448]{1,0:T(1,128)} %refs_0_.1, ...), custom_call_target="tpu_custom_call" | custom-call | flops 1409286144 | bytes 5505024 | tf_op jit(solution)/shard_map/early/pallas_call | solution.py:260
  15.5 0.0 collective-permute-done.refs_1_
  15.5 0.0 collective-permute-done.2.refs_3_
  15.5 0.0 collective-permute-done.4.refs_5_
  15.5 0.0 collective-permute-done.6.refs_7_
  15.6 0.8 %decode.1.refs_0_ = bf16[8,4096]{1,0:T(8,128)(2,1)S(1)} custom-call(bf16[4,5120]{1,0:T(4,128)(2,1)S(1)} %pack.1.refs_0_, bf16[4,5120]{1,0:T(4,128)(2,1)S(1)} %collective-permute-done.refs_1_, bf16[4,5120]{1,0:T(4,128)(2,1)S(1)} %collective-permute-done.1.refs_2_, bf16[4,5120]{1,0:T(4,128)(2,1)S(1)} %collective-permute-done.2.refs_3_, ...), custom_call_target="tpu_custom_call" | custom-call | flops 1000000000 | bytes 1048576 | tf_op jit(solution)/shard_map/decode/pallas_call | solution.py:429
  16.4 0.1 collective-permute-start.10
  16.4 1.4 %collective-permute-start.12 = (bf16[8,4096]{1,0:T(8,128)(2,1)S(1)}, bf16[8,4096]{1,0:T(8,128)(2,1)S(1)}, u32[]{:S(2)}, u32[]{:S(2)}) collective-permute-start(bf16[8,4096]{1,0:T(8,128)(2,1)S(1)} %decode.1.refs_0_), channel_id=1, source_target_pairs={{0,12},{2,14},{4,8},{6,10},{8,4},{10,6},{12,0},{14,2},{1,13},{3,15... | collective-permute-start | bytes 196616 | tf_op jit(solution)/shard_map/ppermute | solution.py:335
  17.9 2.0 %collective-permute-start.8 = (bf16[8,4096]{1,0:T(8,128)(2,1)S(1)}, bf16[8,4096]{1,0:T(8,128)(2,1)S(1)}, u32[]{:S(2)}, u32[]{:S(2)}) collective-permute-start(bf16[8,4096]{1,0:T(8,128)(2,1)S(1)} %decode.1.refs_0_), channel_id=1, source_target_pairs={{0,4},{2,6},{4,0},{6,2},{8,12},{10,14},{12,8},{14,10},{1,5},{3,7},... | collective-permute-start | bytes 196616 | tf_op jit(solution)/shard_map/ppermute | solution.py:335
  19.9 0.0 collective-permute-start.7
  19.9 3.8 %collective-permute-done.10.refs_4_ = bf16[8,4096]{1,0:T(8,128)(2,1)S(1)} collective-permute-done((bf16[8,4096]{1,0:T(8,128)(2,1)S(1)}, bf16[8,4096]{1,0:T(8,128)(2,1)S(1)}, u32[]{:S(2)}, u32[]{:S(2)}) %collective-permute-start.10) | collective-permute-done | bytes 65568 | tf_op jit(solution)/shard_map/ppermute | solution.py:335
  23.7 0.0 collective-permute-start.11
  23.7 0.0 collective-permute-done.12.refs_6_
  23.7 0.5 %collective-permute-start.13 = (bf16[8,4096]{1,0:T(8,128)(2,1)S(1)}, bf16[8,4096]{1,0:T(8,128)(2,1)S(1)}, u32[]{:S(2)}, u32[]{:S(2)}) collective-permute-start(bf16[8,4096]{1,0:T(8,128)(2,1)S(1)} %collective-permute-done.12.refs_6_), channel_id=1, source_target_pairs={{0,2},{2,0},{4,6},{6,4},{8,10},{10,8},{12,14},{14,12},{1,3},{3,1},... | collective-permute-start | bytes 196616 | tf_op jit(solution)/shard_map/ppermute | solution.py:337
  24.2 0.4 %collective-permute-done.8.refs_2_ = bf16[8,4096]{1,0:T(8,128)(2,1)S(1)} collective-permute-done((bf16[8,4096]{1,0:T(8,128)(2,1)S(1)}, bf16[8,4096]{1,0:T(8,128)(2,1)S(1)}, u32[]{:S(2)}, u32[]{:S(2)}) %collective-permute-start.8) | collective-permute-done | bytes 65568 | tf_op jit(solution)/shard_map/ppermute | solution.py:335
  24.6 0.0 collective-permute-start.9
  24.7 0.0 slice-start.1
  24.7 4.6 %late.1 = (bf16[3,448,1024]{2,1,0:T(8,128)(2,1)S(1)}, bf16[1,448,1024]{2,1,0:T(8,128)(2,1)S(1)}, bf16[1,448,128]{2,1,0:T(8,128)(2,1)S(1)}, bf16[1,448,128]{2,1,0:T(8,128)(2,1)S(1)}) custom-call(bf16[3,448,1024]{2,1,0:T(8,128)(2,1)S(1)} %get-tuple-element.18.refs_0_, ...), custom_call_target="tpu_custom_call", output_to_operand_aliasing={{0}: (4, {})} | custom-call | flops 1409286144 | bytes 5505024 | tf_op jit(solution)/shard_map/late/pallas_call | solution.py:280
  29.3 0.0 collective-permute-done.7.refs_1_
  29.3 0.0 collective-permute-done.11.refs_5_
  29.3 0.0 collective-permute-done.13.refs_7_
  29.3 0.0 collective-permute-done.9.refs_3_
  29.4 0.0 slice-done
  29.4 0.0 slice-done.1
  29.4 2.1 %project.1 = (bf16[16,1024]{1,0:T(8,128)(2,1)S(1)}, f32[16,1024]{1,0:T(8,128)S(1)}) custom-call(bf16[8,4096]{1,0:T(8,128)(2,1)S(1)} %decode.1.refs_0_, bf16[8,4096]{1,0:T(8,128)(2,1)S(1)} %collective-permute-done.7.refs_1_, bf16[8,4096]{1,0:T(8,128)(2,1)S(1)} %collective-permute-done.8.refs_2_, bf16[8,4096]{1,0:T(8,128)(2,1)S(1)} %collective-permute-done.9.refs_3_, ...), custom_call_target="tpu_custom_call" | custom-call | flops 1000000000 | bytes 8388608 | tf_op jit(solution)/shard_map/project/pallas_call | solution.py:478
  31.5 1.5 %collective-permute-start.14 = (bf16[16,1024]{1,0:T(8,128)(2,1)S(1)}, bf16[16,1024]{1,0:T(8,128)(2,1)S(1)}, u32[]{:S(2)}, u32[]{:S(2)}) collective-permute-start(bf16[16,1024]{1,0:T(8,128)(2,1)S(1)} %get-tuple-element.33), channel_id=1, source_target_pairs={{0,1},{1,0},{2,3},{3,2},{4,5},{5,4},{6,7},{7,6},{8,9},{9,8},{10,11... | collective-permute-start | bytes 98312 | tf_op jit(solution)/shard_map/ppermute | solution.py:529
  33.0 2.3 %last.1 = bf16[448,4096]{1,0:T(8,128)(2,1)} custom-call(bf16[3,448,1024]{2,1,0:T(8,128)(2,1)S(1)} %get-tuple-element.23.refs_0_, bf16[1,448,1024]{2,1,0:T(8,128)(2,1)S(1)} %get-tuple-element.24.refs_1_, bf16[1,448,128]{2,1,0:T(8,128)(2,1)S(1)} %get-tuple-element.25.refs_2_, bf16[1,448,128]{2,1,0:T(8,128)(2,1)S(1)} %get-tuple-element.26.refs_3_, ...), custom_call_target="tpu_custom_call" | custom-call | flops 469762048 | bytes 1835008 | tf_op jit(solution)/shard_map/last/pallas_call | solution.py:303
  35.3 0.2 collective-permute-done.14
  35.4 0.6 %add_convert_fusion = bf16[16,1024]{1,0:T(8,128)(2,1)} fusion(f32[16,1024]{1,0:T(8,128)S(1)} %get-tuple-element.32, bf16[16,1024]{1,0:T(8,128)(2,1)S(1)} %collective-permute-done.14), kind=kLoop, calls=%fused_computation | loop fusion | flops 49152 | bytes 131072 | tf_op jit(solution)/shard_map/convert_element_type | solution.py:530
  (1 shorter events, 0.0 us)
Async XLA Ops:
  1.4 5.7 %collective-permute-start.1 = (bf16[4,5120]{1,0:T(4,128)(2,1)S(1)}, bf16[4,5120]{1,0:T(4,128)(2,1)S(1)}, u32[]{:S(2)}, u32[]{:S(2)}) collective-permute-start(bf16[4,5120]{1,0:T(4,128)(2,1)S(1)} %pack.1.refs_0_), channel_id=1, source_target_pairs={{0,4},{2,6},{4,0},{6,2},{8,12},{10,14},{12,8},{14,10},{1,5},{3,7},... | collective-permute-start | bytes 122888 | tf_op jit(solution)/shard_map/ppermute | solution.py:335
  4.5 5.7 %collective-permute-start.3 = (bf16[4,5120]{1,0:T(4,128)(2,1)S(1)}, bf16[4,5120]{1,0:T(4,128)(2,1)S(1)}, u32[]{:S(2)}, u32[]{:S(2)}) collective-permute-start(bf16[4,5120]{1,0:T(4,128)(2,1)S(1)} %pack.1.refs_0_), channel_id=1, source_target_pairs={{0,8},{2,10},{4,12},{6,14},{8,0},{10,2},{12,4},{14,6},{1,9},{3,11}... | collective-permute-start | bytes 122888 | tf_op jit(solution)/shard_map/ppermute | solution.py:335
  7.1 5.8 %collective-permute-start.5 = (bf16[4,5120]{1,0:T(4,128)(2,1)S(1)}, bf16[4,5120]{1,0:T(4,128)(2,1)S(1)}, u32[]{:S(2)}, u32[]{:S(2)}) collective-permute-start(bf16[4,5120]{1,0:T(4,128)(2,1)S(1)} %pack.1.refs_0_), channel_id=1, source_target_pairs={{0,12},{2,14},{4,8},{6,10},{8,4},{10,6},{12,0},{14,2},{1,13},{3,15... | collective-permute-start | bytes 122888 | tf_op jit(solution)/shard_map/ppermute | solution.py:335
  7.1 8.5 %collective-permute-start = (bf16[4,5120]{1,0:T(4,128)(2,1)S(1)}, bf16[4,5120]{1,0:T(4,128)(2,1)S(1)}, u32[]{:S(2)}, u32[]{:S(2)}) collective-permute-start(bf16[4,5120]{1,0:T(4,128)(2,1)S(1)} %pack.1.refs_0_), channel_id=1, source_target_pairs={{0,2},{2,0},{4,6},{6,4},{8,10},{10,8},{12,14},{14,12},{1,3},{3,1},... | collective-permute-start | bytes 122888 | tf_op jit(solution)/shard_map/ppermute | solution.py:337
  7.1 8.5 %collective-permute-start.2 = (bf16[4,5120]{1,0:T(4,128)(2,1)S(1)}, bf16[4,5120]{1,0:T(4,128)(2,1)S(1)}, u32[]{:S(2)}, u32[]{:S(2)}) collective-permute-start(bf16[4,5120]{1,0:T(4,128)(2,1)S(1)} %collective-permute-done.1.refs_2_), channel_id=1, source_target_pairs={{0,2},{2,0},{4,6},{6,4},{8,10},{10,8},{12,14},{14,12},{1,3},{3,1},... | collective-permute-start | bytes 122888 | tf_op jit(solution)/shard_map/ppermute | solution.py:337
  10.1 5.4 %collective-permute-start.4 = (bf16[4,5120]{1,0:T(4,128)(2,1)S(1)}, bf16[4,5120]{1,0:T(4,128)(2,1)S(1)}, u32[]{:S(2)}, u32[]{:S(2)}) collective-permute-start(bf16[4,5120]{1,0:T(4,128)(2,1)S(1)} %collective-permute-done.3.refs_4_), channel_id=1, source_target_pairs={{0,2},{2,0},{4,6},{6,4},{8,10},{10,8},{12,14},{14,12},{1,3},{3,1},... | collective-permute-start | bytes 122888 | tf_op jit(solution)/shard_map/ppermute | solution.py:337
  12.9 2.7 %collective-permute-start.6 = (bf16[4,5120]{1,0:T(4,128)(2,1)S(1)}, bf16[4,5120]{1,0:T(4,128)(2,1)S(1)}, u32[]{:S(2)}, u32[]{:S(2)}) collective-permute-start(bf16[4,5120]{1,0:T(4,128)(2,1)S(1)} %collective-permute-done.5.refs_6_), channel_id=1, source_target_pairs={{0,2},{2,0},{4,6},{6,4},{8,10},{10,8},{12,14},{14,12},{1,3},{3,1},... | collective-permute-start | bytes 122888 | tf_op jit(solution)/shard_map/ppermute | solution.py:337
  12.9 16.5 %slice-start = ((s8[8388608]{0:T(1024)(128)(4,1)}), s8[4194304]{0:T(1024)(128)(4,1)S(1)}, s32[]{:S(2)}) async-start(s8[8388608]{0:T(1024)(128)(4,1)} %bitcast.2), calls=%async_computation | async-start | bytes 8388608
  16.4 7.3 %collective-permute-start.10 = (bf16[8,4096]{1,0:T(8,128)(2,1)S(1)}, bf16[8,4096]{1,0:T(8,128)(2,1)S(1)}, u32[]{:S(2)}, u32[]{:S(2)}) collective-permute-start(bf16[8,4096]{1,0:T(8,128)(2,1)S(1)} %decode.1.refs_0_), channel_id=1, source_target_pairs={{0,8},{2,10},{4,12},{6,14},{8,0},{10,2},{12,4},{14,6},{1,9},{3,11}... | collective-permute-start | bytes 196616 | tf_op jit(solution)/shard_map/ppermute | solution.py:335
  16.4 7.3 %collective-permute-start.12 = (bf16[8,4096]{1,0:T(8,128)(2,1)S(1)}, bf16[8,4096]{1,0:T(8,128)(2,1)S(1)}, u32[]{:S(2)}, u32[]{:S(2)}) collective-permute-start(bf16[8,4096]{1,0:T(8,128)(2,1)S(1)} %decode.1.refs_0_), channel_id=1, source_target_pairs={{0,12},{2,14},{4,8},{6,10},{8,4},{10,6},{12,0},{14,2},{1,13},{3,15... | collective-permute-start | bytes 196616 | tf_op jit(solution)/shard_map/ppermute | solution.py:335
  17.9 6.8 %collective-permute-start.8 = (bf16[8,4096]{1,0:T(8,128)(2,1)S(1)}, bf16[8,4096]{1,0:T(8,128)(2,1)S(1)}, u32[]{:S(2)}, u32[]{:S(2)}) collective-permute-start(bf16[8,4096]{1,0:T(8,128)(2,1)S(1)} %decode.1.refs_0_), channel_id=1, source_target_pairs={{0,4},{2,6},{4,0},{6,2},{8,12},{10,14},{12,8},{14,10},{1,5},{3,7},... | collective-permute-start | bytes 196616 | tf_op jit(solution)/shard_map/ppermute | solution.py:335
  19.9 9.4 %collective-permute-start.7 = (bf16[8,4096]{1,0:T(8,128)(2,1)S(1)}, bf16[8,4096]{1,0:T(8,128)(2,1)S(1)}, u32[]{:S(2)}, u32[]{:S(2)}) collective-permute-start(bf16[8,4096]{1,0:T(8,128)(2,1)S(1)} %decode.1.refs_0_), channel_id=1, source_target_pairs={{0,2},{2,0},{4,6},{6,4},{8,10},{10,8},{12,14},{14,12},{1,3},{3,1},... | collective-permute-start | bytes 196616 | tf_op jit(solution)/shard_map/ppermute | solution.py:337
  23.7 5.6 %collective-permute-start.11 = (bf16[8,4096]{1,0:T(8,128)(2,1)S(1)}, bf16[8,4096]{1,0:T(8,128)(2,1)S(1)}, u32[]{:S(2)}, u32[]{:S(2)}) collective-permute-start(bf16[8,4096]{1,0:T(8,128)(2,1)S(1)} %collective-permute-done.10.refs_4_), channel_id=1, source_target_pairs={{0,2},{2,0},{4,6},{6,4},{8,10},{10,8},{12,14},{14,12},{1,3},{3,1},... | collective-permute-start | bytes 196616 | tf_op jit(solution)/shard_map/ppermute | solution.py:337
  23.7 5.6 %collective-permute-start.13 = (bf16[8,4096]{1,0:T(8,128)(2,1)S(1)}, bf16[8,4096]{1,0:T(8,128)(2,1)S(1)}, u32[]{:S(2)}, u32[]{:S(2)}) collective-permute-start(bf16[8,4096]{1,0:T(8,128)(2,1)S(1)} %collective-permute-done.12.refs_6_), channel_id=1, source_target_pairs={{0,2},{2,0},{4,6},{6,4},{8,10},{10,8},{12,14},{14,12},{1,3},{3,1},... | collective-permute-start | bytes 196616 | tf_op jit(solution)/shard_map/ppermute | solution.py:337
  24.6 4.7 %collective-permute-start.9 = (bf16[8,4096]{1,0:T(8,128)(2,1)S(1)}, bf16[8,4096]{1,0:T(8,128)(2,1)S(1)}, u32[]{:S(2)}, u32[]{:S(2)}) collective-permute-start(bf16[8,4096]{1,0:T(8,128)(2,1)S(1)} %collective-permute-done.8.refs_2_), channel_id=1, source_target_pairs={{0,2},{2,0},{4,6},{6,4},{8,10},{10,8},{12,14},{14,12},{1,3},{3,1},... | collective-permute-start | bytes 196616 | tf_op jit(solution)/shard_map/ppermute | solution.py:337
  24.7 4.7 %slice-start.1 = ((s8[8388608]{0:T(1024)(128)(4,1)}), s8[4194304]{0:T(1024)(128)(4,1)S(1)}, s32[]{:S(2)}) async-start(s8[8388608]{0:T(1024)(128)(4,1)} %bitcast.2), calls=%async_computation.1 | async-start | bytes 8388608
  31.5 3.9 %collective-permute-start.14 = (bf16[16,1024]{1,0:T(8,128)(2,1)S(1)}, bf16[16,1024]{1,0:T(8,128)(2,1)S(1)}, u32[]{:S(2)}, u32[]{:S(2)}) collective-permute-start(bf16[16,1024]{1,0:T(8,128)(2,1)S(1)} %get-tuple-element.33), channel_id=1, source_target_pairs={{0,1},{1,0},{2,3},{3,2},{4,5},{5,4},{6,7},{7,6},{8,9},{9,8},{10,11... | collective-permute-start | bytes 98312 | tf_op jit(solution)/shard_map/ppermute | solution.py:529

commit v5 on v4

--- a/solution.py
+++ b/solution.py
@@ -11,28 +11,50 @@
 HEAD_DIM = 128
 LOG2E = 1.4426950408889634
 ROW_BLOCK = 32
+EARLY, LATE = 0.07, 0.55
 VMEM = pl.BlockSpec(memory_space=pltpu.VMEM)
 HBM = pl.BlockSpec(memory_space=pltpu.HBM)
 
 
-def attend(items, group, window, q_ref, k_ref, v_ref, bias_ref, s_ref, p_ref, o_ref,
-           finished=lambda head, b: None):
-    block = ROW_BLOCK
-    stacked = group * block
+def prompt_items(heads, rows, group, window):
+    items = []
+    for head in range(heads):
+        row = 0
+        while row < rows:
+            count = 2 * ROW_BLOCK if row + 2 * ROW_BLOCK <= window else ROW_BLOCK
+            count = min(count, rows - row)
+            start = max(0, row + count - window)
+            span = min(window, -(-(row + count) // HEAD_DIM) * HEAD_DIM)
+            items.append(((head, row, count, start, span), group * count + 2 * HEAD_DIM))
+            row += count
+    return items
+
+
+def shares(heads, rows, group, window):
+    items = prompt_items(heads, rows, group, window)
+    total = sum(price for _, price in items)
+    parts, spent = ([], [], []), 0
+    for item, price in items:
+        spent += price
+        share = spent / total
+        parts[0 if share <= EARLY else 1 if share <= EARLY + LATE else 2].append(item)
+    return parts
+
+
+def attend(items, group, q_ref, k_ref, v_ref, bias_ref, s_ref, p_ref, o_ref,
+           ready=lambda item: None, finished=lambda item: None):
     scale = HEAD_DIM ** (-0.5) * LOG2E
 
-    def place_of(t):
-        head, b = items[t]
-        start = max(0, (b + 1) * block - window)
-        span = min(window, -(-(b + 1) * block // HEAD_DIM) * HEAD_DIM)
-        return head, b, slice(b * block, (b + 1) * block), start, span
-
     def score(t):
-        head, _, at, start, span = place_of(t)
+        head, row, count, start, span = items[t]
         query = jnp.concatenate(
-            [q_ref[head, at, h * HEAD_DIM : (h + 1) * HEAD_DIM] for h in range(group)], axis=0
-        )
-        s_ref[t % 2, :, :span] = lax.dot_general(
+            [
+                q_ref[head, row : row + count, h * HEAD_DIM : (h + 1) * HEAD_DIM]
+                for h in range(group)
+            ],
+            axis=0,
+        )
+        s_ref[t % 2, : group * count, :span] = lax.dot_general(
             query,
             k_ref[head, start : start + span, :],
             (((1,), (1,)), ((), ())),
@@ -40,28 +62,32 @@
         )
 
     def weigh(t):
-        _, b, _, _, span = place_of(t)
-        scores = s_ref[t % 2, :, :span].reshape(group, block, span) * scale
-        scores = scores + bias_ref[b, :, :span][None]
+        _, row, count, _, span = items[t]
+        scores = s_ref[t % 2, : group * count, :span].reshape(group, count, span) * scale
+        scores = scores + bias_ref[row : row + count, :span][None]
         highest = jnp.max(scores, axis=-1, keepdims=True)
-        weights = jnp.exp2(scores - highest).astype(jnp.bfloat16).reshape(stacked, span)
+        weights = jnp.exp2(scores - highest).astype(jnp.bfloat16).reshape(group * count, span)
         for c in range(span // HEAD_DIM):
-            p_ref[t % 2, c] = weights[:, c * HEAD_DIM : (c + 1) * HEAD_DIM]
+            p_ref[t % 2, c, : group * count] = weights[:, c * HEAD_DIM : (c + 1) * HEAD_DIM]
 
     def combine(t):
-        head, _, at, start, span = place_of(t)
+        head, row, count, start, span = items[t]
         values = v_ref[head, start : start + span, :]
         values = jnp.concatenate([values, jnp.ones_like(values)], axis=1)
-        weights = jnp.concatenate([p_ref[t % 2, c] for c in range(span // HEAD_DIM)], axis=1)
+        weights = jnp.concatenate(
+            [p_ref[t % 2, c, : group * count] for c in range(span // HEAD_DIM)], axis=1
+        )
         both = jnp.dot(weights, values, preferred_element_type=jnp.float32)
         result = (both[:, :HEAD_DIM] / both[:, HEAD_DIM:]).astype(jnp.bfloat16)
         for h in range(group):
-            o_ref[head, at, h * HEAD_DIM : (h + 1) * HEAD_DIM] = result[
-                h * block : (h + 1) * block
+            o_ref[head, row : row + count, h * HEAD_DIM : (h + 1) * HEAD_DIM] = result[
+                h * count : (h + 1) * count
             ]
 
     total = len(items)
     for t in range(total + 2):
+        if t < total:
+            ready(items[t])
         if t >= 2:
             combine(t - 2)
         if t < total:
@@ -69,21 +95,19 @@
         if 1 <= t <= total:
             weigh(t - 1)
         if t >= 2:
-            finished(*items[t - 2])
-
-
-def early_kernel(n, tp, group, window, home_rows, slots, head_items, *refs):
-    (doc_hbm, q_hbm, k_hbm, v_hbm, start_hbm, len_hbm, ck_hbm, cv_hbm) = refs[:8]
+            finished(items[t - 2])
+
+
+def early_kernel(n, tp, near, group, window, home_rows, slots, items, *refs):
+    (doc_ref, start_ref, len_ref, q_hbm, k_hbm, v_hbm, ck_hbm, cv_hbm) = refs[:8]
     (o_ref, q_ref, k_ref, v_ref, bias_ref, ck_ref, cv_ref, pick_ref, seg_ref, gather_ref) = (
         refs[8:18]
     )
-    doc_ref, start_ref, len_ref, s_ref, p_ref, sems = refs[18:]
-    near, rows, width = q_ref.shape
-    block = ROW_BLOCK
-    blocks = rows // block
+    s_ref, p_ref, sems = refs[18:]
+    _, rows, width = q_ref.shape
     cap = ck_hbm.shape[0]
-    requests = start_hbm.shape[1]
-    cut = head_items * block
+    requests = start_ref.shape[1]
+    cut = max(item[1] + item[2] for item in items)
     copies = {}
 
     def begin(name, src, dst):
@@ -91,9 +115,6 @@
         copies[name] = copy
         copy.start()
 
-    begin("doc", doc_hbm, doc_ref)
-    begin("start", start_hbm, start_ref)
-    begin("len", len_hbm, len_ref)
     for i in range(near):
         lanes = slice(i * HEAD_DIM, (i + 1) * HEAD_DIM)
         cols = slice(i * width, (i + 1) * width)
@@ -111,9 +132,8 @@
     def grid(shape):
         return lax.broadcasted_iota(jnp.int32, shape, 0), lax.broadcasted_iota(jnp.int32, shape, 1)
 
-    for name in ("doc", "start", "len"):
-        copies[name].wait()
-    for b in range(blocks):
+    block = ROW_BLOCK
+    for b in range(rows // block):
         start = max(0, (b + 1) * block - window)
         key_doc = jnp.broadcast_to(
             doc_ref[:, start : start + window].astype(jnp.float32), (block, window)
@@ -122,7 +142,7 @@
         row, col = row + b * block, col + start
         row_doc = jnp.sum(jnp.where(row == col, key_doc, 0.0), axis=1, keepdims=True)
         allowed = (col <= row) & (key_doc == row_doc)
-        bias_ref[b] = jnp.where(allowed, 0.0, -jnp.inf)
+        bias_ref[b * block : (b + 1) * block] = jnp.where(allowed, 0.0, -jnp.inf)
 
     me = lax.axis_index("pool")
     first = start_ref[...].astype(jnp.float32)
@@ -156,80 +176,96 @@
     cell = grid((slots, cap))[1].astype(jnp.float32)
     seg_ref[...] = jnp.where((cell >= low) & (cell < high), 0.0, -jnp.inf)
 
-    copies["k", 0].wait()
-    copies["q"].wait()
-    copies["v", 0].wait()
-    items = [(0, b) for b in range(head_items)]
-    attend(items, group, window, q_ref, k_ref, v_ref, bias_ref, s_ref, p_ref, o_ref)
+    taken = ("q", ("k", 0), ("v", 0))
+    for name in taken:
+        copies[name].wait()
+    attend(items, group, q_ref, k_ref, v_ref, bias_ref, s_ref, p_ref, o_ref)
     for name, copy in copies.items():
-        if name not in ("doc", "start", "len", "q", ("k", 0), ("v", 0)):
+        if name not in taken:
             copy.wait()
 
 
-def late_kernel(group, window, head_items, *refs):
-    (q_ref, k_ref, v_ref, bias_ref, _, q_hbm, k_hbm, v_hbm) = refs[:8]
-    (o_ref, q2_ref, k2_ref, v2_ref, s_ref, p_ref, sems) = refs[8:]
-    near, rows, width = q_ref.shape
-    blocks = rows // ROW_BLOCK
+def late_kernel(near, group, items, *refs):
+    bias_ref = refs[4]
+    q_hbm, k_hbm, v_hbm, q_ref, k_ref, v_ref, o_ref, s_ref, p_ref, sems = refs[5:]
+    heads, _, width = q_ref.shape
+    copies, waited = {}, set()
+    for i in range(near, heads):
+        lanes = slice(i * HEAD_DIM, (i + 1) * HEAD_DIM)
+        cols = slice(i * width, (i + 1) * width)
+        copies[i] = [
+            pltpu.make_async_copy(src, dst, sems.at[3 * (i - near) + j])
+            for j, (src, dst) in enumerate(
+                (
+                    (q_hbm.at[:, cols], q_ref.at[i]),
+                    (k_hbm.at[:, lanes], k_ref.at[i]),
+                    (v_hbm.at[:, lanes], v_ref.at[i]),
+                )
+            )
+        ]
+        for copy in copies[i]:
+            copy.start()
+
+    def ready(item):
+        head = item[0]
+        if head in copies and head not in waited:
+            waited.add(head)
+            for copy in copies[head]:
+                copy.wait()
+
+    attend(items, group, q_ref, k_ref, v_ref, bias_ref, s_ref, p_ref, o_ref, ready)
+    for head in copies:
+        ready((head,))
+
+
+def last_kernel(group, items, *refs):
+    (q_ref, k_ref, v_ref, _, bias_ref) = refs[:5]
+    (o_ref, out_hbm, s_ref, p_ref, sems) = refs[5:]
+    heads, rows, width = o_ref.shape
     copies = []
-    for i in range(q2_ref.shape[0]):
-        lanes = slice((near + i) * HEAD_DIM, (near + i + 1) * HEAD_DIM)
-        cols = slice((near + i) * width, (near + i + 1) * width)
-        for src, dst in (
-            (q_hbm.at[:, cols], q2_ref.at[i]),
-            (k_hbm.at[:, lanes], k2_ref.at[i]),
-            (v_hbm.at[:, lanes], v2_ref.at[i]),
-        ):
-            copies.append(pltpu.make_async_copy(src, dst, sems.at[len(copies)]))
+
+    def store(head, lo, hi):
+        if lo < hi:
+            cols = slice(head * width, (head + 1) * width)
+            copies.append(
+                pltpu.make_async_copy(
+                    o_ref.at[head, lo:hi], out_hbm.at[lo:hi, cols], sems.at[len(copies)]
+                )
+            )
             copies[-1].start()
-    items = [(head, b) for head in range(near) for b in range(blocks)][head_items:]
-    attend(items, group, window, q_ref, k_ref, v_ref, bias_ref, s_ref, p_ref, o_ref)
+
+    stored = {}
+    for head in range(heads):
+        mine = [item for item in items if item[0] == head]
+        stored[head] = mine[0][1] if mine else rows
+        store(head, 0, stored[head])
+
+    def finished(item):
+        head, row, count = item[:3]
+        left = [x for x in items if x[0] == head and x[1] > row]
+        if len(left) in (0, 4):
+            store(head, stored[head], row + count)
+            stored[head] = row + count
+
+    attend(items, group, q_ref, k_ref, v_ref, bias_ref, s_ref, p_ref, o_ref, finished=finished)
     for copy in copies:
         copy.wait()
 
 
-def last_kernel(group, window, *refs):
-    (done_ref, q_ref, k_ref, v_ref, bias_ref, out_hbm) = refs[:6]
-    (o_ref, s_ref, p_ref, sems) = refs[6:]
-    near = done_ref.shape[0]
-    far, rows, width = q_ref.shape
-    blocks = rows // ROW_BLOCK
-    cut = blocks // 2
-    copies = []
-
-    def store(src, dst):
-        copies.append(pltpu.make_async_copy(src, dst, sems.at[len(copies)]))
-        copies[-1].start()
-
-    for i in range(near):
-        store(done_ref.at[i], out_hbm.at[:, i * width : (i + 1) * width])
-
-    def finished(head, b):
-        if b + 1 in (cut, blocks):
-            span = slice(0, cut * ROW_BLOCK) if b + 1 == cut else slice(cut * ROW_BLOCK, rows)
-            cols = slice((near + head) * width, (near + head + 1) * width)
-            store(o_ref.at[head, span], out_hbm.at[span, cols])
-
-    items = [(head, b) for head in range(far) for b in range(blocks)]
-    attend(items, group, window, q_ref, k_ref, v_ref, bias_ref, s_ref, p_ref, o_ref,
-           finished)
-    for copy in copies:
-        copy.wait()
-
-
 def pipeline_scratch(group, window):
-    stacked = group * ROW_BLOCK
+    stacked = 2 * group * ROW_BLOCK
     return [
         pltpu.VMEM((2, stacked, window), jnp.float32),
         pltpu.VMEM((2, window // HEAD_DIM, stacked, HEAD_DIM), jnp.bfloat16),
     ]
 
 
-def cost(group, rows, window, heads):
-    return pl.CostEstimate(
-        flops=4 * heads * group * rows * window * HEAD_DIM,
-        bytes_accessed=4 * rows * group * HEAD_DIM * heads,
-        transcendentals=0,
+def kernel_options(items, group, name):
+    flops = sum(4 * group * item[2] * item[4] * HEAD_DIM for item in items)
+    return dict(
+        cost_estimate=pl.CostEstimate(flops=flops, bytes_accessed=1 << 20, transcendentals=0),
+        compiler_params=pltpu.CompilerParams(vmem_limit_bytes=24 << 20),
+        name=name,
     )
 
 
@@ -237,101 +273,88 @@
     return tuple(pltpu.with_memory_space_constraint(x, pltpu.HBM) for x in arrays)
 
 
-def early_part(n, tp, near, group, window, home_rows, head_items, doc_ids, query, key, value,
-               start, length, cache_keys, cache_values):
+def early_part(n, tp, near, group, window, home_rows, items, small, query, key, value,
+               cache_keys, cache_values):
     rows, width = query.shape[0], group * HEAD_DIM
+    heads = key.shape[1] // HEAD_DIM
     slots = 2 * home_rows
-    requests = start.shape[0]
+    requests = small[1].shape[1]
     bf16, f32 = jnp.bfloat16, jnp.float32
     out_shape = [
-        jax.ShapeDtypeStruct((near, rows, width), bf16),
-        jax.ShapeDtypeStruct((near, rows, width), bf16),
-        jax.ShapeDtypeStruct((near, rows, HEAD_DIM), bf16),
-        jax.ShapeDtypeStruct((near, rows, HEAD_DIM), bf16),
-        jax.ShapeDtypeStruct((rows // ROW_BLOCK, ROW_BLOCK, window), f32),
+        jax.ShapeDtypeStruct((heads, rows, width), bf16),
+        jax.ShapeDtypeStruct((heads, rows, width), bf16),
+        jax.ShapeDtypeStruct((heads, rows, HEAD_DIM), bf16),
+        jax.ShapeDtypeStruct((heads, rows, HEAD_DIM), bf16),
+        jax.ShapeDtypeStruct((rows, window), f32),
         jax.ShapeDtypeStruct(cache_keys.shape, bf16),
         jax.ShapeDtypeStruct(cache_values.shape, bf16),
         jax.ShapeDtypeStruct((slots, n * home_rows), bf16),
         jax.ShapeDtypeStruct((slots, cache_keys.shape[0]), f32),
         jax.ShapeDtypeStruct((requests, n * slots), bf16),
     ]
-    operands = (doc_ids, query, key, value, start.reshape(1, -1), length.reshape(1, -1),
-                cache_keys, cache_values)
     return pl.pallas_call(
-        functools.partial(early_kernel, n, tp, group, window, home_rows, slots, head_items),
-        in_specs=[HBM] * len(operands),
+        functools.partial(early_kernel, n, tp, near, group, window, home_rows, slots, items),
+        in_specs=[VMEM] * 3 + [HBM] * 5,
         out_specs=[VMEM] * len(out_shape),
         out_shape=out_shape,
         scratch_shapes=[
-            pltpu.VMEM(doc_ids.shape, jnp.int32),
-            pltpu.VMEM((1, requests), jnp.int32),
-            pltpu.VMEM((1, requests), jnp.int32),
             *pipeline_scratch(group, window),
-            pltpu.SemaphoreType.DMA((6 + 3 * near,)),
+            pltpu.SemaphoreType.DMA((3 + 3 * near,)),
         ],
-        cost_estimate=cost(group, rows, window, near),
-        compiler_params=pltpu.CompilerParams(vmem_limit_bytes=24 << 20),
-        name="early",
-    )(*in_hbm(*operands))
-
-
-def late_part(far, group, window, head_items, done, q, k, v, bias, query, key, value):
-    near, rows, width = q.shape
+        **kernel_options(items, group, "early"),
+    )(*small, *in_hbm(query, key, value, cache_keys, cache_values))
+
+
+def late_part(near, group, window, items, q, k, v, done, bias, query, key, value):
+    held = (q, k, v, done)
     return pl.pallas_call(
-        functools.partial(late_kernel, group, window, head_items),
+        functools.partial(late_kernel, near, group, items),
         in_specs=[VMEM] * 5 + [HBM] * 3,
         out_specs=[VMEM] * 4,
+        out_shape=[jax.ShapeDtypeStruct(x.shape, x.dtype) for x in held],
+        scratch_shapes=[
+            *pipeline_scratch(group, window),
+            pltpu.SemaphoreType.DMA((3 * (q.shape[0] - near),)),
+        ],
+        input_output_aliases={0: 0, 1: 1, 2: 2, 3: 3},
+        **kernel_options(items, group, "late"),
+    )(*held, bias, *in_hbm(query, key, value))
+
+
+def last_part(group, window, items, shape, q, k, v, done, bias):
+    return pl.pallas_call(
+        functools.partial(last_kernel, group, items),
+        in_specs=[VMEM] * 5,
+        out_specs=[VMEM, HBM],
         out_shape=[
             jax.ShapeDtypeStruct(done.shape, done.dtype),
-            jax.ShapeDtypeStruct((far, rows, width), jnp.bfloat16),
-            jax.ShapeDtypeStruct((far, rows, HEAD_DIM), jnp.bfloat16),
-            jax.ShapeDtypeStruct((far, rows, HEAD_DIM), jnp.bfloat16),
+            jax.ShapeDtypeStruct(shape, done.dtype),
         ],
         scratch_shapes=[
             *pipeline_scratch(group, window),
-            pltpu.SemaphoreType.DMA((3 * far,)),
+            pltpu.SemaphoreType.DMA((3 * done.shape[0],)),
         ],
-        input_output_aliases={4: 0},
-        cost_estimate=cost(group, rows, window, near),
-        compiler_params=pltpu.CompilerParams(vmem_limit_bytes=24 << 20),
-        name="late",
-    )(q, k, v, bias, done, *in_hbm(query, key, value))
-
-
-def last_part(group, window, shape, done, q, k, v, bias):
-    far, rows, width = q.shape
-    return pl.pallas_call(
-        functools.partial(last_kernel, group, window),
-        in_specs=[VMEM] * 5,
-        out_specs=HBM,
-        out_shape=jax.ShapeDtypeStruct(shape, jnp.bfloat16),
-        scratch_shapes=[
-            pltpu.VMEM((far, rows, width), jnp.bfloat16),
-            *pipeline_scratch(group, window),
-            pltpu.SemaphoreType.DMA((done.shape[0] + 2 * far,)),
-        ],
-        cost_estimate=cost(group, rows, window, far),
-        compiler_params=pltpu.CompilerParams(vmem_limit_bytes=24 << 20),
-        name="last",
-    )(done, q, k, v, bias)
+        input_output_aliases={3: 0},
+        **kernel_options(items, group, "last"),
+    )(q, k, v, done, bias)[1]
 
 
 def xor_plan(n):
     return n & (n - 1) == 0 and 2 <= n <= 8
 
 
-def far_order(n, name):
+def far_order(n):
     order = list(range(n - 2, 0, -2))
-    if name == "pooled" and len(order) == 3:
+    if len(order) == 3:
         order = [order[1], order[0], order[2]]
     return order
 
 
-def spread(x, n, name):
+def spread(x, n):
     if not xor_plan(n):
         return [lax.all_gather(x, "pool", axis=0, tiled=True)]
     pieces = {0: x}
-    for d in far_order(n, name):
+    for d in far_order(n):
         pieces[d] = lax.ppermute(x, "pool", [(i, i ^ d) for i in range(n)])
     for d in range(0, n, 2):
         pieces[d + 1] = lax.ppermute(
@@ -344,22 +367,27 @@
     return index ^ me if xor_plan(n) else index
 
 
-def pack_kernel(q_ref, k_ref, v_ref, o_ref):
+def pack_kernel(q_ref, k_ref, v_ref, *refs):
+    small, (o_ref, *staged) = refs[:3], refs[3:]
     dq, dk = q_ref.shape[1], k_ref.shape[1]
     o_ref[:, :dq] = q_ref[...]
     o_ref[:, dq : dq + dk] = k_ref[...]
     o_ref[:, dq + dk :] = v_ref[...]
-
-
-def pack(q, k, v):
+    for src, dst in zip(small, staged):
+        dst[...] = src[...]
+
+
+def pack(q, k, v, *small):
     shape = (q.shape[0], q.shape[1] + k.shape[1] + v.shape[1])
-    return pl.pallas_call(
+    packed, *staged = pl.pallas_call(
         pack_kernel,
-        in_specs=[VMEM] * 3,
-        out_specs=VMEM,
-        out_shape=pltpu.VMEM(shape, q.dtype),
+        in_specs=[VMEM] * 6,
+        out_specs=[VMEM] * 4,
+        out_shape=[pltpu.VMEM(shape, q.dtype)]
+        + [pltpu.VMEM(x.shape, x.dtype) for x in small],
         name="pack",
-    )(q, k, v)
+    )(q, k, v, *small)
+    return packed, staged
 
 
 def decode_kernel(kv_local, group, count, *refs):
@@ -509,21 +537,27 @@
     kv_local = home_key.shape[1] // HEAD_DIM
     group = home_query.shape[1] // HEAD_DIM // kv_local
     window = min(rows, rows // 2 + ROW_BLOCK)
-    far = max(1, kv_local // 4)
-    near = kv_local - far
-    head_items = (rows // ROW_BLOCK) * 3 // 7
+    near = max(1, kv_local // 2)
+    early, late, last = shares(kv_local, rows, group, window)
     prompt = (prompt_query, prompt_key, prompt_value)
 
-    homes = spread(pack(home_query, home_key, home_value), n, "home")
-    done, q1, k1, v1, bias, ck, cv, pick, seg, gather = early_part(
-        n, tp, near, group, window, home_rows, head_items, doc_ids, *prompt, cache_start,
-        cache_len, cache_keys, cache_values,
+    packed, small = pack(
+        home_query,
+        home_key,
+        home_value,
+        doc_ids,
+        cache_start.reshape(1, -1),
+        cache_len.reshape(1, -1),
+    )
+    homes = spread(packed, n)
+    done, q, k, v, bias, ck, cv, pick, seg, gather = early_part(
+        n, tp, near, group, window, home_rows, early, small, *prompt, cache_keys, cache_values
     )
     slot_out = decode(homes, pick, seg, ck, cv, group)
-    pooled = spread(slot_out, n, "pooled")
-    done, q2, k2, v2 = late_part(far, group, window, head_items, done, q1, k1, v1, bias, *prompt)
+    pooled = spread(slot_out, n)
+    q, k, v, done = late_part(near, group, window, late, q, k, v, done, bias, *prompt)
     partial = project(pooled, gather, out_weight, tp)
-    prompt_out = last_part(group, window, prompt_query.shape, done, q2, k2, v2, bias)
+    prompt_out = last_part(group, window, last, prompt_query.shape, q, k, v, done, bias)
     if tp == 2:
         send, keep = partial
         other = lax.ppermute(send, "tp", [(0, 1), (1, 0)])

time: 36.3 us -> 35.5 us (0.978)
  Pallas kernels: 13.3 us -> 12.6 us
    pallas_call x4, Pallas kernels: 10.3 us -> 9.62 us  [the longest x1 3.14 us: last_part(): pl.pallas_call(functools.partial(last_kernel, group, items), in_specs=[VM...]
  transfers between devices with their start and end apart: 15 -> 15, of which waited for: 5 -> 4; matrix products, arithmetic and copies ran while one was open for 0% -> 0% of each run, Pallas kernels for 26% -> 25%
where the time goes in v5:
time: 35.5 us; the launch traced here: 35.3 us
  Pallas kernels  12.6 us (35%)
  starting transfers between devices  11.8 us (33%)
  waiting for transfers between devices  9.51 us (27%)
  between operations  0.78 us (2%)
  other arithmetic  0.63 us (2%)
    ppermute x6, waiting for transfers between devices, spread(): pieces[d] = lax.ppermute(x, 'pool', [(i, i ^ d) for i in range(n)])  9.48 us
    ppermute x6, starting transfers between devices, spread(): pieces[d] = lax.ppermute(x, 'pool', [(i, i ^ d) for i in range(n)])  9.25 us
    pallas_call x1, Pallas kernels, last_part(): pl.pallas_call(functools.partial(last_kernel, group, items), in_specs=[VM...  3.14 us
    pallas_call x1, Pallas kernels, late_part(): pl.pallas_call(functools.partial(late_kernel, near, group, items), in_spe...  3.08 us
    pallas_call x1, Pallas kernels, early_part(): pl.pallas_call(functools.partial(early_kernel, n, tp, near, group, window...  2.61 us
    pallas_call x1, Pallas kernels, project(): pl.pallas_call(functools.partial(project_kernel, len(pieces), tp), in_spe...  2.13 us
    ppermute x1, starting transfers between devices, local(): other = lax.ppermute(send, 'tp', [(0, 1), (1, 0)])  1.52 us
    ppermute x8, starting transfers between devices, spread(): lax.ppermute(pieces[d], 'pool', [(i, i ^ 1) for i in range(n)])  1.07 us
  transfers between devices with their start and end apart: 15, of which 4 were waited for; matrix products, arithmetic and copies ran while one was open for 0% of the time, Pallas kernels for 25%

profile of v5, /device:TPU:0, one launch (start us, length us, event | category | flops | bytes accessed | tf_op | source)
XLA Modules:
  0.0 35.3 jit_solution(6096629489181373987)
XLA Ops:
  0.6 0.8 %pack.1 = (bf16[4,5120]{1,0:T(4,128)(2,1)S(1)}, s32[1,448]{1,0:T(1,128)S(1)}, s32[1,32]{1,0:T(1,128)S(1)}, s32[1,32]{1,0:T(1,128)S(1)}) custom-call(bf16[4,4096]{1,0:T(4,128)(2,1)} %q_ref.1, bf16[4,512]{1,0:T(4,128)(2,1)} %k_ref.1, bf16[4,512]{1,0:T(4,128)(2,1)} %v_ref.1, s32[1,448]{1,0:T(1,128)} %refs_0_.1, s32[1,32]{1,0:T(1,128)} %bitcast.4, s32[1,32]{1,0:T(1,128)} %bitcast.5), custom_call_target="tpu_custom_call" | custom-call | tf_op jit(solution)/shard_map/pack/pallas_call | solution.py:382
  1.4 3.1 %collective-permute-start.1 = (bf16[4,5120]{1,0:T(4,128)(2,1)S(1)}, bf16[4,5120]{1,0:T(4,128)(2,1)S(1)}, u32[]{:S(2)}, u32[]{:S(2)}) collective-permute-start(bf16[4,5120]{1,0:T(4,128)(2,1)S(1)} %get-tuple-element.36.refs_0_), channel_id=1, source_target_pairs={{0,4},{2,6},{4,0},{6,2},{8,12},{10,14},{12,8},{14,10},{1,5},{3,7},... | collective-permute-start | bytes 122888 | tf_op jit(solution)/shard_map/ppermute | solution.py:358
  4.6 2.6 %collective-permute-start.3 = (bf16[4,5120]{1,0:T(4,128)(2,1)S(1)}, bf16[4,5120]{1,0:T(4,128)(2,1)S(1)}, u32[]{:S(2)}, u32[]{:S(2)}) collective-permute-start(bf16[4,5120]{1,0:T(4,128)(2,1)S(1)} %get-tuple-element.36.refs_0_), channel_id=1, source_target_pairs={{0,8},{2,10},{4,12},{6,14},{8,0},{10,2},{12,4},{14,6},{1,9},{3,11}... | collective-permute-start | bytes 122888 | tf_op jit(solution)/shard_map/ppermute | solution.py:358
  7.1 0.0 collective-permute-start.5
  7.1 0.0 collective-permute-start
  7.1 0.0 collective-permute-done.1.refs_2_
  7.2 0.5 %collective-permute-start.2 = (bf16[4,5120]{1,0:T(4,128)(2,1)S(1)}, bf16[4,5120]{1,0:T(4,128)(2,1)S(1)}, u32[]{:S(2)}, u32[]{:S(2)}) collective-permute-start(bf16[4,5120]{1,0:T(4,128)(2,1)S(1)} %collective-permute-done.1.refs_2_), channel_id=1, source_target_pairs={{0,2},{2,0},{4,6},{6,4},{8,10},{10,8},{12,14},{14,12},{1,3},{3,1},... | collective-permute-start | bytes 122888 | tf_op jit(solution)/shard_map/ppermute | solution.py:360
  7.7 2.6 %collective-permute-done.3.refs_4_ = bf16[4,5120]{1,0:T(4,128)(2,1)S(1)} collective-permute-done((bf16[4,5120]{1,0:T(4,128)(2,1)S(1)}, bf16[4,5120]{1,0:T(4,128)(2,1)S(1)}, u32[]{:S(2)}, u32[]{:S(2)}) %collective-permute-start.3) | collective-permute-done | bytes 40992 | tf_op jit(solution)/shard_map/ppermute | solution.py:358
  10.2 0.0 collective-permute-start.4
  10.2 2.7 %collective-permute-done.5.refs_6_ = bf16[4,5120]{1,0:T(4,128)(2,1)S(1)} collective-permute-done((bf16[4,5120]{1,0:T(4,128)(2,1)S(1)}, bf16[4,5120]{1,0:T(4,128)(2,1)S(1)}, u32[]{:S(2)}, u32[]{:S(2)}) %collective-permute-start.5) | collective-permute-done | bytes 40992 | tf_op jit(solution)/shard_map/ppermute | solution.py:358
  12.9 0.0 collective-permute-start.6
  12.9 2.6 %early.1 = (bf16[4,448,1024]{2,1,0:T(8,128)(2,1)S(1)}, bf16[4,448,1024]{2,1,0:T(8,128)(2,1)S(1)}, bf16[4,448,128]{2,1,0:T(8,128)(2,1)S(1)}, bf16[4,448,128]{2,1,...) custom-call(s32[1,448]{1,0:T(1,128)S(1)} %get-tuple-element.23.refs_, ...), custom_call_target="tpu_custom_call" | custom-call | flops 67108864 | bytes 1048576 | tf_op jit(solution)/shard_map/early/pallas_call | solution.py:295
  15.6 0.0 collective-permute-done.refs_1_
  15.6 0.0 collective-permute-done.2.refs_3_
  15.6 0.0 collective-permute-done.4.refs_5_
  15.6 0.0 collective-permute-done.6.refs_7_
  15.6 0.0 slice-start
  15.6 0.8 %decode.1.refs_0_ = bf16[8,4096]{1,0:T(8,128)(2,1)S(1)} custom-call(bf16[4,5120]{1,0:T(4,128)(2,1)S(1)} %get-tuple-element.36.refs_0_, bf16[4,5120]{1,0:T(4,128)(2,1)S(1)} %collective-permute-done.refs_1_, bf16[4,5120]{1,0:T(4,128)(2,1)S(1)} %collective-permute-done.1.refs_2_, bf16[4,5120]{1,0:T(4,128)(2,1)S(1)} %collective-permute-done.2.refs_3_, ...), custom_call_target="tpu_custom_call" | custom-call | flops 1000000000 | bytes 1048576 | tf_op jit(solution)/shard_map/decode/pallas_call | solution.py:457
  16.4 0.1 collective-permute-start.10
  16.5 1.4 %collective-permute-start.12 = (bf16[8,4096]{1,0:T(8,128)(2,1)S(1)}, bf16[8,4096]{1,0:T(8,128)(2,1)S(1)}, u32[]{:S(2)}, u32[]{:S(2)}) collective-permute-start(bf16[8,4096]{1,0:T(8,128)(2,1)S(1)} %decode.1.refs_0_), channel_id=1, source_target_pairs={{0,12},{2,14},{4,8},{6,10},{8,4},{10,6},{12,0},{14,2},{1,13},{3,15... | collective-permute-start | bytes 196616 | tf_op jit(solution)/shard_map/ppermute | solution.py:358
  17.9 2.0 %collective-permute-start.8 = (bf16[8,4096]{1,0:T(8,128)(2,1)S(1)}, bf16[8,4096]{1,0:T(8,128)(2,1)S(1)}, u32[]{:S(2)}, u32[]{:S(2)}) collective-permute-start(bf16[8,4096]{1,0:T(8,128)(2,1)S(1)} %decode.1.refs_0_), channel_id=1, source_target_pairs={{0,4},{2,6},{4,0},{6,2},{8,12},{10,14},{12,8},{14,10},{1,5},{3,7},... | collective-permute-start | bytes 196616 | tf_op jit(solution)/shard_map/ppermute | solution.py:358
  20.0 0.0 collective-permute-start.7
  20.0 3.8 %collective-permute-done.10.refs_4_ = bf16[8,4096]{1,0:T(8,128)(2,1)S(1)} collective-permute-done((bf16[8,4096]{1,0:T(8,128)(2,1)S(1)}, bf16[8,4096]{1,0:T(8,128)(2,1)S(1)}, u32[]{:S(2)}, u32[]{:S(2)}) %collective-permute-start.10) | collective-permute-done | bytes 65568 | tf_op jit(solution)/shard_map/ppermute | solution.py:358
  23.7 0.0 collective-permute-start.11
  23.8 0.0 collective-permute-done.12.refs_6_
  23.8 0.5 %collective-permute-start.13 = (bf16[8,4096]{1,0:T(8,128)(2,1)S(1)}, bf16[8,4096]{1,0:T(8,128)(2,1)S(1)}, u32[]{:S(2)}, u32[]{:S(2)}) collective-permute-start(bf16[8,4096]{1,0:T(8,128)(2,1)S(1)} %collective-permute-done.12.refs_6_), channel_id=1, source_target_pairs={{0,2},{2,0},{4,6},{6,4},{8,10},{10,8},{12,14},{14,12},{1,3},{3,1},... | collective-permute-start | bytes 196616 | tf_op jit(solution)/shard_map/ppermute | solution.py:360
  24.3 0.4 %collective-permute-done.8.refs_2_ = bf16[8,4096]{1,0:T(8,128)(2,1)S(1)} collective-permute-done((bf16[8,4096]{1,0:T(8,128)(2,1)S(1)}, bf16[8,4096]{1,0:T(8,128)(2,1)S(1)}, u32[]{:S(2)}, u32[]{:S(2)}) %collective-permute-start.8) | collective-permute-done | bytes 65568 | tf_op jit(solution)/shard_map/ppermute | solution.py:358
  24.7 0.0 collective-permute-start.9
  24.7 0.0 slice-start.1
  24.7 3.1 %late.1 = (bf16[4,448,1024]{2,1,0:T(8,128)(2,1)S(1)}, bf16[4,448,128]{2,1,0:T(8,128)(2,1)S(1)}, bf16[4,448,128]{2,1,0:T(8,128)(2,1)S(1)}, bf16[4,448,1024]{2,1,0:T(8,128)(2,1)S(1)}) custom-call(bf16[4,448,1024]{2,1,0:T(8,128)(2,1)S(1)} %get-tuple-element.26.refs_0_, ...), custom_call_target="tpu_custom_call", output_to_operand_aliasing={{0}: (0, {}), {1}: (1, {}), {2}: (2, {}), {3}: (3, {})} | custom-call | flops 872415232 | bytes 1048576 | tf_op jit(solution)/shard_map/late/pallas_call | solution.py:310
  27.8 0.0 collective-permute-done.7.refs_1_
  27.8 0.0 collective-permute-done.11.refs_5_
  27.8 0.0 collective-permute-done.13.refs_7_
  27.8 0.0 collective-permute-done.9.refs_3_
  27.9 0.0 slice-done
  27.9 0.0 slice-done.1
  27.9 2.1 %project.1 = (bf16[16,1024]{1,0:T(8,128)(2,1)S(1)}, f32[16,1024]{1,0:T(8,128)S(1)}) custom-call(bf16[8,4096]{1,0:T(8,128)(2,1)S(1)} %decode.1.refs_0_, bf16[8,4096]{1,0:T(8,128)(2,1)S(1)} %collective-permute-done.7.refs_1_, bf16[8,4096]{1,0:T(8,128)(2,1)S(1)} %collective-permute-done.8.refs_2_, bf16[8,4096]{1,0:T(8,128)(2,1)S(1)} %collective-permute-done.9.refs_3_, ...), custom_call_target="tpu_custom_call" | custom-call | flops 1000000000 | bytes 8388608 | tf_op jit(solution)/shard_map/project/pallas_call | solution.py:506
  30.0 1.5 %collective-permute-start.14 = (bf16[16,1024]{1,0:T(8,128)(2,1)S(1)}, bf16[16,1024]{1,0:T(8,128)(2,1)S(1)}, u32[]{:S(2)}, u32[]{:S(2)}) collective-permute-start(bf16[16,1024]{1,0:T(8,128)(2,1)S(1)} %get-tuple-element.43), channel_id=1, source_target_pairs={{0,1},{1,0},{2,3},{3,2},{4,5},{5,4},{6,7},{7,6},{8,9},{9,8},{10,11... | collective-permute-start | bytes 98312 | tf_op jit(solution)/shard_map/ppermute | solution.py:563
  31.5 3.1 %last.1 = (bf16[4,448,1024]{2,1,0:T(8,128)(2,1)S(1)}, bf16[448,4096]{1,0:T(8,128)(2,1)}) custom-call(bf16[4,448,1024]{2,1,0:T(8,128)(2,1)S(1)} %get-tuple-element.31.refs_0_, bf16[4,448,128]{2,1,0:T(8,128)(2,1)S(1)} %get-tuple-element.32.refs_1_, bf16[4,448,128]{2,1,0:T(8,128)(2,1)S(1)} %get-tuple-element.33.refs_2_, ...), custom_call_target="tpu_custom_call", output_to_operand_aliasing={{0}: (3, {})} | custom-call | flops 671088640 | bytes 1048576 | tf_op jit(solution)/shard_map/last/pallas_call | solution.py:325
  34.7 0.0 collective-permute-done.14
  34.7 0.6 %add_convert_fusion = bf16[16,1024]{1,0:T(8,128)(2,1)} fusion(f32[16,1024]{1,0:T(8,128)S(1)} %get-tuple-element.42, bf16[16,1024]{1,0:T(8,128)(2,1)S(1)} %collective-permute-done.14), kind=kLoop, calls=%fused_computation | loop fusion | flops 49152 | bytes 131072 | tf_op jit(solution)/shard_map/convert_element_type | solution.py:564
  (1 shorter events, 0.0 us)
Async XLA Ops:
  1.4 5.7 %collective-permute-start.1 = (bf16[4,5120]{1,0:T(4,128)(2,1)S(1)}, bf16[4,5120]{1,0:T(4,128)(2,1)S(1)}, u32[]{:S(2)}, u32[]{:S(2)}) collective-permute-start(bf16[4,5120]{1,0:T(4,128)(2,1)S(1)} %get-tuple-element.36.refs_0_), channel_id=1, source_target_pairs={{0,4},{2,6},{4,0},{6,2},{8,12},{10,14},{12,8},{14,10},{1,5},{3,7},... | collective-permute-start | bytes 122888 | tf_op jit(solution)/shard_map/ppermute | solution.py:358
  4.6 5.7 %collective-permute-start.3 = (bf16[4,5120]{1,0:T(4,128)(2,1)S(1)}, bf16[4,5120]{1,0:T(4,128)(2,1)S(1)}, u32[]{:S(2)}, u32[]{:S(2)}) collective-permute-start(bf16[4,5120]{1,0:T(4,128)(2,1)S(1)} %get-tuple-element.36.refs_0_), channel_id=1, source_target_pairs={{0,8},{2,10},{4,12},{6,14},{8,0},{10,2},{12,4},{14,6},{1,9},{3,11}... | collective-permute-start | bytes 122888 | tf_op jit(solution)/shard_map/ppermute | solution.py:358
  7.1 5.8 %collective-permute-start.5 = (bf16[4,5120]{1,0:T(4,128)(2,1)S(1)}, bf16[4,5120]{1,0:T(4,128)(2,1)S(1)}, u32[]{:S(2)}, u32[]{:S(2)}) collective-permute-start(bf16[4,5120]{1,0:T(4,128)(2,1)S(1)} %get-tuple-element.36.refs_0_), channel_id=1, source_target_pairs={{0,12},{2,14},{4,8},{6,10},{8,4},{10,6},{12,0},{14,2},{1,13},{3,15... | collective-permute-start | bytes 122888 | tf_op jit(solution)/shard_map/ppermute | solution.py:358
  7.1 8.4 %collective-permute-start = (bf16[4,5120]{1,0:T(4,128)(2,1)S(1)}, bf16[4,5120]{1,0:T(4,128)(2,1)S(1)}, u32[]{:S(2)}, u32[]{:S(2)}) collective-permute-start(bf16[4,5120]{1,0:T(4,128)(2,1)S(1)} %get-tuple-element.36.refs_0_), channel_id=1, source_target_pairs={{0,2},{2,0},{4,6},{6,4},{8,10},{10,8},{12,14},{14,12},{1,3},{3,1},... | collective-permute-start | bytes 122888 | tf_op jit(solution)/shard_map/ppermute | solution.py:360
  7.2 8.4 %collective-permute-start.2 = (bf16[4,5120]{1,0:T(4,128)(2,1)S(1)}, bf16[4,5120]{1,0:T(4,128)(2,1)S(1)}, u32[]{:S(2)}, u32[]{:S(2)}) collective-permute-start(bf16[4,5120]{1,0:T(4,128)(2,1)S(1)} %collective-permute-done.1.refs_2_), channel_id=1, source_target_pairs={{0,2},{2,0},{4,6},{6,4},{8,10},{10,8},{12,14},{14,12},{1,3},{3,1},... | collective-permute-start | bytes 122888 | tf_op jit(solution)/shard_map/ppermute | solution.py:360
  10.2 5.4 %collective-permute-start.4 = (bf16[4,5120]{1,0:T(4,128)(2,1)S(1)}, bf16[4,5120]{1,0:T(4,128)(2,1)S(1)}, u32[]{:S(2)}, u32[]{:S(2)}) collective-permute-start(bf16[4,5120]{1,0:T(4,128)(2,1)S(1)} %collective-permute-done.3.refs_4_), channel_id=1, source_target_pairs={{0,2},{2,0},{4,6},{6,4},{8,10},{10,8},{12,14},{14,12},{1,3},{3,1},... | collective-permute-start | bytes 122888 | tf_op jit(solution)/shard_map/ppermute | solution.py:360
  12.9 2.7 %collective-permute-start.6 = (bf16[4,5120]{1,0:T(4,128)(2,1)S(1)}, bf16[4,5120]{1,0:T(4,128)(2,1)S(1)}, u32[]{:S(2)}, u32[]{:S(2)}) collective-permute-start(bf16[4,5120]{1,0:T(4,128)(2,1)S(1)} %collective-permute-done.5.refs_6_), channel_id=1, source_target_pairs={{0,2},{2,0},{4,6},{6,4},{8,10},{10,8},{12,14},{14,12},{1,3},{3,1},... | collective-permute-start | bytes 122888 | tf_op jit(solution)/shard_map/ppermute | solution.py:360
  15.6 12.3 %slice-start = ((s8[8388608]{0:T(1024)(128)(4,1)}), s8[4194304]{0:T(1024)(128)(4,1)S(1)}, s32[]{:S(2)}) async-start(s8[8388608]{0:T(1024)(128)(4,1)} %bitcast.2), calls=%async_computation | async-start | bytes 8388608
  16.4 7.3 %collective-permute-start.10 = (bf16[8,4096]{1,0:T(8,128)(2,1)S(1)}, bf16[8,4096]{1,0:T(8,128)(2,1)S(1)}, u32[]{:S(2)}, u32[]{:S(2)}) collective-permute-start(bf16[8,4096]{1,0:T(8,128)(2,1)S(1)} %decode.1.refs_0_), channel_id=1, source_target_pairs={{0,8},{2,10},{4,12},{6,14},{8,0},{10,2},{12,4},{14,6},{1,9},{3,11}... | collective-permute-start | bytes 196616 | tf_op jit(solution)/shard_map/ppermute | solution.py:358
  16.5 7.3 %collective-permute-start.12 = (bf16[8,4096]{1,0:T(8,128)(2,1)S(1)}, bf16[8,4096]{1,0:T(8,128)(2,1)S(1)}, u32[]{:S(2)}, u32[]{:S(2)}) collective-permute-start(bf16[8,4096]{1,0:T(8,128)(2,1)S(1)} %decode.1.refs_0_), channel_id=1, source_target_pairs={{0,12},{2,14},{4,8},{6,10},{8,4},{10,6},{12,0},{14,2},{1,13},{3,15... | collective-permute-start | bytes 196616 | tf_op jit(solution)/shard_map/ppermute | solution.py:358
  17.9 6.8 %collective-permute-start.8 = (bf16[8,4096]{1,0:T(8,128)(2,1)S(1)}, bf16[8,4096]{1,0:T(8,128)(2,1)S(1)}, u32[]{:S(2)}, u32[]{:S(2)}) collective-permute-start(bf16[8,4096]{1,0:T(8,128)(2,1)S(1)} %decode.1.refs_0_), channel_id=1, source_target_pairs={{0,4},{2,6},{4,0},{6,2},{8,12},{10,14},{12,8},{14,10},{1,5},{3,7},... | collective-permute-start | bytes 196616 | tf_op jit(solution)/shard_map/ppermute | solution.py:358
  20.0 7.9 %collective-permute-start.7 = (bf16[8,4096]{1,0:T(8,128)(2,1)S(1)}, bf16[8,4096]{1,0:T(8,128)(2,1)S(1)}, u32[]{:S(2)}, u32[]{:S(2)}) collective-permute-start(bf16[8,4096]{1,0:T(8,128)(2,1)S(1)} %decode.1.refs_0_), channel_id=1, source_target_pairs={{0,2},{2,0},{4,6},{6,4},{8,10},{10,8},{12,14},{14,12},{1,3},{3,1},... | collective-permute-start | bytes 196616 | tf_op jit(solution)/shard_map/ppermute | solution.py:360
  23.7 4.1 %collective-permute-start.11 = (bf16[8,4096]{1,0:T(8,128)(2,1)S(1)}, bf16[8,4096]{1,0:T(8,128)(2,1)S(1)}, u32[]{:S(2)}, u32[]{:S(2)}) collective-permute-start(bf16[8,4096]{1,0:T(8,128)(2,1)S(1)} %collective-permute-done.10.refs_4_), channel_id=1, source_target_pairs={{0,2},{2,0},{4,6},{6,4},{8,10},{10,8},{12,14},{14,12},{1,3},{3,1},... | collective-permute-start | bytes 196616 | tf_op jit(solution)/shard_map/ppermute | solution.py:360
  23.8 4.1 %collective-permute-start.13 = (bf16[8,4096]{1,0:T(8,128)(2,1)S(1)}, bf16[8,4096]{1,0:T(8,128)(2,1)S(1)}, u32[]{:S(2)}, u32[]{:S(2)}) collective-permute-start(bf16[8,4096]{1,0:T(8,128)(2,1)S(1)} %collective-permute-done.12.refs_6_), channel_id=1, source_target_pairs={{0,2},{2,0},{4,6},{6,4},{8,10},{10,8},{12,14},{14,12},{1,3},{3,1},... | collective-permute-start | bytes 196616 | tf_op jit(solution)/shard_map/ppermute | solution.py:360
  24.7 3.2 %collective-permute-start.9 = (bf16[8,4096]{1,0:T(8,128)(2,1)S(1)}, bf16[8,4096]{1,0:T(8,128)(2,1)S(1)}, u32[]{:S(2)}, u32[]{:S(2)}) collective-permute-start(bf16[8,4096]{1,0:T(8,128)(2,1)S(1)} %collective-permute-done.8.refs_2_), channel_id=1, source_target_pairs={{0,2},{2,0},{4,6},{6,4},{8,10},{10,8},{12,14},{14,12},{1,3},{3,1},... | collective-permute-start | bytes 196616 | tf_op jit(solution)/shard_map/ppermute | solution.py:360
  24.7 3.1 %slice-start.1 = ((s8[8388608]{0:T(1024)(128)(4,1)}), s8[4194304]{0:T(1024)(128)(4,1)S(1)}, s32[]{:S(2)}) async-start(s8[8388608]{0:T(1024)(128)(4,1)} %bitcast.2), calls=%async_computation.1 | async-start | bytes 8388608
  30.0 4.7 %collective-permute-start.14 = (bf16[16,1024]{1,0:T(8,128)(2,1)S(1)}, bf16[16,1024]{1,0:T(8,128)(2,1)S(1)}, u32[]{:S(2)}, u32[]{:S(2)}) collective-permute-start(bf16[16,1024]{1,0:T(8,128)(2,1)S(1)} %get-tuple-element.43), channel_id=1, source_target_pairs={{0,1},{1,0},{2,3},{3,2},{4,5},{5,4},{6,7},{7,6},{8,9},{9,8},{10,11... | collective-permute-start | bytes 98312 | tf_op jit(solution)/shard_map/ppermute | solution.py:563

commit v6 on v5

--- a/solution.py
+++ b/solution.py
@@ -11,7 +11,7 @@
 HEAD_DIM = 128
 LOG2E = 1.4426950408889634
 ROW_BLOCK = 32
-EARLY, LATE = 0.07, 0.55
+EARLY, LATE = 0.07, 0.69
 VMEM = pl.BlockSpec(memory_space=pltpu.VMEM)
 HBM = pl.BlockSpec(memory_space=pltpu.HBM)
 
@@ -187,7 +187,7 @@
 
 def late_kernel(near, group, items, *refs):
     bias_ref = refs[4]
-    q_hbm, k_hbm, v_hbm, q_ref, k_ref, v_ref, o_ref, s_ref, p_ref, sems = refs[5:]
+    q_hbm, k_hbm, v_hbm, w_hbm, q_ref, k_ref, v_ref, o_ref, w_ref, s_ref, p_ref, sems = refs[5:]
     heads, _, width = q_ref.shape
     copies, waited = {}, set()
     for i in range(near, heads):
@@ -205,6 +205,10 @@
         ]
         for copy in copies[i]:
             copy.start()
+    weight = pltpu.make_async_copy(
+        w_hbm.at[: w_ref.shape[0]], w_ref, sems.at[3 * (heads - near)]
+    )
+    weight.start()
 
     def ready(item):
         head = item[0]
@@ -216,6 +220,7 @@
     attend(items, group, q_ref, k_ref, v_ref, bias_ref, s_ref, p_ref, o_ref, ready)
     for head in copies:
         ready((head,))
+    weight.wait()
 
 
 def last_kernel(group, items, *refs):
@@ -305,20 +310,22 @@
     )(*small, *in_hbm(query, key, value, cache_keys, cache_values))
 
 
-def late_part(near, group, window, items, q, k, v, done, bias, query, key, value):
+def late_part(near, group, window, items, q, k, v, done, bias, query, key, value, weight):
     held = (q, k, v, done)
+    kept = weight.shape[0] // 4 * 3
     return pl.pallas_call(
         functools.partial(late_kernel, near, group, items),
-        in_specs=[VMEM] * 5 + [HBM] * 3,
-        out_specs=[VMEM] * 4,
-        out_shape=[jax.ShapeDtypeStruct(x.shape, x.dtype) for x in held],
+        in_specs=[VMEM] * 5 + [HBM] * 4,
+        out_specs=[VMEM] * 5,
+        out_shape=[jax.ShapeDtypeStruct(x.shape, x.dtype) for x in held]
+        + [jax.ShapeDtypeStruct((kept, weight.shape[1]), weight.dtype)],
         scratch_shapes=[
             *pipeline_scratch(group, window),
-            pltpu.SemaphoreType.DMA((3 * (q.shape[0] - near),)),
+            pltpu.SemaphoreType.DMA((3 * (q.shape[0] - near) + 1,)),
         ],
         input_output_aliases={0: 0, 1: 1, 2: 2, 3: 3},
         **kernel_options(items, group, "late"),
-    )(*held, bias, *in_hbm(query, key, value))
+    )(*held, bias, *in_hbm(query, key, value, weight))
 
 
 def last_part(group, window, items, shape, q, k, v, done, bias):
@@ -472,19 +479,26 @@
 
 def project_kernel(count, tp, *refs):
     pieces = refs[:count]
-    gather_ref, w_ref, *outs = refs[count:]
-    step = min(512, w_ref.shape[0])
+    gather_ref, w_ref, w_hbm, *outs = refs[count:]
+    *outs, rest_ref, sem = outs
+    kept = w_ref.shape[0]
+    rest = pltpu.make_async_copy(w_hbm.at[kept:], rest_ref, sem)
+    rest.start()
+    step = min(512, rest_ref.shape[0])
     total = None
-    for first in range(0, w_ref.shape[0], step):
+    for first in range(0, w_hbm.shape[0], step):
         cols = slice(first, first + step)
         if count == 1:
             rows = pieces[0][:, cols]
         else:
             rows = jnp.concatenate([p[:, cols] for p in pieces], axis=0)
         rows = jnp.dot(gather_ref[...], rows, preferred_element_type=jnp.float32)
-        part = jnp.dot(
-            rows.astype(jnp.bfloat16), w_ref[cols, :], preferred_element_type=jnp.float32
-        )
+        if first == kept:
+            rest.wait()
+        weight = (
+            w_ref[cols, :] if first < kept else rest_ref[first - kept : first - kept + step, :]
+        )
+        part = jnp.dot(rows.astype(jnp.bfloat16), weight, preferred_element_type=jnp.float32)
         total = part if total is None else total + part
     if tp == 2:
         half = total.shape[0] // 2
@@ -494,7 +508,7 @@
         outs[0][...] = total
 
 
-def project(pieces, gather, weight, tp):
+def project(pieces, gather, kept, weight, tp):
     requests, cols = gather.shape[0], weight.shape[1]
     if tp == 2:
         out_shape = [
@@ -505,15 +519,19 @@
         out_shape = [jax.ShapeDtypeStruct((requests, cols), jnp.float32)]
     return pl.pallas_call(
         functools.partial(project_kernel, len(pieces), tp),
-        in_specs=[VMEM] * (len(pieces) + 2),
+        in_specs=[VMEM] * (len(pieces) + 2) + [HBM],
         out_specs=[VMEM] * len(out_shape),
         out_shape=out_shape,
+        scratch_shapes=[
+            pltpu.VMEM((weight.shape[0] - kept.shape[0], cols), weight.dtype),
+            pltpu.SemaphoreType.DMA,
+        ],
         cost_estimate=pl.CostEstimate(
             flops=10**9, bytes_accessed=2 * weight.size, transcendentals=0
         ),
         compiler_params=pltpu.CompilerParams(vmem_limit_bytes=40 << 20),
         name="project",
-    )(*pieces, gather, weight)
+    )(*pieces, gather, kept, *in_hbm(weight))
 
 
 def local(
@@ -555,8 +573,10 @@
     )
     slot_out = decode(homes, pick, seg, ck, cv, group)
     pooled = spread(slot_out, n)
-    q, k, v, done = late_part(near, group, window, late, q, k, v, done, bias, *prompt)
-    partial = project(pooled, gather, out_weight, tp)
+    q, k, v, done, kept = late_part(
+        near, group, window, late, q, k, v, done, bias, *prompt, out_weight
+    )
+    partial = project(pooled, gather, kept, out_weight, tp)
     prompt_out = last_part(group, window, last, prompt_query.shape, q, k, v, done, bias)
     if tp == 2:
         send, keep = partial

time: 35.5 us -> 35.6 us (level)
  starting transfers between devices: 11.8 us -> 12.8 us
  waiting for transfers between devices: 9.51 us -> 8.56 us
    ppermute x6, waiting for transfers between devices: 9.48 us -> 8.47 us  [spread(): pieces[d] = lax.ppermute(x, 'pool', [(i, i ^ d) for i in range(n)])]
    ppermute x6, starting transfers between devices: 9.25 us -> 10.2 us  [spread(): pieces[d] = lax.ppermute(x, 'pool', [(i, i ^ d) for i in range(n)])]
    pallas_call x1, Pallas kernels: 3.08 us -> 3.88 us  [late_part(): pl.pallas_call(functools.partial(late_kernel, near, group, items), in_spe...]
    pallas_call x1, Pallas kernels: 3.14 us -> 2.34 us  [last_part(): pl.pallas_call(functools.partial(last_kernel, group, items), in_specs=[VM...]
  transfers between devices with their start and end apart: 15 -> 15, of which waited for: 4 -> 5; matrix products, arithmetic and copies ran while one was open for 0% -> 0% of each run, Pallas kernels for 25% -> 25%
where the time goes in v6:
time: 35.6 us; the launch traced here: 35.4 us
  starting transfers between devices  12.8 us (36%)
  Pallas kernels  12.6 us (35%)
  waiting for transfers between devices  8.56 us (24%)
  between operations  0.74 us (2%)
  other arithmetic  0.62 us (2%)
    ppermute x6, starting transfers between devices, spread(): pieces[d] = lax.ppermute(x, 'pool', [(i, i ^ d) for i in range(n)])  10.2 us
    ppermute x6, waiting for transfers between devices, spread(): pieces[d] = lax.ppermute(x, 'pool', [(i, i ^ d) for i in range(n)])  8.47 us
    pallas_call x1, Pallas kernels, late_part(): pl.pallas_call(functools.partial(late_kernel, near, group, items), in_spe...  3.88 us
    pallas_call x1, Pallas kernels, early_part(): pl.pallas_call(functools.partial(early_kernel, n, tp, near, group, window...  2.61 us
    pallas_call x1, Pallas kernels, last_part(): pl.pallas_call(functools.partial(last_kernel, group, items), in_specs=[VM...  2.34 us
    pallas_call x1, Pallas kernels, project(): pl.pallas_call(functools.partial(project_kernel, len(pieces), tp), in_spe...  2.21 us
    ppermute x1, starting transfers between devices, local(): other = lax.ppermute(send, 'tp', [(0, 1), (1, 0)])  1.56 us
    ppermute x8, starting transfers between devices, spread(): lax.ppermute(pieces[d], 'pool', [(i, i ^ 1) for i in range(n)])  1.03 us
  transfers between devices with their start and end apart: 15, of which 5 were waited for; matrix products, arithmetic and copies ran while one was open for 0% of the time, Pallas kernels for 25%

profile of v6, /device:TPU:0, one launch (start us, length us, event | category | flops | bytes accessed | tf_op | source)
XLA Modules:
  0.0 35.4 jit_solution(17720035127558718191)
XLA Ops:
  0.6 0.8 %pack.1 = (bf16[4,5120]{1,0:T(4,128)(2,1)S(1)}, s32[1,448]{1,0:T(1,128)S(1)}, s32[1,32]{1,0:T(1,128)S(1)}, s32[1,32]{1,0:T(1,128)S(1)}) custom-call(bf16[4,4096]{1,0:T(4,128)(2,1)} %q_ref.1, bf16[4,512]{1,0:T(4,128)(2,1)} %k_ref.1, bf16[4,512]{1,0:T(4,128)(2,1)} %v_ref.1, s32[1,448]{1,0:T(1,128)} %refs_0_.1, s32[1,32]{1,0:T(1,128)} %bitcast.2, s32[1,32]{1,0:T(1,128)} %bitcast.3), custom_call_target="tpu_custom_call" | custom-call | tf_op jit(solution)/shard_map/pack/pallas_call | solution.py:389
  1.4 5.1 %collective-permute-start.5 = (bf16[4,5120]{1,0:T(4,128)(2,1)S(1)}, bf16[4,5120]{1,0:T(4,128)(2,1)S(1)}, u32[]{:S(2)}, u32[]{:S(2)}) collective-permute-start(bf16[4,5120]{1,0:T(4,128)(2,1)S(1)} %get-tuple-element.37.refs_0_), channel_id=1, source_target_pairs={{0,12},{2,14},{4,8},{6,10},{8,4},{10,6},{12,0},{14,2},{1,13},{3,15... | collective-permute-start | bytes 122888 | tf_op jit(solution)/shard_map/ppermute | solution.py:365
  6.6 0.0 collective-permute-start.3
  6.6 0.6 %collective-permute-start.1 = (bf16[4,5120]{1,0:T(4,128)(2,1)S(1)}, bf16[4,5120]{1,0:T(4,128)(2,1)S(1)}, u32[]{:S(2)}, u32[]{:S(2)}) collective-permute-start(bf16[4,5120]{1,0:T(4,128)(2,1)S(1)} %get-tuple-element.37.refs_0_), channel_id=1, source_target_pairs={{0,4},{2,6},{4,0},{6,2},{8,12},{10,14},{12,8},{14,10},{1,5},{3,7},... | collective-permute-start | bytes 122888 | tf_op jit(solution)/shard_map/ppermute | solution.py:365
  7.2 0.0 collective-permute-start
  7.2 1.3 %collective-permute-done.5.refs_6_ = bf16[4,5120]{1,0:T(4,128)(2,1)S(1)} collective-permute-done((bf16[4,5120]{1,0:T(4,128)(2,1)S(1)}, bf16[4,5120]{1,0:T(4,128)(2,1)S(1)}, u32[]{:S(2)}, u32[]{:S(2)}) %collective-permute-start.5) | collective-permute-done | bytes 40992 | tf_op jit(solution)/shard_map/ppermute | solution.py:365
  8.6 0.0 collective-permute-start.6
  8.6 2.9 %collective-permute-done.3.refs_4_ = bf16[4,5120]{1,0:T(4,128)(2,1)S(1)} collective-permute-done((bf16[4,5120]{1,0:T(4,128)(2,1)S(1)}, bf16[4,5120]{1,0:T(4,128)(2,1)S(1)}, u32[]{:S(2)}, u32[]{:S(2)}) %collective-permute-start.3) | collective-permute-done | bytes 40992 | tf_op jit(solution)/shard_map/ppermute | solution.py:365
  11.5 0.0 collective-permute-start.4
  11.5 0.0 collective-permute-done.1.refs_2_
  11.5 0.5 %collective-permute-start.2 = (bf16[4,5120]{1,0:T(4,128)(2,1)S(1)}, bf16[4,5120]{1,0:T(4,128)(2,1)S(1)}, u32[]{:S(2)}, u32[]{:S(2)}) collective-permute-start(bf16[4,5120]{1,0:T(4,128)(2,1)S(1)} %collective-permute-done.1.refs_2_), channel_id=1, source_target_pairs={{0,2},{2,0},{4,6},{6,4},{8,10},{10,8},{12,14},{14,12},{1,3},{3,1},... | collective-permute-start | bytes 122888 | tf_op jit(solution)/shard_map/ppermute | solution.py:367
  12.0 2.6 %early.1 = (bf16[4,448,1024]{2,1,0:T(8,128)(2,1)S(1)}, bf16[4,448,1024]{2,1,0:T(8,128)(2,1)S(1)}, bf16[4,448,128]{2,1,0:T(8,128)(2,1)S(1)}, bf16[4,448,128]{2,1,...) custom-call(s32[1,448]{1,0:T(1,128)S(1)} %get-tuple-element.24.refs_, ...), custom_call_target="tpu_custom_call" | custom-call | flops 67108864 | bytes 1048576 | tf_op jit(solution)/shard_map/early/pallas_call | solution.py:300
  14.6 0.0 collective-permute-done.refs_1_
  14.6 0.0 collective-permute-done.6.refs_7_
  14.6 0.0 collective-permute-done.4.refs_5_
  14.6 0.0 collective-permute-done.2.refs_3_
  14.7 0.8 %decode.1.refs_0_ = bf16[8,4096]{1,0:T(8,128)(2,1)S(1)} custom-call(bf16[4,5120]{1,0:T(4,128)(2,1)S(1)} %get-tuple-element.37.refs_0_, bf16[4,5120]{1,0:T(4,128)(2,1)S(1)} %collective-permute-done.refs_1_, bf16[4,5120]{1,0:T(4,128)(2,1)S(1)} %collective-permute-done.1.refs_2_, bf16[4,5120]{1,0:T(4,128)(2,1)S(1)} %collective-permute-done.2.refs_3_, ...), custom_call_target="tpu_custom_call" | custom-call | flops 1000000000 | bytes 1048576 | tf_op jit(solution)/shard_map/decode/pallas_call | solution.py:464
  15.4 1.6 %collective-permute-start.12 = (bf16[8,4096]{1,0:T(8,128)(2,1)S(1)}, bf16[8,4096]{1,0:T(8,128)(2,1)S(1)}, u32[]{:S(2)}, u32[]{:S(2)}) collective-permute-start(bf16[8,4096]{1,0:T(8,128)(2,1)S(1)} %decode.1.refs_0_), channel_id=1, source_target_pairs={{0,12},{2,14},{4,8},{6,10},{8,4},{10,6},{12,0},{14,2},{1,13},{3,15... | collective-permute-start | bytes 196616 | tf_op jit(solution)/shard_map/ppermute | solution.py:365
  17.1 0.0 collective-permute-start.10
  17.1 2.8 %collective-permute-start.8 = (bf16[8,4096]{1,0:T(8,128)(2,1)S(1)}, bf16[8,4096]{1,0:T(8,128)(2,1)S(1)}, u32[]{:S(2)}, u32[]{:S(2)}) collective-permute-start(bf16[8,4096]{1,0:T(8,128)(2,1)S(1)} %decode.1.refs_0_), channel_id=1, source_target_pairs={{0,4},{2,6},{4,0},{6,2},{8,12},{10,14},{12,8},{14,10},{1,5},{3,7},... | collective-permute-start | bytes 196616 | tf_op jit(solution)/shard_map/ppermute | solution.py:365
  19.9 0.0 collective-permute-start.7
  19.9 2.4 %collective-permute-done.12.refs_6_ = bf16[8,4096]{1,0:T(8,128)(2,1)S(1)} collective-permute-done((bf16[8,4096]{1,0:T(8,128)(2,1)S(1)}, bf16[8,4096]{1,0:T(8,128)(2,1)S(1)}, u32[]{:S(2)}, u32[]{:S(2)}) %collective-permute-start.12) | collective-permute-done | bytes 65568 | tf_op jit(solution)/shard_map/ppermute | solution.py:365
  22.3 0.0 collective-permute-start.13
  22.3 1.8 %collective-permute-done.10.refs_4_ = bf16[8,4096]{1,0:T(8,128)(2,1)S(1)} collective-permute-done((bf16[8,4096]{1,0:T(8,128)(2,1)S(1)}, bf16[8,4096]{1,0:T(8,128)(2,1)S(1)}, u32[]{:S(2)}, u32[]{:S(2)}) %collective-permute-start.10) | collective-permute-done | bytes 65568 | tf_op jit(solution)/shard_map/ppermute | solution.py:365
  24.1 0.0 collective-permute-start.11
  24.1 0.0 collective-permute-done.8.refs_2_
  24.1 0.5 %collective-permute-start.9 = (bf16[8,4096]{1,0:T(8,128)(2,1)S(1)}, bf16[8,4096]{1,0:T(8,128)(2,1)S(1)}, u32[]{:S(2)}, u32[]{:S(2)}) collective-permute-start(bf16[8,4096]{1,0:T(8,128)(2,1)S(1)} %collective-permute-done.8.refs_2_), channel_id=1, source_target_pairs={{0,2},{2,0},{4,6},{6,4},{8,10},{10,8},{12,14},{14,12},{1,3},{3,1},... | collective-permute-start | bytes 196616 | tf_op jit(solution)/shard_map/ppermute | solution.py:367
  24.6 3.9 %late.1 = (bf16[4,448,1024]{2,1,0:T(8,128)(2,1)S(1)}, bf16[4,448,128]{2,1,0:T(8,128)(2,1)S(1)}, bf16[4,448,128]{2,1,0:T(8,128)(2,1)S(1)}, bf16[4,448,1024]{2,1,0:T(8,128)(2,1)S(1)}, bf16[3072,1024]{1,0:T(8,128)(2,1)S(1)}) custom-call(bf16[4,448,1024]{2,1,0:T(8,128)(2,1)S(1)} %get-tuple-elemen, ...), custom_call_target="tpu_custom_call", output_to_operand_aliasing={{0}: (0, {}), {1}: (1, {}), {2}: (2, {}), {3}: (3, {})} | custom-call | flops 1140850688 | bytes 1048576 | tf_op jit(solution)/shard_map/late/pallas_call | solution.py:316
  28.5 0.0 collective-permute-done.7.refs_1_
  28.5 0.0 collective-permute-done.13.refs_7_
  28.5 0.0 collective-permute-done.11.refs_5_
  28.6 0.0 collective-permute-done.9.refs_3_
  28.6 2.2 %project.1 = (bf16[16,1024]{1,0:T(8,128)(2,1)S(1)}, f32[16,1024]{1,0:T(8,128)S(1)}) custom-call(bf16[8,4096]{1,0:T(8,128)(2,1)S(1)} %decode.1.refs_0_, bf16[8,4096]{1,0:T(8,128)(2,1)S(1)} %collective-permute-done.7.refs_1_, bf16[8,4096]{1,0:T(8,128)(2,1)S(1)} %collective-permute-done.8.refs_2_, bf16[8,4096]{1,0:T(8,128)(2,1)S(1)} %collective-permute-done.9.refs_3_, ...), custom_call_target="tpu_custom_call" | custom-call | flops 1000000000 | bytes 8388608 | tf_op jit(solution)/shard_map/project/pallas_call | solution.py:520
  30.8 1.6 %collective-permute-start.14 = (bf16[16,1024]{1,0:T(8,128)(2,1)S(1)}, bf16[16,1024]{1,0:T(8,128)(2,1)S(1)}, u32[]{:S(2)}, u32[]{:S(2)}) collective-permute-start(bf16[16,1024]{1,0:T(8,128)(2,1)S(1)} %get-tuple-element.45), channel_id=1, source_target_pairs={{0,1},{1,0},{2,3},{3,2},{4,5},{5,4},{6,7},{7,6},{8,9},{9,8},{10,11... | collective-permute-start | bytes 98312 | tf_op jit(solution)/shard_map/ppermute | solution.py:583
  32.3 2.3 %last.1 = (bf16[4,448,1024]{2,1,0:T(8,128)(2,1)S(1)}, bf16[448,4096]{1,0:T(8,128)(2,1)}) custom-call(bf16[4,448,1024]{2,1,0:T(8,128)(2,1)S(1)} %get-tuple-element.32.refs_0_, bf16[4,448,128]{2,1,0:T(8,128)(2,1)S(1)} %get-tuple-element.33.refs_1_, bf16[4,448,128]{2,1,0:T(8,128)(2,1)S(1)} %get-tuple-element.34.refs_2_, ...), custom_call_target="tpu_custom_call", output_to_operand_aliasing={{0}: (3, {})} | custom-call | flops 402653184 | bytes 1048576 | tf_op jit(solution)/shard_map/last/pallas_call | solution.py:332
  34.7 0.1 collective-permute-done.14
  34.8 0.6 %add_convert_fusion = bf16[16,1024]{1,0:T(8,128)(2,1)} fusion(f32[16,1024]{1,0:T(8,128)S(1)} %get-tuple-element.44, bf16[16,1024]{1,0:T(8,128)(2,1)S(1)} %collective-permute-done.14), kind=kLoop, calls=%fused_computation | loop fusion | flops 49152 | bytes 131072 | tf_op jit(solution)/shard_map/convert_element_type | solution.py:584
Async XLA Ops:
  1.4 7.1 %collective-permute-start.5 = (bf16[4,5120]{1,0:T(4,128)(2,1)S(1)}, bf16[4,5120]{1,0:T(4,128)(2,1)S(1)}, u32[]{:S(2)}, u32[]{:S(2)}) collective-permute-start(bf16[4,5120]{1,0:T(4,128)(2,1)S(1)} %get-tuple-element.37.refs_0_), channel_id=1, source_target_pairs={{0,12},{2,14},{4,8},{6,10},{8,4},{10,6},{12,0},{14,2},{1,13},{3,15... | collective-permute-start | bytes 122888 | tf_op jit(solution)/shard_map/ppermute | solution.py:365
  6.6 4.9 %collective-permute-start.3 = (bf16[4,5120]{1,0:T(4,128)(2,1)S(1)}, bf16[4,5120]{1,0:T(4,128)(2,1)S(1)}, u32[]{:S(2)}, u32[]{:S(2)}) collective-permute-start(bf16[4,5120]{1,0:T(4,128)(2,1)S(1)} %get-tuple-element.37.refs_0_), channel_id=1, source_target_pairs={{0,8},{2,10},{4,12},{6,14},{8,0},{10,2},{12,4},{14,6},{1,9},{3,11}... | collective-permute-start | bytes 122888 | tf_op jit(solution)/shard_map/ppermute | solution.py:365
  6.6 4.9 %collective-permute-start.1 = (bf16[4,5120]{1,0:T(4,128)(2,1)S(1)}, bf16[4,5120]{1,0:T(4,128)(2,1)S(1)}, u32[]{:S(2)}, u32[]{:S(2)}) collective-permute-start(bf16[4,5120]{1,0:T(4,128)(2,1)S(1)} %get-tuple-element.37.refs_0_), channel_id=1, source_target_pairs={{0,4},{2,6},{4,0},{6,2},{8,12},{10,14},{12,8},{14,10},{1,5},{3,7},... | collective-permute-start | bytes 122888 | tf_op jit(solution)/shard_map/ppermute | solution.py:365
  7.2 7.4 %collective-permute-start = (bf16[4,5120]{1,0:T(4,128)(2,1)S(1)}, bf16[4,5120]{1,0:T(4,128)(2,1)S(1)}, u32[]{:S(2)}, u32[]{:S(2)}) collective-permute-start(bf16[4,5120]{1,0:T(4,128)(2,1)S(1)} %get-tuple-element.37.refs_0_), channel_id=1, source_target_pairs={{0,2},{2,0},{4,6},{6,4},{8,10},{10,8},{12,14},{14,12},{1,3},{3,1},... | collective-permute-start | bytes 122888 | tf_op jit(solution)/shard_map/ppermute | solution.py:367
  8.6 6.1 %collective-permute-start.6 = (bf16[4,5120]{1,0:T(4,128)(2,1)S(1)}, bf16[4,5120]{1,0:T(4,128)(2,1)S(1)}, u32[]{:S(2)}, u32[]{:S(2)}) collective-permute-start(bf16[4,5120]{1,0:T(4,128)(2,1)S(1)} %collective-permute-done.5.refs_6_), channel_id=1, source_target_pairs={{0,2},{2,0},{4,6},{6,4},{8,10},{10,8},{12,14},{14,12},{1,3},{3,1},... | collective-permute-start | bytes 122888 | tf_op jit(solution)/shard_map/ppermute | solution.py:367
  11.5 3.2 %collective-permute-start.4 = (bf16[4,5120]{1,0:T(4,128)(2,1)S(1)}, bf16[4,5120]{1,0:T(4,128)(2,1)S(1)}, u32[]{:S(2)}, u32[]{:S(2)}) collective-permute-start(bf16[4,5120]{1,0:T(4,128)(2,1)S(1)} %collective-permute-done.3.refs_4_), channel_id=1, source_target_pairs={{0,2},{2,0},{4,6},{6,4},{8,10},{10,8},{12,14},{14,12},{1,3},{3,1},... | collective-permute-start | bytes 122888 | tf_op jit(solution)/shard_map/ppermute | solution.py:367
  11.5 3.2 %collective-permute-start.2 = (bf16[4,5120]{1,0:T(4,128)(2,1)S(1)}, bf16[4,5120]{1,0:T(4,128)(2,1)S(1)}, u32[]{:S(2)}, u32[]{:S(2)}) collective-permute-start(bf16[4,5120]{1,0:T(4,128)(2,1)S(1)} %collective-permute-done.1.refs_2_), channel_id=1, source_target_pairs={{0,2},{2,0},{4,6},{6,4},{8,10},{10,8},{12,14},{14,12},{1,3},{3,1},... | collective-permute-start | bytes 122888 | tf_op jit(solution)/shard_map/ppermute | solution.py:367
  15.4 6.8 %collective-permute-start.12 = (bf16[8,4096]{1,0:T(8,128)(2,1)S(1)}, bf16[8,4096]{1,0:T(8,128)(2,1)S(1)}, u32[]{:S(2)}, u32[]{:S(2)}) collective-permute-start(bf16[8,4096]{1,0:T(8,128)(2,1)S(1)} %decode.1.refs_0_), channel_id=1, source_target_pairs={{0,12},{2,14},{4,8},{6,10},{8,4},{10,6},{12,0},{14,2},{1,13},{3,15... | collective-permute-start | bytes 196616 | tf_op jit(solution)/shard_map/ppermute | solution.py:365
  17.1 7.0 %collective-permute-start.10 = (bf16[8,4096]{1,0:T(8,128)(2,1)S(1)}, bf16[8,4096]{1,0:T(8,128)(2,1)S(1)}, u32[]{:S(2)}, u32[]{:S(2)}) collective-permute-start(bf16[8,4096]{1,0:T(8,128)(2,1)S(1)} %decode.1.refs_0_), channel_id=1, source_target_pairs={{0,8},{2,10},{4,12},{6,14},{8,0},{10,2},{12,4},{14,6},{1,9},{3,11}... | collective-permute-start | bytes 196616 | tf_op jit(solution)/shard_map/ppermute | solution.py:365
  17.1 7.0 %collective-permute-start.8 = (bf16[8,4096]{1,0:T(8,128)(2,1)S(1)}, bf16[8,4096]{1,0:T(8,128)(2,1)S(1)}, u32[]{:S(2)}, u32[]{:S(2)}) collective-permute-start(bf16[8,4096]{1,0:T(8,128)(2,1)S(1)} %decode.1.refs_0_), channel_id=1, source_target_pairs={{0,4},{2,6},{4,0},{6,2},{8,12},{10,14},{12,8},{14,10},{1,5},{3,7},... | collective-permute-start | bytes 196616 | tf_op jit(solution)/shard_map/ppermute | solution.py:365
  19.9 8.6 %collective-permute-start.7 = (bf16[8,4096]{1,0:T(8,128)(2,1)S(1)}, bf16[8,4096]{1,0:T(8,128)(2,1)S(1)}, u32[]{:S(2)}, u32[]{:S(2)}) collective-permute-start(bf16[8,4096]{1,0:T(8,128)(2,1)S(1)} %decode.1.refs_0_), channel_id=1, source_target_pairs={{0,2},{2,0},{4,6},{6,4},{8,10},{10,8},{12,14},{14,12},{1,3},{3,1},... | collective-permute-start | bytes 196616 | tf_op jit(solution)/shard_map/ppermute | solution.py:367
  22.3 6.3 %collective-permute-start.13 = (bf16[8,4096]{1,0:T(8,128)(2,1)S(1)}, bf16[8,4096]{1,0:T(8,128)(2,1)S(1)}, u32[]{:S(2)}, u32[]{:S(2)}) collective-permute-start(bf16[8,4096]{1,0:T(8,128)(2,1)S(1)} %collective-permute-done.12.refs_6_), channel_id=1, source_target_pairs={{0,2},{2,0},{4,6},{6,4},{8,10},{10,8},{12,14},{14,12},{1,3},{3,1},... | collective-permute-start | bytes 196616 | tf_op jit(solution)/shard_map/ppermute | solution.py:367
  24.1 4.4 %collective-permute-start.11 = (bf16[8,4096]{1,0:T(8,128)(2,1)S(1)}, bf16[8,4096]{1,0:T(8,128)(2,1)S(1)}, u32[]{:S(2)}, u32[]{:S(2)}) collective-permute-start(bf16[8,4096]{1,0:T(8,128)(2,1)S(1)} %collective-permute-done.10.refs_4_), channel_id=1, source_target_pairs={{0,2},{2,0},{4,6},{6,4},{8,10},{10,8},{12,14},{14,12},{1,3},{3,1},... | collective-permute-start | bytes 196616 | tf_op jit(solution)/shard_map/ppermute | solution.py:367
  24.1 4.4 %collective-permute-start.9 = (bf16[8,4096]{1,0:T(8,128)(2,1)S(1)}, bf16[8,4096]{1,0:T(8,128)(2,1)S(1)}, u32[]{:S(2)}, u32[]{:S(2)}) collective-permute-start(bf16[8,4096]{1,0:T(8,128)(2,1)S(1)} %collective-permute-done.8.refs_2_), channel_id=1, source_target_pairs={{0,2},{2,0},{4,6},{6,4},{8,10},{10,8},{12,14},{14,12},{1,3},{3,1},... | collective-permute-start | bytes 196616 | tf_op jit(solution)/shard_map/ppermute | solution.py:367
  30.8 4.0 %collective-permute-start.14 = (bf16[16,1024]{1,0:T(8,128)(2,1)S(1)}, bf16[16,1024]{1,0:T(8,128)(2,1)S(1)}, u32[]{:S(2)}, u32[]{:S(2)}) collective-permute-start(bf16[16,1024]{1,0:T(8,128)(2,1)S(1)} %get-tuple-element.45), channel_id=1, source_target_pairs={{0,1},{1,0},{2,3},{3,2},{4,5},{5,4},{6,7},{7,6},{8,9},{9,8},{10,11... | collective-permute-start | bytes 98312 | tf_op jit(solution)/shard_map/ppermute | solution.py:583

commit v7 on v6

--- a/solution.py
+++ b/solution.py
@@ -11,7 +11,7 @@
 HEAD_DIM = 128
 LOG2E = 1.4426950408889634
 ROW_BLOCK = 32
-EARLY, LATE = 0.07, 0.69
+EARLY, LATE = 0.05, 0.69
 VMEM = pl.BlockSpec(memory_space=pltpu.VMEM)
 HBM = pl.BlockSpec(memory_space=pltpu.HBM)
 
@@ -37,7 +37,8 @@
     for item, price in items:
         spent += price
         share = spent / total
-        parts[0 if share <= EARLY else 1 if share <= EARLY + LATE else 2].append(item)
+        first = share <= EARLY or not parts[0]
+        parts[0 if first else 1 if share <= EARLY + LATE else 2].append(item)
     return parts
 
 
@@ -362,10 +363,11 @@
         return [lax.all_gather(x, "pool", axis=0, tiled=True)]
     pieces = {0: x}
     for d in far_order(n):
-        pieces[d] = lax.ppermute(x, "pool", [(i, i ^ d) for i in range(n)])
+        pieces[d + 1] = lax.ppermute(x, "pool", [(i, i ^ (d + 1)) for i in range(n)])
     for d in range(0, n, 2):
-        pieces[d + 1] = lax.ppermute(
-            pieces[d], "pool", [(i, i ^ 1) for i in range(n)]
+        have = d + 1 if d else 0
+        pieces[have ^ 1] = lax.ppermute(
+            pieces[have], "pool", [(i, i ^ 1) for i in range(n)]
         )
     return [pieces[d] for d in range(n)]
 
@@ -555,7 +557,7 @@
     kv_local = home_key.shape[1] // HEAD_DIM
     group = home_query.shape[1] // HEAD_DIM // kv_local
     window = min(rows, rows // 2 + ROW_BLOCK)
-    near = max(1, kv_local // 2)
+    near = max(1, kv_local // 4)
     early, late, last = shares(kv_local, rows, group, window)
     prompt = (prompt_query, prompt_key, prompt_value)
 

time: 35.6 us -> 35.1 us (0.986)
  waiting for transfers between devices: 8.56 us -> 7.64 us
  starting transfers between devices: 12.8 us -> 13.4 us
    ppermute x14, waiting for transfers between devices: 8.49 us -> 7.64 us  [the longest x6 7.62 us: spread(): pieces[d + 1] = lax.ppermute(x, 'pool', [(i, i ^ d + 1) for i in range(n)])]
    pallas_call x1, Pallas kernels: 2.61 us -> 1.97 us  [early_part(): pl.pallas_call(functools.partial(early_kernel, n, tp, near, group, window...]
    ppermute x14, starting transfers between devices: 11.3 us -> 11.8 us  [the longest x6 9.57 us: spread(): pieces[d + 1] = lax.ppermute(x, 'pool', [(i, i ^ d + 1) for i in range(n)])]
  transfers between devices with their start and end apart: 15 -> 15, of which waited for: 5 -> 4; matrix products, arithmetic and copies ran while one was open for 0% -> 0% of each run, Pallas kernels for 25% -> 25%
where the time goes in v7:
time: 35.1 us; the launch traced here: 34.8 us
  starting transfers between devices  13.4 us (38%)
  Pallas kernels  12.4 us (35%)
  waiting for transfers between devices  7.64 us (22%)
  between operations  0.75 us (2%)
  other arithmetic  0.62 us (2%)
    ppermute x6, starting transfers between devices, spread(): pieces[d + 1] = lax.ppermute(x, 'pool', [(i, i ^ d + 1) for i in range(n)])  9.57 us
    ppermute x6, waiting for transfers between devices, spread(): pieces[d + 1] = lax.ppermute(x, 'pool', [(i, i ^ d + 1) for i in range(n)])  7.62 us
    pallas_call x1, Pallas kernels, late_part(): pl.pallas_call(functools.partial(late_kernel, near, group, items), in_spe...  4.21 us
    pallas_call x1, Pallas kernels, last_part(): pl.pallas_call(functools.partial(last_kernel, group, items), in_specs=[VM...  2.44 us
    ppermute x8, starting transfers between devices, spread(): lax.ppermute(pieces[have], 'pool', [(i, i ^ 1) for i in range(n)])  2.28 us
    pallas_call x1, Pallas kernels, project(): pl.pallas_call(functools.partial(project_kernel, len(pieces), tp), in_spe...  2.21 us
    pallas_call x1, Pallas kernels, early_part(): pl.pallas_call(functools.partial(early_kernel, n, tp, near, group, window...  1.97 us
    ppermute x1, starting transfers between devices, local(): other = lax.ppermute(send, 'tp', [(0, 1), (1, 0)])  1.55 us
  transfers between devices with their start and end apart: 15, of which 4 were waited for; matrix products, arithmetic and copies ran while one was open for 0% of the time, Pallas kernels for 25%

profile of v7, /device:TPU:0, one launch (start us, length us, event | category | flops | bytes accessed | tf_op | source)
XLA Modules:
  0.0 34.8 jit_solution(258127855611138957)
XLA Ops:
  0.6 0.8 %pack.1 = (bf16[4,5120]{1,0:T(4,128)(2,1)S(1)}, s32[1,448]{1,0:T(1,128)S(1)}, s32[1,32]{1,0:T(1,128)S(1)}, s32[1,32]{1,0:T(1,128)S(1)}) custom-call(bf16[4,4096]{1,0:T(4,128)(2,1)} %q_ref.1, bf16[4,512]{1,0:T(4,128)(2,1)} %k_ref.1, bf16[4,512]{1,0:T(4,128)(2,1)} %v_ref.1, s32[1,448]{1,0:T(1,128)} %refs_0_.1, s32[1,32]{1,0:T(1,128)} %bitcast.2, s32[1,32]{1,0:T(1,128)} %bitcast.3), custom_call_target="tpu_custom_call" | custom-call | tf_op jit(solution)/shard_map/pack/pallas_call | solution.py:391
  1.4 4.6 %collective-permute-start.5 = (bf16[4,5120]{1,0:T(4,128)(2,1)S(1)}, bf16[4,5120]{1,0:T(4,128)(2,1)S(1)}, u32[]{:S(2)}, u32[]{:S(2)}) collective-permute-start(bf16[4,5120]{1,0:T(4,128)(2,1)S(1)} %get-tuple-element.37.refs_0_), channel_id=1, source_target_pairs={{0,14},{2,12},{4,10},{6,8},{8,6},{10,4},{12,2},{14,0},{1,15},{3,13... | collective-permute-start | bytes 122888 | tf_op jit(solution)/shard_map/ppermute | solution.py:366
  6.0 0.0 collective-permute-start.3
  6.0 0.9 %collective-permute-start.1 = (bf16[4,5120]{1,0:T(4,128)(2,1)S(1)}, bf16[4,5120]{1,0:T(4,128)(2,1)S(1)}, u32[]{:S(2)}, u32[]{:S(2)}) collective-permute-start(bf16[4,5120]{1,0:T(4,128)(2,1)S(1)} %get-tuple-element.37.refs_0_), channel_id=1, source_target_pairs={{0,6},{2,4},{4,2},{6,0},{8,14},{10,12},{12,10},{14,8},{1,7},{3,5},... | collective-permute-start | bytes 122888 | tf_op jit(solution)/shard_map/ppermute | solution.py:366
  6.9 0.0 collective-permute-start
  6.9 1.0 %collective-permute-done.5.refs_7_ = bf16[4,5120]{1,0:T(4,128)(2,1)S(1)} collective-permute-done((bf16[4,5120]{1,0:T(4,128)(2,1)S(1)}, bf16[4,5120]{1,0:T(4,128)(2,1)S(1)}, u32[]{:S(2)}, u32[]{:S(2)}) %collective-permute-start.5) | collective-permute-done | bytes 40992 | tf_op jit(solution)/shard_map/ppermute | solution.py:366
  8.0 0.4 %collective-permute-start.6 = (bf16[4,5120]{1,0:T(4,128)(2,1)S(1)}, bf16[4,5120]{1,0:T(4,128)(2,1)S(1)}, u32[]{:S(2)}, u32[]{:S(2)}) collective-permute-start(bf16[4,5120]{1,0:T(4,128)(2,1)S(1)} %collective-permute-done.5.refs_7_), channel_id=1, source_target_pairs={{0,2},{2,0},{4,6},{6,4},{8,10},{10,8},{12,14},{14,12},{1,3},{3,1},... | collective-permute-start | bytes 122888 | tf_op jit(solution)/shard_map/ppermute | solution.py:369
  8.4 2.3 %collective-permute-done.3.refs_5_ = bf16[4,5120]{1,0:T(4,128)(2,1)S(1)} collective-permute-done((bf16[4,5120]{1,0:T(4,128)(2,1)S(1)}, bf16[4,5120]{1,0:T(4,128)(2,1)S(1)}, u32[]{:S(2)}, u32[]{:S(2)}) %collective-permute-start.3) | collective-permute-done | bytes 40992 | tf_op jit(solution)/shard_map/ppermute | solution.py:366
  10.7 0.3 collective-permute-start.4
  11.0 0.0 collective-permute-done.1.refs_3_
  11.0 0.2 collective-permute-start.2
  11.2 2.0 %early.1 = (bf16[4,448,1024]{2,1,0:T(8,128)(2,1)S(1)}, bf16[4,448,1024]{2,1,0:T(8,128)(2,1)S(1)}, bf16[4,448,128]{2,1,0:T(8,128)(2,1)S(1)}, bf16[4,448,128]{2,1,...) custom-call(s32[1,448]{1,0:T(1,128)S(1)} %get-tuple-element.24.refs_, ...), custom_call_target="tpu_custom_call" | custom-call | flops 33554432 | bytes 1048576 | tf_op jit(solution)/shard_map/early/pallas_call | solution.py:301
  13.2 0.0 collective-permute-done.refs_1_
  13.2 0.0 collective-permute-done.6.refs_6_
  13.2 0.0 collective-permute-done.4.refs_4_
  13.3 0.0 collective-permute-done.2.refs_2_
  13.3 0.8 %decode.1.refs_0_ = bf16[8,4096]{1,0:T(8,128)(2,1)S(1)} custom-call(bf16[4,5120]{1,0:T(4,128)(2,1)S(1)} %get-tuple-element.37.refs_0_, bf16[4,5120]{1,0:T(4,128)(2,1)S(1)} %collective-permute-done.refs_1_, bf16[4,5120]{1,0:T(4,128)(2,1)S(1)} %collective-permute-done.2.refs_2_, bf16[4,5120]{1,0:T(4,128)(2,1)S(1)} %collective-permute-done.1.refs_3_, ...), custom_call_target="tpu_custom_call" | custom-call | flops 1000000000 | bytes 1048576 | tf_op jit(solution)/shard_map/decode/pallas_call | solution.py:466
  14.1 2.0 %collective-permute-start.12 = (bf16[8,4096]{1,0:T(8,128)(2,1)S(1)}, bf16[8,4096]{1,0:T(8,128)(2,1)S(1)}, u32[]{:S(2)}, u32[]{:S(2)}) collective-permute-start(bf16[8,4096]{1,0:T(8,128)(2,1)S(1)} %decode.1.refs_0_), channel_id=1, source_target_pairs={{0,14},{2,12},{4,10},{6,8},{8,6},{10,4},{12,2},{14,0},{1,15},{3,13... | collective-permute-start | bytes 196616 | tf_op jit(solution)/shard_map/ppermute | solution.py:366
  16.1 0.3 collective-permute-start.10
  16.4 1.8 %collective-permute-start.8 = (bf16[8,4096]{1,0:T(8,128)(2,1)S(1)}, bf16[8,4096]{1,0:T(8,128)(2,1)S(1)}, u32[]{:S(2)}, u32[]{:S(2)}) collective-permute-start(bf16[8,4096]{1,0:T(8,128)(2,1)S(1)} %decode.1.refs_0_), channel_id=1, source_target_pairs={{0,6},{2,4},{4,2},{6,0},{8,14},{10,12},{12,10},{14,8},{1,7},{3,5},... | collective-permute-start | bytes 196616 | tf_op jit(solution)/shard_map/ppermute | solution.py:366
  18.1 0.2 collective-permute-start.7
  18.3 1.7 %collective-permute-done.12.refs_7_ = bf16[8,4096]{1,0:T(8,128)(2,1)S(1)} collective-permute-done((bf16[8,4096]{1,0:T(8,128)(2,1)S(1)}, bf16[8,4096]{1,0:T(8,128)(2,1)S(1)}, u32[]{:S(2)}, u32[]{:S(2)}) %collective-permute-start.12) | collective-permute-done | bytes 65568 | tf_op jit(solution)/shard_map/ppermute | solution.py:366
  20.0 0.6 %collective-permute-start.13 = (bf16[8,4096]{1,0:T(8,128)(2,1)S(1)}, bf16[8,4096]{1,0:T(8,128)(2,1)S(1)}, u32[]{:S(2)}, u32[]{:S(2)}) collective-permute-start(bf16[8,4096]{1,0:T(8,128)(2,1)S(1)} %collective-permute-done.12.refs_7_), channel_id=1, source_target_pairs={{0,2},{2,0},{4,6},{6,4},{8,10},{10,8},{12,14},{14,12},{1,3},{3,1},... | collective-permute-start | bytes 196616 | tf_op jit(solution)/shard_map/ppermute | solution.py:369
  20.6 2.6 %collective-permute-done.10.refs_5_ = bf16[8,4096]{1,0:T(8,128)(2,1)S(1)} collective-permute-done((bf16[8,4096]{1,0:T(8,128)(2,1)S(1)}, bf16[8,4096]{1,0:T(8,128)(2,1)S(1)}, u32[]{:S(2)}, u32[]{:S(2)}) %collective-permute-start.10) | collective-permute-done | bytes 65568 | tf_op jit(solution)/shard_map/ppermute | solution.py:366
  23.2 0.1 collective-permute-start.11
  23.3 0.0 collective-permute-done.8.refs_3_
  23.3 0.4 %collective-permute-start.9 = (bf16[8,4096]{1,0:T(8,128)(2,1)S(1)}, bf16[8,4096]{1,0:T(8,128)(2,1)S(1)}, u32[]{:S(2)}, u32[]{:S(2)}) collective-permute-start(bf16[8,4096]{1,0:T(8,128)(2,1)S(1)} %collective-permute-done.8.refs_3_), channel_id=1, source_target_pairs={{0,2},{2,0},{4,6},{6,4},{8,10},{10,8},{12,14},{14,12},{1,3},{3,1},... | collective-permute-start | bytes 196616 | tf_op jit(solution)/shard_map/ppermute | solution.py:369
  23.7 4.2 %late.1 = (bf16[4,448,1024]{2,1,0:T(8,128)(2,1)S(1)}, bf16[4,448,128]{2,1,0:T(8,128)(2,1)S(1)}, bf16[4,448,128]{2,1,0:T(8,128)(2,1)S(1)}, bf16[4,448,1024]{2,1,0:T(8,128)(2,1)S(1)}, bf16[3072,1024]{1,0:T(8,128)(2,1)S(1)}) custom-call(bf16[4,448,1024]{2,1,0:T(8,128)(2,1)S(1)} %get-tuple-elemen, ...), custom_call_target="tpu_custom_call", output_to_operand_aliasing={{0}: (0, {}), {1}: (1, {}), {2}: (2, {}), {3}: (3, {})} | custom-call | flops 1140850688 | bytes 1048576 | tf_op jit(solution)/shard_map/late/pallas_call | solution.py:317
  28.0 0.0 collective-permute-done.7.refs_1_
  28.0 0.0 collective-permute-done.13.refs_6_
  28.0 0.0 collective-permute-done.11.refs_4_
  28.0 0.0 collective-permute-done.9.refs_2_
  28.0 2.2 %project.1 = (bf16[16,1024]{1,0:T(8,128)(2,1)S(1)}, f32[16,1024]{1,0:T(8,128)S(1)}) custom-call(bf16[8,4096]{1,0:T(8,128)(2,1)S(1)} %decode.1.refs_0_, bf16[8,4096]{1,0:T(8,128)(2,1)S(1)} %collective-permute-done.7.refs_1_, bf16[8,4096]{1,0:T(8,128)(2,1)S(1)} %collective-permute-done.9.refs_2_, bf16[8,4096]{1,0:T(8,128)(2,1)S(1)} %collective-permute-done.8.refs_3_, ...), custom_call_target="tpu_custom_call" | custom-call | flops 1000000000 | bytes 8388608 | tf_op jit(solution)/shard_map/project/pallas_call | solution.py:522
  30.2 1.6 %collective-permute-start.14 = (bf16[16,1024]{1,0:T(8,128)(2,1)S(1)}, bf16[16,1024]{1,0:T(8,128)(2,1)S(1)}, u32[]{:S(2)}, u32[]{:S(2)}) collective-permute-start(bf16[16,1024]{1,0:T(8,128)(2,1)S(1)} %get-tuple-element.45), channel_id=1, source_target_pairs={{0,1},{1,0},{2,3},{3,2},{4,5},{5,4},{6,7},{7,6},{8,9},{9,8},{10,11... | collective-permute-start | bytes 98312 | tf_op jit(solution)/shard_map/ppermute | solution.py:585
  31.8 2.4 %last.1 = (bf16[4,448,1024]{2,1,0:T(8,128)(2,1)S(1)}, bf16[448,4096]{1,0:T(8,128)(2,1)}) custom-call(bf16[4,448,1024]{2,1,0:T(8,128)(2,1)S(1)} %get-tuple-element.32.refs_0_, bf16[4,448,128]{2,1,0:T(8,128)(2,1)S(1)} %get-tuple-element.33.refs_1_, bf16[4,448,128]{2,1,0:T(8,128)(2,1)S(1)} %get-tuple-element.34.refs_2_, ...), custom_call_target="tpu_custom_call", output_to_operand_aliasing={{0}: (3, {})} | custom-call | flops 436207616 | bytes 1048576 | tf_op jit(solution)/shard_map/last/pallas_call | solution.py:333
  34.2 0.0 collective-permute-done.14
  34.2 0.6 %add_convert_fusion = bf16[16,1024]{1,0:T(8,128)(2,1)} fusion(f32[16,1024]{1,0:T(8,128)S(1)} %get-tuple-element.44, bf16[16,1024]{1,0:T(8,128)(2,1)S(1)} %collective-permute-done.14), kind=kLoop, calls=%fused_computation | loop fusion | flops 49152 | bytes 131072 | tf_op jit(solution)/shard_map/convert_element_type | solution.py:586
Async XLA Ops:
  1.4 6.5 %collective-permute-start.5 = (bf16[4,5120]{1,0:T(4,128)(2,1)S(1)}, bf16[4,5120]{1,0:T(4,128)(2,1)S(1)}, u32[]{:S(2)}, u32[]{:S(2)}) collective-permute-start(bf16[4,5120]{1,0:T(4,128)(2,1)S(1)} %get-tuple-element.37.refs_0_), channel_id=1, source_target_pairs={{0,14},{2,12},{4,10},{6,8},{8,6},{10,4},{12,2},{14,0},{1,15},{3,13... | collective-permute-start | bytes 122888 | tf_op jit(solution)/shard_map/ppermute | solution.py:366
  6.0 4.7 %collective-permute-start.3 = (bf16[4,5120]{1,0:T(4,128)(2,1)S(1)}, bf16[4,5120]{1,0:T(4,128)(2,1)S(1)}, u32[]{:S(2)}, u32[]{:S(2)}) collective-permute-start(bf16[4,5120]{1,0:T(4,128)(2,1)S(1)} %get-tuple-element.37.refs_0_), channel_id=1, source_target_pairs={{0,10},{2,8},{4,14},{6,12},{8,2},{10,0},{12,6},{14,4},{1,11},{3,9}... | collective-permute-start | bytes 122888 | tf_op jit(solution)/shard_map/ppermute | solution.py:366
  6.0 5.0 %collective-permute-start.1 = (bf16[4,5120]{1,0:T(4,128)(2,1)S(1)}, bf16[4,5120]{1,0:T(4,128)(2,1)S(1)}, u32[]{:S(2)}, u32[]{:S(2)}) collective-permute-start(bf16[4,5120]{1,0:T(4,128)(2,1)S(1)} %get-tuple-element.37.refs_0_), channel_id=1, source_target_pairs={{0,6},{2,4},{4,2},{6,0},{8,14},{10,12},{12,10},{14,8},{1,7},{3,5},... | collective-permute-start | bytes 122888 | tf_op jit(solution)/shard_map/ppermute | solution.py:366
  6.9 6.3 %collective-permute-start = (bf16[4,5120]{1,0:T(4,128)(2,1)S(1)}, bf16[4,5120]{1,0:T(4,128)(2,1)S(1)}, u32[]{:S(2)}, u32[]{:S(2)}) collective-permute-start(bf16[4,5120]{1,0:T(4,128)(2,1)S(1)} %get-tuple-element.37.refs_0_), channel_id=1, source_target_pairs={{0,2},{2,0},{4,6},{6,4},{8,10},{10,8},{12,14},{14,12},{1,3},{3,1},... | collective-permute-start | bytes 122888 | tf_op jit(solution)/shard_map/ppermute | solution.py:369
  8.0 5.3 %collective-permute-start.6 = (bf16[4,5120]{1,0:T(4,128)(2,1)S(1)}, bf16[4,5120]{1,0:T(4,128)(2,1)S(1)}, u32[]{:S(2)}, u32[]{:S(2)}) collective-permute-start(bf16[4,5120]{1,0:T(4,128)(2,1)S(1)} %collective-permute-done.5.refs_7_), channel_id=1, source_target_pairs={{0,2},{2,0},{4,6},{6,4},{8,10},{10,8},{12,14},{14,12},{1,3},{3,1},... | collective-permute-start | bytes 122888 | tf_op jit(solution)/shard_map/ppermute | solution.py:369
  10.7 2.5 %collective-permute-start.4 = (bf16[4,5120]{1,0:T(4,128)(2,1)S(1)}, bf16[4,5120]{1,0:T(4,128)(2,1)S(1)}, u32[]{:S(2)}, u32[]{:S(2)}) collective-permute-start(bf16[4,5120]{1,0:T(4,128)(2,1)S(1)} %collective-permute-done.3.refs_5_), channel_id=1, source_target_pairs={{0,2},{2,0},{4,6},{6,4},{8,10},{10,8},{12,14},{14,12},{1,3},{3,1},... | collective-permute-start | bytes 122888 | tf_op jit(solution)/shard_map/ppermute | solution.py:369
  11.0 2.2 %collective-permute-start.2 = (bf16[4,5120]{1,0:T(4,128)(2,1)S(1)}, bf16[4,5120]{1,0:T(4,128)(2,1)S(1)}, u32[]{:S(2)}, u32[]{:S(2)}) collective-permute-start(bf16[4,5120]{1,0:T(4,128)(2,1)S(1)} %collective-permute-done.1.refs_3_), channel_id=1, source_target_pairs={{0,2},{2,0},{4,6},{6,4},{8,10},{10,8},{12,14},{14,12},{1,3},{3,1},... | collective-permute-start | bytes 122888 | tf_op jit(solution)/shard_map/ppermute | solution.py:369
  14.1 5.9 %collective-permute-start.12 = (bf16[8,4096]{1,0:T(8,128)(2,1)S(1)}, bf16[8,4096]{1,0:T(8,128)(2,1)S(1)}, u32[]{:S(2)}, u32[]{:S(2)}) collective-permute-start(bf16[8,4096]{1,0:T(8,128)(2,1)S(1)} %decode.1.refs_0_), channel_id=1, source_target_pairs={{0,14},{2,12},{4,10},{6,8},{8,6},{10,4},{12,2},{14,0},{1,15},{3,13... | collective-permute-start | bytes 196616 | tf_op jit(solution)/shard_map/ppermute | solution.py:366
  16.1 7.1 %collective-permute-start.10 = (bf16[8,4096]{1,0:T(8,128)(2,1)S(1)}, bf16[8,4096]{1,0:T(8,128)(2,1)S(1)}, u32[]{:S(2)}, u32[]{:S(2)}) collective-permute-start(bf16[8,4096]{1,0:T(8,128)(2,1)S(1)} %decode.1.refs_0_), channel_id=1, source_target_pairs={{0,10},{2,8},{4,14},{6,12},{8,2},{10,0},{12,6},{14,4},{1,11},{3,9}... | collective-permute-start | bytes 196616 | tf_op jit(solution)/shard_map/ppermute | solution.py:366
  16.4 7.0 %collective-permute-start.8 = (bf16[8,4096]{1,0:T(8,128)(2,1)S(1)}, bf16[8,4096]{1,0:T(8,128)(2,1)S(1)}, u32[]{:S(2)}, u32[]{:S(2)}) collective-permute-start(bf16[8,4096]{1,0:T(8,128)(2,1)S(1)} %decode.1.refs_0_), channel_id=1, source_target_pairs={{0,6},{2,4},{4,2},{6,0},{8,14},{10,12},{12,10},{14,8},{1,7},{3,5},... | collective-permute-start | bytes 196616 | tf_op jit(solution)/shard_map/ppermute | solution.py:366
  18.1 9.8 %collective-permute-start.7 = (bf16[8,4096]{1,0:T(8,128)(2,1)S(1)}, bf16[8,4096]{1,0:T(8,128)(2,1)S(1)}, u32[]{:S(2)}, u32[]{:S(2)}) collective-permute-start(bf16[8,4096]{1,0:T(8,128)(2,1)S(1)} %decode.1.refs_0_), channel_id=1, source_target_pairs={{0,2},{2,0},{4,6},{6,4},{8,10},{10,8},{12,14},{14,12},{1,3},{3,1},... | collective-permute-start | bytes 196616 | tf_op jit(solution)/shard_map/ppermute | solution.py:369
  20.0 8.0 %collective-permute-start.13 = (bf16[8,4096]{1,0:T(8,128)(2,1)S(1)}, bf16[8,4096]{1,0:T(8,128)(2,1)S(1)}, u32[]{:S(2)}, u32[]{:S(2)}) collective-permute-start(bf16[8,4096]{1,0:T(8,128)(2,1)S(1)} %collective-permute-done.12.refs_7_), channel_id=1, source_target_pairs={{0,2},{2,0},{4,6},{6,4},{8,10},{10,8},{12,14},{14,12},{1,3},{3,1},... | collective-permute-start | bytes 196616 | tf_op jit(solution)/shard_map/ppermute | solution.py:369
  23.2 4.8 %collective-permute-start.11 = (bf16[8,4096]{1,0:T(8,128)(2,1)S(1)}, bf16[8,4096]{1,0:T(8,128)(2,1)S(1)}, u32[]{:S(2)}, u32[]{:S(2)}) collective-permute-start(bf16[8,4096]{1,0:T(8,128)(2,1)S(1)} %collective-permute-done.10.refs_5_), channel_id=1, source_target_pairs={{0,2},{2,0},{4,6},{6,4},{8,10},{10,8},{12,14},{14,12},{1,3},{3,1},... | collective-permute-start | bytes 196616 | tf_op jit(solution)/shard_map/ppermute | solution.py:369
  23.3 4.6 %collective-permute-start.9 = (bf16[8,4096]{1,0:T(8,128)(2,1)S(1)}, bf16[8,4096]{1,0:T(8,128)(2,1)S(1)}, u32[]{:S(2)}, u32[]{:S(2)}) collective-permute-start(bf16[8,4096]{1,0:T(8,128)(2,1)S(1)} %collective-permute-done.8.refs_3_), channel_id=1, source_target_pairs={{0,2},{2,0},{4,6},{6,4},{8,10},{10,8},{12,14},{14,12},{1,3},{3,1},... | collective-permute-start | bytes 196616 | tf_op jit(solution)/shard_map/ppermute | solution.py:369
  30.2 4.0 %collective-permute-start.14 = (bf16[16,1024]{1,0:T(8,128)(2,1)S(1)}, bf16[16,1024]{1,0:T(8,128)(2,1)S(1)}, u32[]{:S(2)}, u32[]{:S(2)}) collective-permute-start(bf16[16,1024]{1,0:T(8,128)(2,1)S(1)} %get-tuple-element.45), channel_id=1, source_target_pairs={{0,1},{1,0},{2,3},{3,2},{4,5},{5,4},{6,7},{7,6},{8,9},{9,8},{10,11... | collective-permute-start | bytes 98312 | tf_op jit(solution)/shard_map/ppermute | solution.py:585

commit v8 on v7

--- a/solution.py
+++ b/solution.py
@@ -11,7 +11,8 @@
 HEAD_DIM = 128
 LOG2E = 1.4426950408889634
 ROW_BLOCK = 32
-EARLY, LATE = 0.05, 0.69
+EARLY, AHEAD, LATE = 0.05, 0.15, 0.54
+FIRST_CHIP = 2
 VMEM = pl.BlockSpec(memory_space=pltpu.VMEM)
 HBM = pl.BlockSpec(memory_space=pltpu.HBM)
 
@@ -33,12 +34,15 @@
 def shares(heads, rows, group, window):
     items = prompt_items(heads, rows, group, window)
     total = sum(price for _, price in items)
-    parts, spent = ([], [], []), 0
+    parts, spent = ([], [], [], []), 0
     for item, price in items:
         spent += price
         share = spent / total
         first = share <= EARLY or not parts[0]
-        parts[0 if first else 1 if share <= EARLY + LATE else 2].append(item)
+        ahead = share <= EARLY + AHEAD and item[0] == 0
+        parts[0 if first else 1 if ahead else 2 if share <= EARLY + AHEAD + LATE else 3].append(
+            item
+        )
     return parts
 
 
@@ -99,7 +103,7 @@
             finished(items[t - 2])
 
 
-def early_kernel(n, tp, near, group, window, home_rows, slots, items, *refs):
+def early_kernel(n, tp, near, group, window, home_rows, slots, items, ahead, *refs):
     (doc_ref, start_ref, len_ref, q_hbm, k_hbm, v_hbm, ck_hbm, cv_hbm) = refs[:8]
     (o_ref, q_ref, k_ref, v_ref, bias_ref, ck_ref, cv_ref, pick_ref, seg_ref, gather_ref) = (
         refs[8:18]
@@ -185,8 +189,12 @@
         if name not in taken:
             copy.wait()
 
-
-def late_kernel(near, group, items, *refs):
+    @pl.when(me < FIRST_CHIP)
+    def _():
+        attend(ahead, group, q_ref, k_ref, v_ref, bias_ref, s_ref, p_ref, o_ref)
+
+
+def late_kernel(near, group, ahead, items, *refs):
     bias_ref = refs[4]
     q_hbm, k_hbm, v_hbm, w_hbm, q_ref, k_ref, v_ref, o_ref, w_ref, s_ref, p_ref, sems = refs[5:]
     heads, _, width = q_ref.shape
@@ -218,6 +226,10 @@
             for copy in copies[head]:
                 copy.wait()
 
+    @pl.when(lax.axis_index("pool") >= FIRST_CHIP)
+    def _():
+        attend(ahead, group, q_ref, k_ref, v_ref, bias_ref, s_ref, p_ref, o_ref)
+
     attend(items, group, q_ref, k_ref, v_ref, bias_ref, s_ref, p_ref, o_ref, ready)
     for head in copies:
         ready((head,))
@@ -279,7 +291,7 @@
     return tuple(pltpu.with_memory_space_constraint(x, pltpu.HBM) for x in arrays)
 
 
-def early_part(n, tp, near, group, window, home_rows, items, small, query, key, value,
+def early_part(n, tp, near, group, window, home_rows, items, ahead, small, query, key, value,
                cache_keys, cache_values):
     rows, width = query.shape[0], group * HEAD_DIM
     heads = key.shape[1] // HEAD_DIM
@@ -299,7 +311,9 @@
         jax.ShapeDtypeStruct((requests, n * slots), bf16),
     ]
     return pl.pallas_call(
-        functools.partial(early_kernel, n, tp, near, group, window, home_rows, slots, items),
+        functools.partial(
+            early_kernel, n, tp, near, group, window, home_rows, slots, items, ahead
+        ),
         in_specs=[VMEM] * 3 + [HBM] * 5,
         out_specs=[VMEM] * len(out_shape),
         out_shape=out_shape,
@@ -311,11 +325,11 @@
     )(*small, *in_hbm(query, key, value, cache_keys, cache_values))
 
 
-def late_part(near, group, window, items, q, k, v, done, bias, query, key, value, weight):
+def late_part(near, group, window, ahead, items, q, k, v, done, bias, query, key, value, weight):
     held = (q, k, v, done)
     kept = weight.shape[0] // 4 * 3
     return pl.pallas_call(
-        functools.partial(late_kernel, near, group, items),
+        functools.partial(late_kernel, near, group, ahead, items),
         in_specs=[VMEM] * 5 + [HBM] * 4,
         out_specs=[VMEM] * 5,
         out_shape=[jax.ShapeDtypeStruct(x.shape, x.dtype) for x in held]
@@ -351,18 +365,18 @@
     return n & (n - 1) == 0 and 2 <= n <= 8
 
 
-def far_order(n):
+def far_order(n, name):
     order = list(range(n - 2, 0, -2))
-    if len(order) == 3:
-        order = [order[1], order[0], order[2]]
+    if name == "pooled" and len(order) == 3:
+        order = [order[1], order[2], order[0]]
     return order
 
 
-def spread(x, n):
+def spread(x, n, name):
     if not xor_plan(n):
         return [lax.all_gather(x, "pool", axis=0, tiled=True)]
     pieces = {0: x}
-    for d in far_order(n):
+    for d in far_order(n, name):
         pieces[d + 1] = lax.ppermute(x, "pool", [(i, i ^ (d + 1)) for i in range(n)])
     for d in range(0, n, 2):
         have = d + 1 if d else 0
@@ -558,7 +572,7 @@
     group = home_query.shape[1] // HEAD_DIM // kv_local
     window = min(rows, rows // 2 + ROW_BLOCK)
     near = max(1, kv_local // 4)
-    early, late, last = shares(kv_local, rows, group, window)
+    early, ahead, late, last = shares(kv_local, rows, group, window)
     prompt = (prompt_query, prompt_key, prompt_value)
 
     packed, small = pack(
@@ -569,14 +583,15 @@
         cache_start.reshape(1, -1),
         cache_len.reshape(1, -1),
     )
-    homes = spread(packed, n)
+    homes = spread(packed, n, "home")
     done, q, k, v, bias, ck, cv, pick, seg, gather = early_part(
-        n, tp, near, group, window, home_rows, early, small, *prompt, cache_keys, cache_values
+        n, tp, near, group, window, home_rows, early, ahead, small, *prompt, cache_keys,
+        cache_values,
     )
     slot_out = decode(homes, pick, seg, ck, cv, group)
-    pooled = spread(slot_out, n)
+    pooled = spread(slot_out, n, "pooled")
     q, k, v, done, kept = late_part(
-        near, group, window, late, q, k, v, done, bias, *prompt, out_weight
+        near, group, window, ahead, late, q, k, v, done, bias, *prompt, out_weight
     )
     partial = project(pooled, gather, kept, out_weight, tp)
     prompt_out = last_part(group, window, last, prompt_query.shape, q, k, v, done, bias)

time: 35.1 us -> 35.9 us (1.023)
  Pallas kernels: 12.4 us -> 13.6 us
  waiting for transfers between devices: 7.64 us -> 7.2 us
    pallas_call x1, Pallas kernels: 1.97 us -> 3.13 us  [early_part(): pl.pallas_call(functools.partial(early_kernel, n, tp, near, group, window...]
    ppermute x6, waiting for transfers between devices: 7.62 us -> 7.18 us  [spread(): pieces[d + 1] = lax.ppermute(x, 'pool', [(i, i ^ d + 1) for i in range(n)])]
  transfers between devices with their start and end apart: 15 -> 15, of which waited for: 4 -> 4; matrix products, arithmetic and copies ran while one was open for 0% -> 0% of each run, Pallas kernels for 25% -> 27%
where the time goes in v8:
time: 35.9 us; the launch traced here: 35.6 us
  Pallas kernels  13.6 us (38%)
  starting transfers between devices  13.5 us (38%)
  waiting for transfers between devices  7.2 us (20%)
  between operations  0.75 us (2%)
  other arithmetic  0.62 us (2%)
    ppermute x6, starting transfers between devices, spread(): pieces[d + 1] = lax.ppermute(x, 'pool', [(i, i ^ d + 1) for i in range(n)])  9.58 us
    ppermute x6, waiting for transfers between devices, spread(): pieces[d + 1] = lax.ppermute(x, 'pool', [(i, i ^ d + 1) for i in range(n)])  7.18 us
    pallas_call x1, Pallas kernels, late_part(): pl.pallas_call(functools.partial(late_kernel, near, group, ahead, items),...  4.18 us
    pallas_call x1, Pallas kernels, early_part(): pl.pallas_call(functools.partial(early_kernel, n, tp, near, group, window...  3.13 us
    pallas_call x1, Pallas kernels, last_part(): pl.pallas_call(functools.partial(last_kernel, group, items), in_specs=[VM...  2.44 us
    ppermute x8, starting transfers between devices, spread(): lax.ppermute(pieces[have], 'pool', [(i, i ^ 1) for i in range(n)])  2.36 us
    pallas_call x1, Pallas kernels, project(): pl.pallas_call(functools.partial(project_kernel, len(pieces), tp), in_spe...  2.21 us
    ppermute x1, starting transfers between devices, local(): other = lax.ppermute(send, 'tp', [(0, 1), (1, 0)])  1.54 us
  transfers between devices with their start and end apart: 15, of which 4 were waited for; matrix products, arithmetic and copies ran while one was open for 0% of the time, Pallas kernels for 27%

profile of v8, /device:TPU:0, one launch (start us, length us, event | category | flops | bytes accessed | tf_op | source)
XLA Modules:
  0.0 35.6 jit_solution(2431614775461303796)
XLA Ops:
  0.6 0.8 %pack.1 = (bf16[4,5120]{1,0:T(4,128)(2,1)S(1)}, s32[1,448]{1,0:T(1,128)S(1)}, s32[1,32]{1,0:T(1,128)S(1)}, s32[1,32]{1,0:T(1,128)S(1)}) custom-call(bf16[4,4096]{1,0:T(4,128)(2,1)} %q_ref.1, bf16[4,512]{1,0:T(4,128)(2,1)} %k_ref.1, bf16[4,512]{1,0:T(4,128)(2,1)} %v_ref.1, s32[1,448]{1,0:T(1,128)} %refs_0_.1, s32[1,32]{1,0:T(1,128)} %bitcast.2, s32[1,32]{1,0:T(1,128)} %bitcast.3), custom_call_target="tpu_custom_call" | custom-call | tf_op jit(solution)/shard_map/pack/pallas_call | solution.py:405
  1.4 4.6 %collective-permute-start.5 = (bf16[4,5120]{1,0:T(4,128)(2,1)S(1)}, bf16[4,5120]{1,0:T(4,128)(2,1)S(1)}, u32[]{:S(2)}, u32[]{:S(2)}) collective-permute-start(bf16[4,5120]{1,0:T(4,128)(2,1)S(1)} %get-tuple-element.37.refs_0_), channel_id=1, source_target_pairs={{0,14},{2,12},{4,10},{6,8},{8,6},{10,4},{12,2},{14,0},{1,15},{3,13... | collective-permute-start | bytes 122888 | tf_op jit(solution)/shard_map/ppermute | solution.py:380
  6.0 0.0 collective-permute-start.3
  6.0 0.9 %collective-permute-start.1 = (bf16[4,5120]{1,0:T(4,128)(2,1)S(1)}, bf16[4,5120]{1,0:T(4,128)(2,1)S(1)}, u32[]{:S(2)}, u32[]{:S(2)}) collective-permute-start(bf16[4,5120]{1,0:T(4,128)(2,1)S(1)} %get-tuple-element.37.refs_0_), channel_id=1, source_target_pairs={{0,6},{2,4},{4,2},{6,0},{8,14},{10,12},{12,10},{14,8},{1,7},{3,5},... | collective-permute-start | bytes 122888 | tf_op jit(solution)/shard_map/ppermute | solution.py:380
  6.9 0.0 collective-permute-start
  6.9 1.0 %collective-permute-done.5.refs_7_ = bf16[4,5120]{1,0:T(4,128)(2,1)S(1)} collective-permute-done((bf16[4,5120]{1,0:T(4,128)(2,1)S(1)}, bf16[4,5120]{1,0:T(4,128)(2,1)S(1)}, u32[]{:S(2)}, u32[]{:S(2)}) %collective-permute-start.5) | collective-permute-done | bytes 40992 | tf_op jit(solution)/shard_map/ppermute | solution.py:380
  8.0 0.4 %collective-permute-start.6 = (bf16[4,5120]{1,0:T(4,128)(2,1)S(1)}, bf16[4,5120]{1,0:T(4,128)(2,1)S(1)}, u32[]{:S(2)}, u32[]{:S(2)}) collective-permute-start(bf16[4,5120]{1,0:T(4,128)(2,1)S(1)} %collective-permute-done.5.refs_7_), channel_id=1, source_target_pairs={{0,2},{2,0},{4,6},{6,4},{8,10},{10,8},{12,14},{14,12},{1,3},{3,1},... | collective-permute-start | bytes 122888 | tf_op jit(solution)/shard_map/ppermute | solution.py:383
  8.4 2.3 %collective-permute-done.3.refs_5_ = bf16[4,5120]{1,0:T(4,128)(2,1)S(1)} collective-permute-done((bf16[4,5120]{1,0:T(4,128)(2,1)S(1)}, bf16[4,5120]{1,0:T(4,128)(2,1)S(1)}, u32[]{:S(2)}, u32[]{:S(2)}) %collective-permute-start.3) | collective-permute-done | bytes 40992 | tf_op jit(solution)/shard_map/ppermute | solution.py:380
  10.7 0.3 collective-permute-start.4
  11.0 0.0 collective-permute-done.1.refs_3_
  11.0 0.2 collective-permute-start.2
  11.2 3.1 %early.1 = (bf16[4,448,1024]{2,1,0:T(8,128)(2,1)S(1)}, bf16[4,448,1024]{2,1,0:T(8,128)(2,1)S(1)}, bf16[4,448,128]{2,1,0:T(8,128)(2,1)S(1)}, bf16[4,448,128]{2,1,...) custom-call(s32[1,448]{1,0:T(1,128)S(1)} %get-tuple-element.24.refs_, ...), custom_call_target="tpu_custom_call" | custom-call | flops 33554432 | bytes 1048576 | tf_op jit(solution)/shard_map/early/pallas_call | solution.py:313
  14.4 0.0 collective-permute-done.refs_1_
  14.4 0.0 collective-permute-done.6.refs_6_
  14.4 0.0 collective-permute-done.4.refs_4_
  14.4 0.0 collective-permute-done.2.refs_2_
  14.4 0.8 %decode.1.refs_0_ = bf16[8,4096]{1,0:T(8,128)(2,1)S(1)} custom-call(bf16[4,5120]{1,0:T(4,128)(2,1)S(1)} %get-tuple-element.37.refs_0_, bf16[4,5120]{1,0:T(4,128)(2,1)S(1)} %collective-permute-done.refs_1_, bf16[4,5120]{1,0:T(4,128)(2,1)S(1)} %collective-permute-done.2.refs_2_, bf16[4,5120]{1,0:T(4,128)(2,1)S(1)} %collective-permute-done.1.refs_3_, ...), custom_call_target="tpu_custom_call" | custom-call | flops 1000000000 | bytes 1048576 | tf_op jit(solution)/shard_map/decode/pallas_call | solution.py:480
  15.2 0.9 %collective-permute-start.12 = (bf16[8,4096]{1,0:T(8,128)(2,1)S(1)}, bf16[8,4096]{1,0:T(8,128)(2,1)S(1)}, u32[]{:S(2)}, u32[]{:S(2)}) collective-permute-start(bf16[8,4096]{1,0:T(8,128)(2,1)S(1)} %decode.1.refs_0_), channel_id=1, source_target_pairs={{0,14},{2,12},{4,10},{6,8},{8,6},{10,4},{12,2},{14,0},{1,15},{3,13... | collective-permute-start | bytes 196616 | tf_op jit(solution)/shard_map/ppermute | solution.py:380
  16.1 0.3 collective-permute-start.10
  16.4 2.9 %collective-permute-start.8 = (bf16[8,4096]{1,0:T(8,128)(2,1)S(1)}, bf16[8,4096]{1,0:T(8,128)(2,1)S(1)}, u32[]{:S(2)}, u32[]{:S(2)}) collective-permute-start(bf16[8,4096]{1,0:T(8,128)(2,1)S(1)} %decode.1.refs_0_), channel_id=1, source_target_pairs={{0,6},{2,4},{4,2},{6,0},{8,14},{10,12},{12,10},{14,8},{1,7},{3,5},... | collective-permute-start | bytes 196616 | tf_op jit(solution)/shard_map/ppermute | solution.py:380
  19.3 0.2 collective-permute-start.7
  19.5 1.6 %collective-permute-done.12.refs_7_ = bf16[8,4096]{1,0:T(8,128)(2,1)S(1)} collective-permute-done((bf16[8,4096]{1,0:T(8,128)(2,1)S(1)}, bf16[8,4096]{1,0:T(8,128)(2,1)S(1)}, u32[]{:S(2)}, u32[]{:S(2)}) %collective-permute-start.12) | collective-permute-done | bytes 65568 | tf_op jit(solution)/shard_map/ppermute | solution.py:380
  21.2 0.7 %collective-permute-start.13 = (bf16[8,4096]{1,0:T(8,128)(2,1)S(1)}, bf16[8,4096]{1,0:T(8,128)(2,1)S(1)}, u32[]{:S(2)}, u32[]{:S(2)}) collective-permute-start(bf16[8,4096]{1,0:T(8,128)(2,1)S(1)} %collective-permute-done.12.refs_7_), channel_id=1, source_target_pairs={{0,2},{2,0},{4,6},{6,4},{8,10},{10,8},{12,14},{14,12},{1,3},{3,1},... | collective-permute-start | bytes 196616 | tf_op jit(solution)/shard_map/ppermute | solution.py:383
  21.9 2.2 %collective-permute-done.10.refs_5_ = bf16[8,4096]{1,0:T(8,128)(2,1)S(1)} collective-permute-done((bf16[8,4096]{1,0:T(8,128)(2,1)S(1)}, bf16[8,4096]{1,0:T(8,128)(2,1)S(1)}, u32[]{:S(2)}, u32[]{:S(2)}) %collective-permute-start.10) | collective-permute-done | bytes 65568 | tf_op jit(solution)/shard_map/ppermute | solution.py:380
  24.0 0.1 collective-permute-start.11
  24.1 0.0 collective-permute-done.8.refs_3_
  24.1 0.4 %collective-permute-start.9 = (bf16[8,4096]{1,0:T(8,128)(2,1)S(1)}, bf16[8,4096]{1,0:T(8,128)(2,1)S(1)}, u32[]{:S(2)}, u32[]{:S(2)}) collective-permute-start(bf16[8,4096]{1,0:T(8,128)(2,1)S(1)} %collective-permute-done.8.refs_3_), channel_id=1, source_target_pairs={{0,2},{2,0},{4,6},{6,4},{8,10},{10,8},{12,14},{14,12},{1,3},{3,1},... | collective-permute-start | bytes 196616 | tf_op jit(solution)/shard_map/ppermute | solution.py:383
  24.5 4.2 %late.1 = (bf16[4,448,1024]{2,1,0:T(8,128)(2,1)S(1)}, bf16[4,448,128]{2,1,0:T(8,128)(2,1)S(1)}, bf16[4,448,128]{2,1,0:T(8,128)(2,1)S(1)}, bf16[4,448,1024]{2,1,0:T(8,128)(2,1)S(1)}, bf16[3072,1024]{1,0:T(8,128)(2,1)S(1)}) custom-call(bf16[4,448,1024]{2,1,0:T(8,128)(2,1)S(1)} %get-tuple-elemen, ...), custom_call_target="tpu_custom_call", output_to_operand_aliasing={{0}: (0, {}), {1}: (1, {}), {2}: (2, {}), {3}: (3, {})} | custom-call | flops 872415232 | bytes 1048576 | tf_op jit(solution)/shard_map/late/pallas_call | solution.py:331
  28.7 0.0 collective-permute-done.7.refs_1_
  28.7 0.0 collective-permute-done.13.refs_6_
  28.7 0.0 collective-permute-done.11.refs_4_
  28.8 0.0 collective-permute-done.9.refs_2_
  28.8 2.2 %project.1 = (bf16[16,1024]{1,0:T(8,128)(2,1)S(1)}, f32[16,1024]{1,0:T(8,128)S(1)}) custom-call(bf16[8,4096]{1,0:T(8,128)(2,1)S(1)} %decode.1.refs_0_, bf16[8,4096]{1,0:T(8,128)(2,1)S(1)} %collective-permute-done.7.refs_1_, bf16[8,4096]{1,0:T(8,128)(2,1)S(1)} %collective-permute-done.9.refs_2_, bf16[8,4096]{1,0:T(8,128)(2,1)S(1)} %collective-permute-done.8.refs_3_, ...), custom_call_target="tpu_custom_call" | custom-call | flops 1000000000 | bytes 8388608 | tf_op jit(solution)/shard_map/project/pallas_call | solution.py:536
  31.0 1.5 %collective-permute-start.14 = (bf16[16,1024]{1,0:T(8,128)(2,1)S(1)}, bf16[16,1024]{1,0:T(8,128)(2,1)S(1)}, u32[]{:S(2)}, u32[]{:S(2)}) collective-permute-start(bf16[16,1024]{1,0:T(8,128)(2,1)S(1)} %get-tuple-element.45), channel_id=1, source_target_pairs={{0,1},{1,0},{2,3},{3,2},{4,5},{5,4},{6,7},{7,6},{8,9},{9,8},{10,11... | collective-permute-start | bytes 98312 | tf_op jit(solution)/shard_map/ppermute | solution.py:600
  32.5 2.4 %last.1 = (bf16[4,448,1024]{2,1,0:T(8,128)(2,1)S(1)}, bf16[448,4096]{1,0:T(8,128)(2,1)}) custom-call(bf16[4,448,1024]{2,1,0:T(8,128)(2,1)S(1)} %get-tuple-element.32.refs_0_, bf16[4,448,128]{2,1,0:T(8,128)(2,1)S(1)} %get-tuple-element.33.refs_1_, bf16[4,448,128]{2,1,0:T(8,128)(2,1)S(1)} %get-tuple-element.34.refs_2_, ...), custom_call_target="tpu_custom_call", output_to_operand_aliasing={{0}: (3, {})} | custom-call | flops 436207616 | bytes 1048576 | tf_op jit(solution)/shard_map/last/pallas_call | solution.py:347
  35.0 0.0 collective-permute-done.14
  35.0 0.6 %add_convert_fusion = bf16[16,1024]{1,0:T(8,128)(2,1)} fusion(f32[16,1024]{1,0:T(8,128)S(1)} %get-tuple-element.44, bf16[16,1024]{1,0:T(8,128)(2,1)S(1)} %collective-permute-done.14), kind=kLoop, calls=%fused_computation | loop fusion | flops 49152 | bytes 131072 | tf_op jit(solution)/shard_map/convert_element_type | solution.py:601
Async XLA Ops:
  1.4 6.5 %collective-permute-start.5 = (bf16[4,5120]{1,0:T(4,128)(2,1)S(1)}, bf16[4,5120]{1,0:T(4,128)(2,1)S(1)}, u32[]{:S(2)}, u32[]{:S(2)}) collective-permute-start(bf16[4,5120]{1,0:T(4,128)(2,1)S(1)} %get-tuple-element.37.refs_0_), channel_id=1, source_target_pairs={{0,14},{2,12},{4,10},{6,8},{8,6},{10,4},{12,2},{14,0},{1,15},{3,13... | collective-permute-start | bytes 122888 | tf_op jit(solution)/shard_map/ppermute | solution.py:380
  6.0 4.7 %collective-permute-start.3 = (bf16[4,5120]{1,0:T(4,128)(2,1)S(1)}, bf16[4,5120]{1,0:T(4,128)(2,1)S(1)}, u32[]{:S(2)}, u32[]{:S(2)}) collective-permute-start(bf16[4,5120]{1,0:T(4,128)(2,1)S(1)} %get-tuple-element.37.refs_0_), channel_id=1, source_target_pairs={{0,10},{2,8},{4,14},{6,12},{8,2},{10,0},{12,6},{14,4},{1,11},{3,9}... | collective-permute-start | bytes 122888 | tf_op jit(solution)/shard_map/ppermute | solution.py:380
  6.0 5.0 %collective-permute-start.1 = (bf16[4,5120]{1,0:T(4,128)(2,1)S(1)}, bf16[4,5120]{1,0:T(4,128)(2,1)S(1)}, u32[]{:S(2)}, u32[]{:S(2)}) collective-permute-start(bf16[4,5120]{1,0:T(4,128)(2,1)S(1)} %get-tuple-element.37.refs_0_), channel_id=1, source_target_pairs={{0,6},{2,4},{4,2},{6,0},{8,14},{10,12},{12,10},{14,8},{1,7},{3,5},... | collective-permute-start | bytes 122888 | tf_op jit(solution)/shard_map/ppermute | solution.py:380
  6.9 7.4 %collective-permute-start = (bf16[4,5120]{1,0:T(4,128)(2,1)S(1)}, bf16[4,5120]{1,0:T(4,128)(2,1)S(1)}, u32[]{:S(2)}, u32[]{:S(2)}) collective-permute-start(bf16[4,5120]{1,0:T(4,128)(2,1)S(1)} %get-tuple-element.37.refs_0_), channel_id=1, source_target_pairs={{0,2},{2,0},{4,6},{6,4},{8,10},{10,8},{12,14},{14,12},{1,3},{3,1},... | collective-permute-start | bytes 122888 | tf_op jit(solution)/shard_map/ppermute | solution.py:383
  8.0 6.4 %collective-permute-start.6 = (bf16[4,5120]{1,0:T(4,128)(2,1)S(1)}, bf16[4,5120]{1,0:T(4,128)(2,1)S(1)}, u32[]{:S(2)}, u32[]{:S(2)}) collective-permute-start(bf16[4,5120]{1,0:T(4,128)(2,1)S(1)} %collective-permute-done.5.refs_7_), channel_id=1, source_target_pairs={{0,2},{2,0},{4,6},{6,4},{8,10},{10,8},{12,14},{14,12},{1,3},{3,1},... | collective-permute-start | bytes 122888 | tf_op jit(solution)/shard_map/ppermute | solution.py:383
  10.7 3.7 %collective-permute-start.4 = (bf16[4,5120]{1,0:T(4,128)(2,1)S(1)}, bf16[4,5120]{1,0:T(4,128)(2,1)S(1)}, u32[]{:S(2)}, u32[]{:S(2)}) collective-permute-start(bf16[4,5120]{1,0:T(4,128)(2,1)S(1)} %collective-permute-done.3.refs_5_), channel_id=1, source_target_pairs={{0,2},{2,0},{4,6},{6,4},{8,10},{10,8},{12,14},{14,12},{1,3},{3,1},... | collective-permute-start | bytes 122888 | tf_op jit(solution)/shard_map/ppermute | solution.py:383
  11.0 3.4 %collective-permute-start.2 = (bf16[4,5120]{1,0:T(4,128)(2,1)S(1)}, bf16[4,5120]{1,0:T(4,128)(2,1)S(1)}, u32[]{:S(2)}, u32[]{:S(2)}) collective-permute-start(bf16[4,5120]{1,0:T(4,128)(2,1)S(1)} %collective-permute-done.1.refs_3_), channel_id=1, source_target_pairs={{0,2},{2,0},{4,6},{6,4},{8,10},{10,8},{12,14},{14,12},{1,3},{3,1},... | collective-permute-start | bytes 122888 | tf_op jit(solution)/shard_map/ppermute | solution.py:383
  15.2 5.9 %collective-permute-start.12 = (bf16[8,4096]{1,0:T(8,128)(2,1)S(1)}, bf16[8,4096]{1,0:T(8,128)(2,1)S(1)}, u32[]{:S(2)}, u32[]{:S(2)}) collective-permute-start(bf16[8,4096]{1,0:T(8,128)(2,1)S(1)} %decode.1.refs_0_), channel_id=1, source_target_pairs={{0,14},{2,12},{4,10},{6,8},{8,6},{10,4},{12,2},{14,0},{1,15},{3,13... | collective-permute-start | bytes 196616 | tf_op jit(solution)/shard_map/ppermute | solution.py:380
  16.1 7.9 %collective-permute-start.10 = (bf16[8,4096]{1,0:T(8,128)(2,1)S(1)}, bf16[8,4096]{1,0:T(8,128)(2,1)S(1)}, u32[]{:S(2)}, u32[]{:S(2)}) collective-permute-start(bf16[8,4096]{1,0:T(8,128)(2,1)S(1)} %decode.1.refs_0_), channel_id=1, source_target_pairs={{0,10},{2,8},{4,14},{6,12},{8,2},{10,0},{12,6},{14,4},{1,11},{3,9}... | collective-permute-start | bytes 196616 | tf_op jit(solution)/shard_map/ppermute | solution.py:380
  16.4 7.8 %collective-permute-start.8 = (bf16[8,4096]{1,0:T(8,128)(2,1)S(1)}, bf16[8,4096]{1,0:T(8,128)(2,1)S(1)}, u32[]{:S(2)}, u32[]{:S(2)}) collective-permute-start(bf16[8,4096]{1,0:T(8,128)(2,1)S(1)} %decode.1.refs_0_), channel_id=1, source_target_pairs={{0,6},{2,4},{4,2},{6,0},{8,14},{10,12},{12,10},{14,8},{1,7},{3,5},... | collective-permute-start | bytes 196616 | tf_op jit(solution)/shard_map/ppermute | solution.py:380
  19.3 9.4 %collective-permute-start.7 = (bf16[8,4096]{1,0:T(8,128)(2,1)S(1)}, bf16[8,4096]{1,0:T(8,128)(2,1)S(1)}, u32[]{:S(2)}, u32[]{:S(2)}) collective-permute-start(bf16[8,4096]{1,0:T(8,128)(2,1)S(1)} %decode.1.refs_0_), channel_id=1, source_target_pairs={{0,2},{2,0},{4,6},{6,4},{8,10},{10,8},{12,14},{14,12},{1,3},{3,1},... | collective-permute-start | bytes 196616 | tf_op jit(solution)/shard_map/ppermute | solution.py:383
  21.2 7.6 %collective-permute-start.13 = (bf16[8,4096]{1,0:T(8,128)(2,1)S(1)}, bf16[8,4096]{1,0:T(8,128)(2,1)S(1)}, u32[]{:S(2)}, u32[]{:S(2)}) collective-permute-start(bf16[8,4096]{1,0:T(8,128)(2,1)S(1)} %collective-permute-done.12.refs_7_), channel_id=1, source_target_pairs={{0,2},{2,0},{4,6},{6,4},{8,10},{10,8},{12,14},{14,12},{1,3},{3,1},... | collective-permute-start | bytes 196616 | tf_op jit(solution)/shard_map/ppermute | solution.py:383
  24.0 4.7 %collective-permute-start.11 = (bf16[8,4096]{1,0:T(8,128)(2,1)S(1)}, bf16[8,4096]{1,0:T(8,128)(2,1)S(1)}, u32[]{:S(2)}, u32[]{:S(2)}) collective-permute-start(bf16[8,4096]{1,0:T(8,128)(2,1)S(1)} %collective-permute-done.10.refs_5_), channel_id=1, source_target_pairs={{0,2},{2,0},{4,6},{6,4},{8,10},{10,8},{12,14},{14,12},{1,3},{3,1},... | collective-permute-start | bytes 196616 | tf_op jit(solution)/shard_map/ppermute | solution.py:383
  24.1 4.6 %collective-permute-start.9 = (bf16[8,4096]{1,0:T(8,128)(2,1)S(1)}, bf16[8,4096]{1,0:T(8,128)(2,1)S(1)}, u32[]{:S(2)}, u32[]{:S(2)}) collective-permute-start(bf16[8,4096]{1,0:T(8,128)(2,1)S(1)} %collective-permute-done.8.refs_3_), channel_id=1, source_target_pairs={{0,2},{2,0},{4,6},{6,4},{8,10},{10,8},{12,14},{14,12},{1,3},{3,1},... | collective-permute-start | bytes 196616 | tf_op jit(solution)/shard_map/ppermute | solution.py:383
  31.0 4.0 %collective-permute-start.14 = (bf16[16,1024]{1,0:T(8,128)(2,1)S(1)}, bf16[16,1024]{1,0:T(8,128)(2,1)S(1)}, u32[]{:S(2)}, u32[]{:S(2)}) collective-permute-start(bf16[16,1024]{1,0:T(8,128)(2,1)S(1)} %get-tuple-element.45), channel_id=1, source_target_pairs={{0,1},{1,0},{2,3},{3,2},{4,5},{5,4},{6,7},{7,6},{8,9},{9,8},{10,11... | collective-permute-start | bytes 98312 | tf_op jit(solution)/shard_map/ppermute | solution.py:600
